TPU v7x, 512 devices: a whole 4x8x8 slice. The times are simulated.
512 devices in a mesh: gx: 32 (over y_lo, z, core), gy: 16 (over x, y_hi).
Axes of the slice: x: 4, y: 8 (y_hi: 4, y_lo: 2; y = y_hi * 2 + y_lo), z: 8, core: 2. Of those that a mesh axis runs over, the one named last changes fastest.
Arguments:
- displacement: float32 [3, 256, 128, 128], P(None, 'gx', 'gy'), may hold values from -6 to 6
- velocity: float32 [3, 256, 128, 128], P(None, 'gx', 'gy'), may hold values from -6 to 6
- region: int32 [256, 128, 128], P('gx', 'gy'), may hold values from 0 to 3
- bond_words: int32 [11, 256, 128, 128], P(None, 'gx', 'gy'), may hold values from 0 to 4095, as said below
- moduli: float32 [3, 4], replicated, may hold values from 0.5 to 2
Outputs:
- new_displacement: float32 [3, 256, 128, 128], P(None, 'gx', 'gy')
- new_velocity: float32 [3, 256, 128, 128], P(None, 'gx', 'gy')
Inputs may be any that keep to these rules, and one draw needn't show every extreme that they name: `bond_words`: bonds are the integer offsets (a, b, c) with 0 < a*a + b*b + c*c <= 9, numbered 0 to 121 in increasing lexicographic order. Bond q of a node is bit q % 12 of word q // 12 (bit 0 the lowest); a set bit means the bond is intact. A bond whose far end lies outside the grid is never intact; the six bonds of length one are intact wherever they stay inside the grid; bond q of node p equals bond 121 - q of node p + xi_q.
All inputs are finite; a program needn't handle non-finite values.
Results may differ from a plain program's by a relative error of at most 0.00002.
Values sent between devices are 32-bit elements; how exact they have to be, the bound alone decides.
No kernel may reach another device: no remote copies, remote signals or barrier semaphores. Data moves between devices by JAX's collectives and lax.ppermute only.
A program may use at most 64 MiB of HBM per device.

v0:
```python
import math

import jax
import jax.numpy as jnp
from jax import lax
from jax.sharding import PartitionSpec as P

HORIZON = 3


time_step = 0.3
bits_per_word = 12


def extended(x, sides, width):
    for axis, dim in sides:
        size, length = (lax.axis_size(axis), x.shape[dim])
        up = [(i, (i + 1) % size) for i in range(size - 1)]
        down = [(j, i) for i, j in up]
        last = lax.slice_in_dim(x, length - width, length, axis=dim)
        first = lax.slice_in_dim(x, 0, width, axis=dim)
        before = lax.ppermute(last, axis, up)
        after = lax.ppermute(first, axis, down)
        x = jnp.concatenate([before, x, after], axis=dim)
    return x


def bond_offsets():
    listed = []
    for shift_x in range(-HORIZON, HORIZON + 1):
        for shift_y in range(-HORIZON, HORIZON + 1):
            for shift_z in range(-HORIZON, HORIZON + 1):
                radius = shift_x * shift_x + shift_y * shift_y + shift_z * shift_z
                if 0 < radius <= HORIZON * HORIZON:
                    listed.append((shift_x, shift_y, shift_z))
    return listed


def bond_length(offset):
    return math.sqrt(offset[0] * offset[0] + offset[1] * offset[1] + offset[2] * offset[2])


def bond_bit(bond_words, number):
    word_index = number // bits_per_word
    bit_shift = number % bits_per_word
    return jnp.bitwise_and(jnp.right_shift(bond_words[word_index], bit_shift), 1).astype(
        jnp.float32
    )


def materials(region, moduli):
    fields = jnp.zeros((3,) + region.shape, jnp.float32)
    for material in range(moduli.shape[1]):
        fields = jnp.where(
            (region == material)[None], moduli[:, material][:, None, None, None], fields
        )
    return (fields[0], fields[1], fields[2])


def window(padded, offset, block_shape):
    start_x = HORIZON + offset[0]
    start_y = HORIZON + offset[1]
    start_z = HORIZON + offset[2]
    return padded[
        ...,
        start_x : start_x + block_shape[0],
        start_y : start_y + block_shape[1],
        start_z : start_z + block_shape[2],
    ]


def stretch_of(padded, centre, offset):
    length = bond_length(offset)
    block_shape = centre.shape[1:]
    start_x = HORIZON + offset[0]
    start_y = HORIZON + offset[1]
    start_z = HORIZON + offset[2]
    along = None
    for position in range(3):
        if offset[position] != 0:
            neighbour = padded[
                position,
                start_x : start_x + block_shape[0],
                start_y : start_y + block_shape[1],
                start_z : start_z + block_shape[2],
            ]
            term = (neighbour - centre[position]) * (offset[position] / length)
            along = term if along is None else along + term
    return along


def pad_depth(field):
    margins = ((0, 0),) * (field.ndim - 1) + ((HORIZON, HORIZON),)
    return jnp.pad(field, margins)


def on_device(displacement, velocity, region, bond_words, moduli):
    offsets = bond_offsets()
    block_shape = region.shape
    bulk_modulus, shear_modulus, density = materials(region, moduli)
    volume = jnp.zeros(block_shape, jnp.float32)
    for number, offset in enumerate(offsets):
        volume = volume + bond_bit(bond_words, number) * bond_length(offset)
    pressure_ratio = (3.0 * bulk_modulus - 5.0 * shear_modulus) / volume
    shear_term = 15.0 * shear_modulus / volume
    inverse_mass = 1.0 / density
    shear_padded = pad_depth(extended(shear_term, (("gx", 0), ("gy", 1)), HORIZON))
    imbalance = [jnp.zeros(block_shape, jnp.float32) for position in range(3)]
    for number, offset in enumerate(offsets):
        intact = bond_bit(bond_words, number)
        length = bond_length(offset)
        for position in range(3):
            if offset[position] != 0:
                imbalance[position] = imbalance[position] + intact * (offset[position] / length)
    padded = extended(displacement, (("gx", 1), ("gy", 2)), HORIZON)
    padded = pad_depth(padded)
    accumulated = jnp.zeros(block_shape, jnp.float32)
    shear_pull = [jnp.zeros(block_shape, jnp.float32) for position in range(3)]
    for number, offset in enumerate(offsets):
        intact = bond_bit(bond_words, number)
        length = bond_length(offset)
        weighted = intact * stretch_of(padded, displacement, offset)
        accumulated = accumulated + weighted
        for position in range(3):
            if offset[position] != 0:
                shear_pull[position] = shear_pull[position] + weighted * (
                    offset[position] / (length * length)
                )
    dilatation = 3.0 * accumulated / volume
    pressure_term = dilatation * pressure_ratio
    pressure_padded = pad_depth(extended(pressure_term, (("gx", 0), ("gy", 1)), HORIZON))
    force_parts = [jnp.zeros(block_shape, jnp.float32) for position in range(3)]
    for number, offset in enumerate(offsets):
        length = bond_length(offset)
        stretch = stretch_of(padded, displacement, offset)
        coefficient = bond_bit(bond_words, number) * (
            window(pressure_padded, offset, block_shape)
            + window(shear_padded, offset, block_shape) * stretch * (1.0 / length)
        )
        for position in range(3):
            if offset[position] != 0:
                force_parts[position] = force_parts[position] + coefficient * (
                    offset[position] / length
                )
    for position in range(3):
        force_parts[position] = (
            force_parts[position]
            + pressure_term * imbalance[position]
            + shear_term * shear_pull[position]
        )
    force_sum = jnp.stack(force_parts)
    velocity = velocity + time_step * force_sum * inverse_mass
    displacement = displacement + time_step * velocity
    return (displacement, velocity)


def solution(mesh):
    placed = (
        P(None, "gx", "gy", None),
        P(None, "gx", "gy", None),
        P("gx", "gy", None),
        P(None, "gx", "gy", None),
        P(),
    )
    return jax.shard_map(
        on_device,
        mesh=mesh,
        in_specs=placed,
        out_specs=(P(None, "gx", "gy", None), P(None, "gx", "gy", None)),
        check_vma=False,
    )
```

profile of v0, /device:TPU:56, one launch (start us, length us, event | category | flops | bytes accessed | tf_op | source)
XLA Modules:
  0.0 79.0 jit_solution(1125793800493459128)
XLA Ops:
  0.6 0.0 copy-start.4
  0.6 0.8 %fusion.1691 = (f32[3,3,8,128]{3,2,1,0:T(8,128)S(1)}, f32[3,3,8,128]{3,2,1,0:T(8,128)S(1)}) fusion(f32[3,8,8,128]{3,2,1,0:T(8,128)} %param.5), kind=kLoop, calls=%fused_computation.2651 | loop fusion | bytes 147456 | tf_op jit(solution)/shard_map/slice | solution.py:21
  1.4 1.9 %collective-permute-start = (f32[3,3,8,128]{3,2,1,0:T(8,128)S(1)}, f32[3,3,8,128]{3,2,1,0:T(8,128)S(1)}, u32[]{:S(2)}, u32[]{:S(2)}) collective-permute-start(f32[3,3,8,128]{3,2,1,0:T(8,128)S(1)} %get-tuple-element.190), channel_id=1, source_target_pairs={{0,16},{16,32},{32,48},{48,64},{64,80},{80,96},{96,112},{112,128},... | collective-permute-start | bytes 110600 | tf_op jit(solution)/shard_map/ppermute | solution.py:22
  3.4 11.2 %collective-permute-start.1 = (f32[3,3,8,128]{3,2,1,0:T(8,128)S(1)}, f32[3,3,8,128]{3,2,1,0:T(8,128)S(1)}, u32[]{:S(2)}, u32[]{:S(2)}) collective-permute-start(f32[3,3,8,128]{3,2,1,0:T(8,128)S(1)} %get-tuple-element.189), channel_id=1, source_target_pairs={{16,0},{32,16},{48,32},{64,48},{80,64},{96,80},{112,96},{128,112},... | collective-permute-start | bytes 110600 | tf_op jit(solution)/shard_map/ppermute | solution.py:23
  14.5 0.0 copy-done.4
  14.5 0.0 copy-start.3
  14.6 0.6 copy-done.3
  15.2 0.2 slice_reduce_fusion.3
  15.4 0.0 copy-start.1
  15.5 0.1 select_select_fusion
  15.6 0.0 collective-permute-done
  15.6 0.8 copy-done.1
  16.4 0.0 collective-permute-done.1
  16.4 2.7 %collective-permute-start.2 = (f32[3,14,3,128]{3,2,1,0:T(4,128)S(1)}, f32[3,14,3,128]{3,2,1,0:T(4,128)S(1)}, u32[]{:S(2)}, u32[]{:S(2)}) collective-permute-start(f32[3,14,3,128]{3,2,1,0:T(4,128)S(1)} %get-tuple-element.184), channel_id=1, source_target_pairs={{0,1},{1,2},{2,3},{3,4},{4,5},{5,6},{6,7},{7,8},{8,9},{9,10},{10,1... | collective-permute-start | bytes 193544 | tf_op jit(solution)/shard_map/ppermute | solution.py:22
  19.2 4.0 %collective-permute-start.3 = (f32[3,14,3,128]{3,2,1,0:T(4,128)S(1)}, f32[3,14,3,128]{3,2,1,0:T(4,128)S(1)}, u32[]{:S(2)}, u32[]{:S(2)}) collective-permute-start(f32[3,14,3,128]{3,2,1,0:T(4,128)S(1)} %get-tuple-element.185), channel_id=1, source_target_pairs={{1,0},{2,1},{3,2},{4,3},{5,4},{6,5},{7,6},{8,7},{9,8},{10,9},{11,1... | collective-permute-start | bytes 193544 | tf_op jit(solution)/shard_map/ppermute | solution.py:23
  23.2 0.0 copy-start
  23.2 0.5 collective-permute-done.2
  23.7 4.8 %collective-permute-done.3 = f32[3,14,3,128]{3,2,1,0:T(4,128)S(1)} collective-permute-done((f32[3,14,3,128]{3,2,1,0:T(4,128)S(1)}, f32[3,14,3,128]{3,2,1,0:T(4,128)S(1)}, u32[]{:S(2)}, u32[]{:S(2)}) %collective-permute-start.3) | collective-permute-done | bytes 64544 | tf_op jit(solution)/shard_map/ppermute | solution.py:23
  28.5 0.4 select_maximum_fusion
  29.0 0.0 copy-done
  29.0 0.1 bitcast_multiply_fusion.95
  29.1 0.1 bitcast_multiply_fusion.91
  29.2 0.1 bitcast_multiply_fusion.60
  29.4 0.1 fusion.92
  29.4 0.1 fusion.216
  29.5 0.1 fusion.121
  29.6 2.9 %add_add_fusion = (f32[8,8,128]{2,1,0:T(8,128)S(1)}, f32[8,8,128]{2,1,0:T(8,128)S(1)}, f32[8,8,128]{2,1,0:T(8,128)S(1)}, f32[8,8,128]{2,1,0:T(8,128)S(1)}, f32[8...) fusion(f32[8,8,128]{2,1,0:T(8,128)S(1)} %get-tuple-element.156,, ...), kind=kLoop, calls=%fused_computation.2511 | loop fusion | flops 9846784 | bytes 11868160 | tf_op jit(solution)/shard_map/add | solution.py:123
  32.5 2.2 %fusion.693 = (f32[8,8,128]{2,1,0:T(8,128)S(1)}, f32[8,8,128]{2,1,0:T(8,128)S(1)}, f32[8,8,128]{2,1,0:T(8,128)S(1)}) fusion(f32[3,8,8,128]{3,2,1,0:T(8,128)S(1)} %select_select_fusion, f32[8,8,128]{2,1,0:T(8,128)S(1)} %get-tuple-element.156, f32[8,8,128]{2,1,0:T(8,128)S(1)} %get-tuple-element.154, f32[8,8,128]{2,1,0:T(8,128)S(1)} %get-tuple-element.148, ...), kind=kLoop, calls=%fused_computation.926 | loop fusion | flops 7086080 | bytes 4587520 | tf_op jit(solution)/shard_map/mul | solution.py:130
  34.7 1.9 %collective-permute-start.4 = (f32[3,8,128]{2,1,0:T(8,128)S(1)}, f32[3,8,128]{2,1,0:T(8,128)S(1)}, u32[]{:S(2)}, u32[]{:S(2)}) collective-permute-start(f32[3,8,128]{2,1,0:T(8,128)S(1)} %get-tuple-element.203), channel_id=1, source_target_pairs={{0,16},{16,32},{32,48},{48,64},{64,80},{80,96},{96,112},{112,128},... | collective-permute-start | bytes 36872 | tf_op jit(solution)/shard_map/ppermute | solution.py:22
  36.6 5.8 %collective-permute-start.6 = (f32[3,8,128]{2,1,0:T(8,128)S(1)}, f32[3,8,128]{2,1,0:T(8,128)S(1)}, u32[]{:S(2)}, u32[]{:S(2)}) collective-permute-start(f32[3,8,128]{2,1,0:T(8,128)S(1)} %get-tuple-element.204), channel_id=1, source_target_pairs={{16,0},{32,16},{48,32},{64,48},{80,64},{96,80},{112,96},{128,112},... | collective-permute-start | bytes 36872 | tf_op jit(solution)/shard_map/ppermute | solution.py:23
  42.4 1.9 %collective-permute-start.5 = (f32[3,8,128]{2,1,0:T(8,128)S(1)}, f32[3,8,128]{2,1,0:T(8,128)S(1)}, u32[]{:S(2)}, u32[]{:S(2)}) collective-permute-start(f32[3,8,128]{2,1,0:T(8,128)S(1)} %get-tuple-element.205), channel_id=1, source_target_pairs={{0,16},{16,32},{32,48},{48,64},{64,80},{80,96},{96,112},{112,128},... | collective-permute-start | bytes 36872 | tf_op jit(solution)/shard_map/ppermute | solution.py:22
  44.3 5.8 %collective-permute-start.9 = (f32[3,8,128]{2,1,0:T(8,128)S(1)}, f32[3,8,128]{2,1,0:T(8,128)S(1)}, u32[]{:S(2)}, u32[]{:S(2)}) collective-permute-start(f32[3,8,128]{2,1,0:T(8,128)S(1)} %get-tuple-element.206), channel_id=1, source_target_pairs={{16,0},{32,16},{48,32},{64,48},{80,64},{96,80},{112,96},{128,112},... | collective-permute-start | bytes 36872 | tf_op jit(solution)/shard_map/ppermute | solution.py:23
  50.1 0.0 collective-permute-done.4
  50.1 0.0 collective-permute-done.6
  50.2 3.3 %collective-permute-start.7 = (f32[14,3,128]{2,1,0:T(4,128)S(1)}, f32[14,3,128]{2,1,0:T(4,128)S(1)}, u32[]{:S(2)}, u32[]{:S(2)}) collective-permute-start(f32[14,3,128]{2,1,0:T(4,128)S(1)} %get-tuple-element.195), channel_id=1, source_target_pairs={{0,1},{1,2},{2,3},{3,4},{4,5},{5,6},{6,7},{7,8},{8,9},{9,10},{10,1... | collective-permute-start | bytes 64520 | tf_op jit(solution)/shard_map/ppermute | solution.py:22
  53.4 3.5 %collective-permute-start.8 = (f32[14,3,128]{2,1,0:T(4,128)S(1)}, f32[14,3,128]{2,1,0:T(4,128)S(1)}, u32[]{:S(2)}, u32[]{:S(2)}) collective-permute-start(f32[14,3,128]{2,1,0:T(4,128)S(1)} %get-tuple-element.196), channel_id=1, source_target_pairs={{1,0},{2,1},{3,2},{4,3},{5,4},{6,5},{7,6},{8,7},{9,8},{10,9},{11,1... | collective-permute-start | bytes 64520 | tf_op jit(solution)/shard_map/ppermute | solution.py:23
  56.9 0.0 collective-permute-done.5
  56.9 0.0 collective-permute-done.9
  57.0 5.4 %collective-permute-start.10 = (f32[14,3,128]{2,1,0:T(4,128)S(1)}, f32[14,3,128]{2,1,0:T(4,128)S(1)}, u32[]{:S(2)}, u32[]{:S(2)}) collective-permute-start(f32[14,3,128]{2,1,0:T(4,128)S(1)} %get-tuple-element.197), channel_id=1, source_target_pairs={{0,1},{1,2},{2,3},{3,4},{4,5},{5,6},{6,7},{7,8},{8,9},{9,10},{10,1... | collective-permute-start | bytes 64520 | tf_op jit(solution)/shard_map/ppermute | solution.py:22
  62.4 1.9 %collective-permute-start.11 = (f32[14,3,128]{2,1,0:T(4,128)S(1)}, f32[14,3,128]{2,1,0:T(4,128)S(1)}, u32[]{:S(2)}, u32[]{:S(2)}) collective-permute-start(f32[14,3,128]{2,1,0:T(4,128)S(1)} %get-tuple-element.198), channel_id=1, source_target_pairs={{1,0},{2,1},{3,2},{4,3},{5,4},{6,5},{7,6},{8,7},{9,8},{10,9},{11,1... | collective-permute-start | bytes 64520 | tf_op jit(solution)/shard_map/ppermute | solution.py:23
  64.3 0.0 collective-permute-done.7
  64.3 0.0 collective-permute-done.8
  64.3 0.2 select_maximum_fusion.6
  64.5 0.0 collective-permute-done.10
  64.5 6.6 %collective-permute-done.11 = f32[14,3,128]{2,1,0:T(4,128)S(1)} collective-permute-done((f32[14,3,128]{2,1,0:T(4,128)S(1)}, f32[14,3,128]{2,1,0:T(4,128)S(1)}, u32[]{:S(2)}, u32[]{:S(2)}) %collective-permute-start.11) | collective-permute-done | bytes 21536 | tf_op jit(solution)/shard_map/ppermute | solution.py:23
  71.1 0.2 select_maximum_fusion.2
  71.3 0.1 fusion.482
  71.5 0.1 fusion.459
  71.6 0.1 fusion.501
  71.8 2.5 %fusion.1549 = (f32[1,8,8,128]{3,2,1,0:T(8,128)S(1)}, f32[8,8,128]{2,1,0:T(8,128)S(1)}, f32[8,8,128]{2,1,0:T(8,128)S(1)}, f32[8,8,128]{2,1,0:T(8,128)S(1)}, f32[...) fusion(f32[8,8,128]{2,1,0:T(8,128)S(1)} %bitcast_divide_fusion,, ...), kind=kLoop, calls=%fused_computation.2632 | loop fusion | flops 10534912 | bytes 10502144 | tf_op jit(solution)/shard_map/stack | solution.py:151
  74.2 2.1 %fusion.1176 = f32[1,8,8,128]{3,2,1,0:T(8,128)S(1)} fusion(f32[8,8,128]{2,1,0:T(8,128)S(1)} %get-tuple-element.156, f32[8,8,128]{2,1,0:T(8,128)S(1)} %get-tuple-element.154, f32[8,8,128]{2,1,0:T(8,128)S(1)} %get-tuple-element.146, f32[8,8,128]{2,1,0:T(8,128)S(1)} %get-tuple-element.158, f32[8,8,128]{2,1,0:T(8,128)S(1)} %get-tuple-element.45, ...), kind=kLoop, calls=%fused_computation.1674 | loop fusion | flops 9068544 | bytes 8126464 | tf_op jit(solution)/shard_map/stack | solution.py:151
  76.3 0.0 copy-start.2
  76.3 2.0 %fusion.1164 = f32[1,8,8,128]{3,2,1,0:T(8,128)S(1)} fusion(f32[8,8,128]{2,1,0:T(8,128)S(1)} %get-tuple-element.154, f32[8,8,128]{2,1,0:T(8,128)S(1)} %get-tuple-element.158, f32[8,8,128]{2,1,0:T(8,128)S(1)} %get-tuple-element.50, f32[8,8,128]{2,1,0:T(8,128)S(1)} %get-tuple-element.49, f32[8,8,128]{2,1,0:T(8,128)S(1)} %get-tuple-element.48, ...), kind=kLoop, calls=%fused_computation.1651 | loop fusion | flops 9142272 | bytes 8159232 | tf_op jit(solution)/shard_map/stack | solution.py:151
  78.3 0.0 copy-done.2
  78.3 0.7 multiply_add_fusion
  (15 shorter events, 0.2 us)
Async XLA Ops:
  0.6 13.9 %copy-start.4 = (s32[8,8,128]{2,1,0:T(8,128)S(1)}, s32[8,8,128]{2,1,0:T(8,128)}, u32[]{:S(2)}) copy-start(s32[8,8,128]{2,1,0:T(8,128)} %param.7) | copy-start | bytes 98308
  1.4 14.1 %collective-permute-start = (f32[3,3,8,128]{3,2,1,0:T(8,128)S(1)}, f32[3,3,8,128]{3,2,1,0:T(8,128)S(1)}, u32[]{:S(2)}, u32[]{:S(2)}) collective-permute-start(f32[3,3,8,128]{3,2,1,0:T(8,128)S(1)} %get-tuple-element.190), channel_id=1, source_target_pairs={{0,16},{16,32},{32,48},{48,64},{64,80},{80,96},{96,112},{112,128},... | collective-permute-start | bytes 110600 | tf_op jit(solution)/shard_map/ppermute | solution.py:22
  3.4 13.0 %collective-permute-start.1 = (f32[3,3,8,128]{3,2,1,0:T(8,128)S(1)}, f32[3,3,8,128]{3,2,1,0:T(8,128)S(1)}, u32[]{:S(2)}, u32[]{:S(2)}) collective-permute-start(f32[3,3,8,128]{3,2,1,0:T(8,128)S(1)} %get-tuple-element.189), channel_id=1, source_target_pairs={{16,0},{32,16},{48,32},{64,48},{80,64},{96,80},{112,96},{128,112},... | collective-permute-start | bytes 110600 | tf_op jit(solution)/shard_map/ppermute | solution.py:23
  14.5 0.7 copy-start.3
  15.4 0.9 %copy-start.1 = (f32[3,8,8,128]{3,2,1,0:T(8,128)S(1)}, f32[3,8,8,128]{3,2,1,0:T(8,128)}, u32[]{:S(2)}) copy-start(f32[3,8,8,128]{3,2,1,0:T(8,128)} %param.5) | copy-start | bytes 294916
  16.4 7.3 %collective-permute-start.2 = (f32[3,14,3,128]{3,2,1,0:T(4,128)S(1)}, f32[3,14,3,128]{3,2,1,0:T(4,128)S(1)}, u32[]{:S(2)}, u32[]{:S(2)}) collective-permute-start(f32[3,14,3,128]{3,2,1,0:T(4,128)S(1)} %get-tuple-element.184), channel_id=1, source_target_pairs={{0,1},{1,2},{2,3},{3,4},{4,5},{5,6},{6,7},{7,8},{8,9},{9,10},{10,1... | collective-permute-start | bytes 193544 | tf_op jit(solution)/shard_map/ppermute | solution.py:22
  19.2 9.4 %collective-permute-start.3 = (f32[3,14,3,128]{3,2,1,0:T(4,128)S(1)}, f32[3,14,3,128]{3,2,1,0:T(4,128)S(1)}, u32[]{:S(2)}, u32[]{:S(2)}) collective-permute-start(f32[3,14,3,128]{3,2,1,0:T(4,128)S(1)} %get-tuple-element.185), channel_id=1, source_target_pairs={{1,0},{2,1},{3,2},{4,3},{5,4},{6,5},{7,6},{8,7},{9,8},{10,9},{11,1... | collective-permute-start | bytes 193544 | tf_op jit(solution)/shard_map/ppermute | solution.py:23
  23.2 5.8 %copy-start = (s32[11,8,8,128]{3,2,1,0:T(8,128)S(1)}, s32[11,8,8,128]{3,2,1,0:T(8,128)}, u32[]{:S(2)}) copy-start(s32[11,8,8,128]{3,2,1,0:T(8,128)} %param.8) | copy-start | bytes 1081348
  34.7 15.4 %collective-permute-start.4 = (f32[3,8,128]{2,1,0:T(8,128)S(1)}, f32[3,8,128]{2,1,0:T(8,128)S(1)}, u32[]{:S(2)}, u32[]{:S(2)}) collective-permute-start(f32[3,8,128]{2,1,0:T(8,128)S(1)} %get-tuple-element.203), channel_id=1, source_target_pairs={{0,16},{16,32},{32,48},{48,64},{64,80},{80,96},{96,112},{112,128},... | collective-permute-start | bytes 36872 | tf_op jit(solution)/shard_map/ppermute | solution.py:22
  36.6 13.5 %collective-permute-start.6 = (f32[3,8,128]{2,1,0:T(8,128)S(1)}, f32[3,8,128]{2,1,0:T(8,128)S(1)}, u32[]{:S(2)}, u32[]{:S(2)}) collective-permute-start(f32[3,8,128]{2,1,0:T(8,128)S(1)} %get-tuple-element.204), channel_id=1, source_target_pairs={{16,0},{32,16},{48,32},{64,48},{80,64},{96,80},{112,96},{128,112},... | collective-permute-start | bytes 36872 | tf_op jit(solution)/shard_map/ppermute | solution.py:23
  42.4 14.5 %collective-permute-start.5 = (f32[3,8,128]{2,1,0:T(8,128)S(1)}, f32[3,8,128]{2,1,0:T(8,128)S(1)}, u32[]{:S(2)}, u32[]{:S(2)}) collective-permute-start(f32[3,8,128]{2,1,0:T(8,128)S(1)} %get-tuple-element.205), channel_id=1, source_target_pairs={{0,16},{16,32},{32,48},{48,64},{64,80},{80,96},{96,112},{112,128},... | collective-permute-start | bytes 36872 | tf_op jit(solution)/shard_map/ppermute | solution.py:22
  44.3 12.6 %collective-permute-start.9 = (f32[3,8,128]{2,1,0:T(8,128)S(1)}, f32[3,8,128]{2,1,0:T(8,128)S(1)}, u32[]{:S(2)}, u32[]{:S(2)}) collective-permute-start(f32[3,8,128]{2,1,0:T(8,128)S(1)} %get-tuple-element.206), channel_id=1, source_target_pairs={{16,0},{32,16},{48,32},{64,48},{80,64},{96,80},{112,96},{128,112},... | collective-permute-start | bytes 36872 | tf_op jit(solution)/shard_map/ppermute | solution.py:23
  50.2 14.1 %collective-permute-start.7 = (f32[14,3,128]{2,1,0:T(4,128)S(1)}, f32[14,3,128]{2,1,0:T(4,128)S(1)}, u32[]{:S(2)}, u32[]{:S(2)}) collective-permute-start(f32[14,3,128]{2,1,0:T(4,128)S(1)} %get-tuple-element.195), channel_id=1, source_target_pairs={{0,1},{1,2},{2,3},{3,4},{4,5},{5,6},{6,7},{7,8},{8,9},{9,10},{10,1... | collective-permute-start | bytes 64520 | tf_op jit(solution)/shard_map/ppermute | solution.py:22
  53.4 10.9 %collective-permute-start.8 = (f32[14,3,128]{2,1,0:T(4,128)S(1)}, f32[14,3,128]{2,1,0:T(4,128)S(1)}, u32[]{:S(2)}, u32[]{:S(2)}) collective-permute-start(f32[14,3,128]{2,1,0:T(4,128)S(1)} %get-tuple-element.196), channel_id=1, source_target_pairs={{1,0},{2,1},{3,2},{4,3},{5,4},{6,5},{7,6},{8,7},{9,8},{10,9},{11,1... | collective-permute-start | bytes 64520 | tf_op jit(solution)/shard_map/ppermute | solution.py:23
  57.0 7.5 %collective-permute-start.10 = (f32[14,3,128]{2,1,0:T(4,128)S(1)}, f32[14,3,128]{2,1,0:T(4,128)S(1)}, u32[]{:S(2)}, u32[]{:S(2)}) collective-permute-start(f32[14,3,128]{2,1,0:T(4,128)S(1)} %get-tuple-element.197), channel_id=1, source_target_pairs={{0,1},{1,2},{2,3},{3,4},{4,5},{5,6},{6,7},{7,8},{8,9},{9,10},{10,1... | collective-permute-start | bytes 64520 | tf_op jit(solution)/shard_map/ppermute | solution.py:22
  62.4 8.8 %collective-permute-start.11 = (f32[14,3,128]{2,1,0:T(4,128)S(1)}, f32[14,3,128]{2,1,0:T(4,128)S(1)}, u32[]{:S(2)}, u32[]{:S(2)}) collective-permute-start(f32[14,3,128]{2,1,0:T(4,128)S(1)} %get-tuple-element.198), channel_id=1, source_target_pairs={{1,0},{2,1},{3,2},{4,3},{5,4},{6,5},{7,6},{8,7},{9,8},{10,9},{11,1... | collective-permute-start | bytes 64520 | tf_op jit(solution)/shard_map/ppermute | solution.py:23
  76.3 2.0 %copy-start.2 = (f32[3,8,8,128]{3,2,1,0:T(8,128)S(1)}, f32[3,8,8,128]{3,2,1,0:T(8,128)}, u32[]{:S(2)}) copy-start(f32[3,8,8,128]{3,2,1,0:T(8,128)} %param.6) | copy-start | bytes 294916
where the time goes:
time: 79.5 us; the launch traced here: 79 us
  starting transfers between devices  49.2 us (62%)
  other arithmetic  14.2 us (18%)
  waiting for transfers between devices  12 us (15%)
  local copies, waits for them, and re-layouts  2.54 us (3%)
  between operations  1.09 us (1%)
    ppermute x6, starting transfers between devices, extended(): after = lax.ppermute(first, axis, down)  32.1 us
    ppermute x6, starting transfers between devices, extended(): before = lax.ppermute(last, axis, up)  17.1 us
    ppermute x6, waiting for transfers between devices, extended(): after = lax.ppermute(first, axis, down)  11.5 us
    another operation x3, other arithmetic, on_device(): force_sum = jnp.stack(force_parts)  6.5 us
    add x1, other arithmetic, on_device(): accumulated = accumulated + weighted  2.93 us
    mul x1, other arithmetic, on_device(): pressure_term = dilatation * pressure_ratio  2.18 us
  transfers between devices with their start and end apart: 12, of which 3 were waited for; matrix products, arithmetic and copies ran while one was open for 1% of the time, Pallas kernels for 0%

commit v1 on v0

v1 whole, which is shorter than its diff:
```python
import math

import jax
import jax.numpy as jnp
from jax import lax
from jax.experimental import pallas as pl
from jax.experimental.pallas import tpu as pltpu
from jax.sharding import PartitionSpec as P

HORIZON = 3
time_step = 0.3
bits_per_word = 12
F32 = jnp.float32
LANES = 128

OFFSETS = [
    (a, b, c)
    for a in range(-HORIZON, HORIZON + 1)
    for b in range(-HORIZON, HORIZON + 1)
    for c in range(-HORIZON, HORIZON + 1)
    if 0 < a * a + b * b + c * c <= HORIZON * HORIZON
]
CLASSES = sorted({a * a + b * b + c * c for a, b, c in OFFSETS})
WORDS = (len(OFFSETS) + bits_per_word - 1) // bits_per_word


def square(offset):
    return offset[0] * offset[0] + offset[1] * offset[1] + offset[2] * offset[2]


SU = 14
SW = 9
SH = 7
SP = 9
BLOCKS = (-3, 5)
SLAB = 54


def rolled(value, shift):
    return value if shift == 0 else pltpu.roll(value, (-shift) % LANES, 1)


def u_at(ref, component, shift, x, y):
    return ref[component * 7 + shift + 3, pl.ds((x + 8) * SU + y + 3, 8, stride=SU), :]


def word_at(ref, k, x, y):
    return ref[k, pl.ds((x + 8) * SW + y, 8, stride=SW), :]


def uh_at(ref, component, shift, x, h):
    return ref[component * 7 + shift + 3, pl.ds((x + 5) * SH + h, 8, stride=SH), :]


def scaled(value, factor):
    if factor == 1:
        return value
    if factor == -1:
        return -value
    return value * float(factor)


def combined(values, offset):
    total = None
    for value, factor in zip(values, offset):
        if factor == 0:
            continue
        if total is None:
            total = scaled(value, factor)
        elif factor == 1:
            total = total + value
        elif factor == -1:
            total = total - value
        else:
            total = total + value * float(factor)
    return total


def bit(word, number):
    return (word & (1 << (number % bits_per_word))) != 0


def add_to(store, key, value):
    store[key] = value if store.get(key) is None else store[key] + value


def by_class(store):
    total = None
    for cls, value in store.items():
        term = value * (1.0 / math.sqrt(cls))
        total = term if total is None else total + term
    return total


def chosen(region, moduli_ref, row):
    value = jnp.where(region == 1, moduli_ref[row, 1], moduli_ref[row, 0])
    value = jnp.where(region == 2, moduli_ref[row, 2], value)
    return jnp.where(region == 3, moduli_ref[row, 3], value)


def crossing(y):
    found = []
    for number, offset in enumerate(OFFSETS):
        target = y + offset[1]
        if target < 0:
            found.append((number, offset, target + 3))
        elif target > 7:
            found.append((number, offset, target - 8 + 3))
    return found


def slabs_x(u_ref, w_ref, r_ref, even_ref, odd_ref):
    parity = lax.axis_index("gx") % 2
    for ref, right in ((even_ref, 1 - parity), (odd_ref, parity)):
        w_start = right * 5
        u_start = right * 2
        for k in range(WORDS):
            for d in range(3):
                ref[k * 3 + d] = w_ref[k, w_start + d].astype(F32)
        for c in range(3):
            for d in range(6):
                ref[33 + c * 6 + d] = u_ref[c, u_start + d]
        for d in range(3):
            ref[51 + d] = r_ref[w_start + d].astype(F32)


def halves(even_ref, odd_ref, parity, tile_left, tile_right, y):
    def pick(tile, left):
        rows = pl.ds(tile * 8 + y, 8, stride=8)
        even, odd = (even_ref[rows, :], odd_ref[rows, :])
        return jnp.where(parity == 0, odd, even) if left else jnp.where(parity == 0, even, odd)

    return pick(tile_left, True), pick(tile_right, False)


def slabs_y(u_ref, even_ref, odd_ref, down_ref, up_ref):
    parity = lax.axis_index("gx") % 2
    for ref, first in ((down_ref, 0), (up_ref, 5)):
        for c in range(3):
            for d in range(3):
                y = first + d
                j = c * 3 + d
                left, right = halves(
                    even_ref, odd_ref, parity, 33 + c * 6 + 1, 33 + c * 6 - 3, y
                )
                ref[pl.ds(j, 8, stride=9), :] = left
                ref[pl.ds(10 * 9 + j, 8, stride=9), :] = right
                ref[pl.ds(5 * 9 + j, 8, stride=9), :] = u_ref[
                    pl.ds(c * 64 + y, 8, stride=8), :
                ]


def inner_dilatation(
    u_ref, w_ref, r_ref, moduli_ref, even_ref, odd_ref, ux_ref, wx_ref, out_ref
):
    parity = lax.axis_index("gx") % 2
    zero = jnp.zeros((8, LANES), F32)
    for y in (-3, -2, -1, 8, 9, 10):
        for lead in range(21):
            for x in (-8, 0, 8):
                ux_ref[lead, pl.ds((x + 8) * SU + y + 3, 8, stride=SU), :] = zero
    for y in range(8):
        for c in range(3):
            left, right = halves(even_ref, odd_ref, parity, 33 + c * 6 - 2, 33 + c * 6, y)
            own = u_ref[pl.ds(c * 64 + y, 8, stride=8), :]
            for x, value in ((-8, left), (8, right), (0, own)):
                for shift in range(-3, 4):
                    ux_ref[
                        c * 7 + shift + 3, pl.ds((x + 8) * SU + y + 3, 8, stride=SU), :
                    ] = rolled(value, shift)
        for k in range(WORDS + 1):
            if k < WORDS:
                left, right = halves(even_ref, odd_ref, parity, k * 3, k * 3, y)
                own = w_ref[pl.ds(k * 64 + y, 8, stride=8), :]
                places = (-3, 8)
            else:
                left, right = halves(even_ref, odd_ref, parity, 46, 46, y)
                own = r_ref[pl.ds(y, 8, stride=8), :]
                places = (-8, 3)
            for x, value in (
                (places[0], left.astype(jnp.int32)),
                (places[1], right.astype(jnp.int32)),
                (0, own),
            ):
                wx_ref[k, pl.ds((x + 8) * SW + y, 8, stride=SW), :] = value

    for index, x0 in enumerate(BLOCKS):

        def row(y, carry, index=index, x0=x0):
            own = [u_at(ux_ref, c, 0, x0, y) for c in range(3)]
            sums = {}
            counts = {}
            word = None
            for number, offset in enumerate(OFFSETS):
                if number % bits_per_word == 0:
                    k = number // bits_per_word
                    word = word_at(wx_ref, k, x0, y)
                    for cls in CLASSES:
                        held = 0
                        for other in range(
                            number, min(number + bits_per_word, len(OFFSETS))
                        ):
                            if square(OFFSETS[other]) == cls:
                                held |= 1 << (other - number)
                        if held:
                            add_to(counts, cls, lax.population_count(word & held))
                difference = [
                    u_at(ux_ref, c, offset[2], x0 + offset[0], y + offset[1]) - own[c]
                    if offset[c] != 0
                    else None
                    for c in range(3)
                ]
                along = combined(difference, offset)
                add_to(
                    sums, square(offset), jnp.where(bit(word, number), along, 0.0)
                )
            volume = None
            for cls in CLASSES:
                term = counts[cls].astype(F32) * math.sqrt(cls)
                volume = term if volume is None else volume + term
            inverse = 1.0 / jnp.where(volume > 0.0, volume, 1.0)
            region = word_at(wx_ref, WORDS, x0, y)
            bulk = chosen(region, moduli_ref, 0)
            shear = chosen(region, moduli_ref, 1)
            out_ref[index * 8 + y] = by_class(sums)
            out_ref[16 + index * 8 + y] = (3.0 * inverse) * (
                (3.0 * bulk - 5.0 * shear) * inverse
            )
            out_ref[32 + index * 8 + y] = 15.0 * shear * inverse
            return carry

        lax.fori_loop(0, 8, row, 0)


def outer_dilatation(
    below_ref, above_ref, wx_ref, part_ref, uh_ref, ps_ref, down_ref, up_ref
):
    for side, ref in enumerate((below_ref, above_ref)):
        for c in range(3):
            for d in range(3):
                for x in (-5, 3, 5):
                    value = ref[pl.ds((x + 5) * 9 + c * 3 + d, 8, stride=9), :]
                    for shift in range(-3, 4):
                        uh_ref[
                            c * 7 + shift + 3,
                            pl.ds((x + 5) * SH + side * 3 + d, 8, stride=SH),
                            :,
                        ] = rolled(value, shift)
    for y in range(8):
        for index, x0 in enumerate(BLOCKS):
            total = part_ref[index * 8 + y]
            sums = {}
            word = None
            loaded = -1
            for number, offset, h in crossing(y):
                if number // bits_per_word != loaded:
                    loaded = number // bits_per_word
                    word = word_at(wx_ref, loaded, x0, y)
                far = [
                    uh_at(uh_ref, c, offset[2], x0 + offset[0], h) if offset[c] != 0 else None
                    for c in range(3)
                ]
                add_to(
                    sums,
                    square(offset),
                    jnp.where(bit(word, number), combined(far, offset), 0.0),
                )
            if sums:
                total = total + by_class(sums)
            rows = pl.ds((x0 + 3) * SP + y, 8, stride=SP)
            ps_ref[0, rows, :] = total * part_ref[16 + index * 8 + y]
            ps_ref[1, rows, :] = part_ref[32 + index * 8 + y]
    for ref, first in ((down_ref, 0), (up_ref, 5)):
        for field in range(2):
            for d in range(3):
                for x in (-2, 2):
                    ref[pl.ds((x + 2) * 6 + field * 3 + d, 8, stride=6), :] = ps_ref[
                        field, pl.ds((x + 3) * SP + first + d, 8, stride=SP), :
                    ]


def px_at(ref, field, shift, x, y):
    return ref[field * 7 + shift + 3, pl.ds((x + 3) * SU + y + 3, 8, stride=SU), :]


def inner_force(ux_ref, wx_ref, ps_ref, out_ref, px_ref):
    zero = jnp.zeros((8, LANES), F32)
    for field in range(2):
        for x in BLOCKS:
            for y in (-3, -2, -1, 8, 9, 10):
                for lead in range(7):
                    px_ref[
                        field * 7 + lead, pl.ds((x + 3) * SU + y + 3, 8, stride=SU), :
                    ] = zero
            for y in range(8):
                value = ps_ref[field, pl.ds((x + 3) * SP + y, 8, stride=SP), :]
                for shift in range(-3, 4):
                    px_ref[
                        field * 7 + shift + 3,
                        pl.ds((x + 3) * SU + y + 3, 8, stride=SU),
                        :,
                    ] = rolled(value, shift)

    def row(y, carry):
        own = [u_at(ux_ref, c, 0, 0, y) for c in range(3)]
        pressure = px_at(px_ref, 0, 0, 0, y)
        shear = px_at(px_ref, 1, 0, 0, y)
        force = [None, None, None]
        word = None
        column = {}
        for number, offset in enumerate(OFFSETS):
            if number % bits_per_word == 0:
                word = word_at(wx_ref, number // bits_per_word, 0, y)
            a, b, c = offset
            difference = [
                u_at(ux_ref, i, c, a, y + b) - own[i] if offset[i] != 0 else None
                for i in range(3)
            ]
            along = combined(difference, offset)
            cls = square(offset)
            value = (pressure + px_at(px_ref, 0, c, a, y + b)) + (
                shear + px_at(px_ref, 1, c, a, y + b)
            ) * (along * (1.0 / cls))
            column[c] = jnp.where(
                bit(word, number), value * (1.0 / math.sqrt(cls)), 0.0
            )
            last = number + 1 == len(OFFSETS) or OFFSETS[number + 1][:2] != (a, b)
            if last:
                force = fold(force, column, a, b)
                column = {}
        for i in range(3):
            out_ref[i * 8 + y] = force[i]
        return carry

    lax.fori_loop(0, 8, row, 0)


def fold(force, column, a, b):
    force = list(force)
    total = None
    for value in column.values():
        total = value if total is None else total + value
    for i, factor in ((0, a), (1, b)):
        if factor != 0:
            term = scaled(total, factor)
            force[i] = term if force[i] is None else force[i] + term
    for c, value in column.items():
        if c > 0:
            term = scaled(value - column[-c], c)
            force[2] = term if force[2] is None else force[2] + term
    return force


def outer_force(
    below_ref,
    above_ref,
    ux_ref,
    uh_ref,
    wx_ref,
    ps_ref,
    part_ref,
    u_ref,
    v_ref,
    moduli_ref,
    new_u_ref,
    new_v_ref,
    ph_ref,
):
    for side, ref in enumerate((below_ref, above_ref)):
        for field in range(2):
            for d in range(3):
                for x in (-2, 2):
                    value = ref[pl.ds((x + 2) * 6 + field * 3 + d, 8, stride=6), :]
                    for shift in range(-3, 4):
                        ph_ref[
                            field * 7 + shift + 3,
                            pl.ds((x + 2) * SH + side * 3 + d, 8, stride=SH),
                            :,
                        ] = rolled(value, shift)
    for y in range(8):
        force = [part_ref[i * 8 + y] for i in range(3)]
        own = [u_at(ux_ref, c, 0, 0, y) for c in range(3)]
        shear = ps_ref[1, pl.ds(3 * SP + y, 8, stride=SP), :]
        column = {}
        bonds = crossing(y)
        loaded = -1
        word = None
        for position, (number, offset, h) in enumerate(bonds):
            if number // bits_per_word != loaded:
                loaded = number // bits_per_word
                word = word_at(wx_ref, loaded, 0, y)
            a, b, c = offset
            cls = square(offset)
            far = [
                uh_at(uh_ref, i, c, a, h) if offset[i] != 0 else None for i in range(3)
            ]
            reach = combined(far, offset)
            along = combined(
                [far[i] - own[i] if offset[i] != 0 else None for i in range(3)], offset
            )
            rows = pl.ds((a + 2) * SH + h, 8, stride=SH)
            far_pressure = ph_ref[c + 3, rows, :]
            far_shear = ph_ref[7 + c + 3, rows, :]
            value = far_pressure + (far_shear * along + shear * reach) * (1.0 / cls)
            column[c] = jnp.where(
                bit(word, number), value * (1.0 / math.sqrt(cls)), 0.0
            )
            if position + 1 == len(bonds) or bonds[position + 1][1][:2] != (a, b):
                force = fold(force, column, a, b)
                column = {}
        density = chosen(word_at(wx_ref, WORDS, 0, y), moduli_ref, 2)
        step = time_step / density
        for i in range(3):
            rows = pl.ds(i * 64 + y, 8, stride=8)
            velocity = v_ref[rows, :] + force[i] * step
            new_v_ref[rows, :] = velocity
            new_u_ref[rows, :] = u_ref[rows, :] + time_step * velocity


def call(body, name, outs, args, scalars=(), scratch=(), flops=1000):
    vmem = pl.BlockSpec(memory_space=pltpu.VMEM)
    smem = pl.BlockSpec(memory_space=pltpu.SMEM)
    return pl.pallas_call(
        body,
        name=name,
        out_shape=[jax.ShapeDtypeStruct(shape, dtype) for shape, dtype in outs],
        in_specs=[smem if position in scalars else vmem for position in range(len(args))],
        out_specs=[vmem for _ in outs],
        scratch_shapes=[pltpu.VMEM(shape, dtype) for shape, dtype in scratch],
        cost_estimate=pl.CostEstimate(flops=flops, bytes_accessed=100000, transcendentals=0),
        compiler_params=pltpu.CompilerParams(vmem_limit_bytes=16 * 1024 * 1024),
    )(*args)


def along_y(down, up):
    size = lax.axis_size("gy")
    upward = [(i, i + 1) for i in range(size - 1)]
    downward = [(i + 1, i) for i in range(size - 1)]
    below = lax.ppermute(up, "gy", upward)
    above = lax.ppermute(down, "gy", downward)
    return below, above


def on_device(displacement, velocity, region, bond_words, moduli):
    even, odd = call(
        slabs_x,
        "slabs_x",
        [((SLAB, 8, LANES), F32)] * 2,
        (displacement, bond_words, region),
    )
    size = lax.axis_size("gx")
    even = lax.ppermute(even, "gx", [(i, i ^ 1) for i in range(size)])
    odd = lax.ppermute(
        odd, "gx", [(i, ((i - 1) ^ 1) + 1) for i in range(1, size - 1)]
    )
    even = even.reshape(SLAB * 8, LANES)
    odd = odd.reshape(SLAB * 8, LANES)
    u = displacement.reshape(192, LANES)
    down, up = call(slabs_y, "slabs_y", [((162, LANES), F32)] * 2, (u, even, odd))
    below, above = along_y(down, up)
    ux, wx, part = call(
        inner_dilatation,
        "inner_dilatation",
        [((21, 24 * SU, LANES), F32), ((12, 24 * SW, LANES), jnp.int32), ((48, 8, LANES), F32)],
        (u, bond_words.reshape(704, LANES), region.reshape(64, LANES), moduli, even, odd),
        scalars=(3,),
        flops=40_000_000,
    )
    uh, ps, down, up = call(
        outer_dilatation,
        "outer_dilatation",
        [
            ((21, 20 * SH, LANES), F32),
            ((2, 16 * SP, LANES), F32),
            ((72, LANES), F32),
            ((72, LANES), F32),
        ],
        (below, above, wx, part),
        flops=4_000_000,
    )
    below, above = along_y(down, up)
    (force,) = call(
        inner_force,
        "inner_force",
        [((24, 8, LANES), F32)],
        (ux, wx, ps),
        scratch=[((14, 16 * SU, LANES), F32)],
        flops=40_000_000,
    )
    new_u, new_v = call(
        outer_force,
        "outer_force",
        [((192, LANES), F32)] * 2,
        (below, above, ux, uh, wx, ps, force, u, velocity.reshape(192, LANES), moduli),
        scalars=(9,),
        scratch=[((14, 12 * SH, LANES), F32)],
        flops=4_000_000,
    )
    return new_u.reshape(displacement.shape), new_v.reshape(velocity.shape)


def solution(mesh):
    placed = (
        P(None, "gx", "gy", None),
        P(None, "gx", "gy", None),
        P("gx", "gy", None),
        P(None, "gx", "gy", None),
        P(),
    )
    return jax.shard_map(
        on_device,
        mesh=mesh,
        in_specs=placed,
        out_specs=(P(None, "gx", "gy", None), P(None, "gx", "gy", None)),
        check_vma=False,
    )
```

time: 79.5 us -> 50.2 us (0.63)
  starting transfers between devices: 49.2 us -> 27.2 us
  other arithmetic: 14.2 us -> 0 us
  Pallas kernels: 0 us -> 9.24 us
  waiting for transfers between devices: 12 us -> 7.97 us
  local copies, waits for them, and re-layouts: 2.54 us -> 4.29 us
    ppermute x12 -> x6, starting transfers between devices: 49.2 us -> 27.2 us  [the longest x1 11.8 us: on_device(): lax.ppermute(odd, 'gx', [(i, (i - 1 ^ 1) + 1) for i in range(1, size - 1)])]
    pallas_call x0 -> x6, Pallas kernels: none -> 9.24 us  [call(): pl.pallas_call(body, name=name, out_shape=[jax.ShapeDtypeStruct(shape, dt...]
    another operation x3 -> x0, other arithmetic: 6.5 us -> none  [on_device(): force_sum = jnp.stack(force_parts)]
    ppermute x12 -> x6, waiting for transfers between devices: 12 us -> 7.97 us  [the longest x1 4.04 us: on_device(): lax.ppermute(odd, 'gx', [(i, (i - 1 ^ 1) + 1) for i in range(1, size - 1)])]
    add x5 -> x0, other arithmetic: 3.81 us -> none  [the longest x1 2.93 us: on_device(): accumulated = accumulated + weighted]
    mul x8 -> x0, other arithmetic: 2.91 us -> none  [the longest x1 2.18 us: on_device(): pressure_term = dilatation * pressure_ratio]
    unnamed x11 -> x12, local copies, waits for them, and re-layouts: 1.44 us -> 4.29 us
    slice x7 -> x0, local copies, waits for them, and re-layouts: 1.07 us -> none  [the longest x1 0.8 us: extended(): first = lax.slice_in_dim(x, 0, width, axis=dim)]
  transfers between devices with their start and end apart: 12 -> 6, of which waited for: 3 -> 2; matrix products, arithmetic and copies ran while one was open for 1% -> 0% of each run, Pallas kernels for 0% -> 14%
where the time goes in v1:
time: 50.2 us; the launch traced here: 49.5 us
  starting transfers between devices  27.2 us (54%)
  Pallas kernels  9.24 us (18%)
  waiting for transfers between devices  7.97 us (16%)
  local copies, waits for them, and re-layouts  4.29 us (9%)
  between operations  0.76 us (2%)
    ppermute x1, starting transfers between devices, on_device(): lax.ppermute(odd, 'gx', [(i, (i - 1 ^ 1) + 1) for i in range(1, size - 1)])  11.8 us
    pallas_call x6, Pallas kernels, call(): pl.pallas_call(body, name=name, out_shape=[jax.ShapeDtypeStruct(shape, dt...  9.24 us
    ppermute x2, starting transfers between devices, along_y(): above = lax.ppermute(down, 'gy', downward)  6.85 us
    ppermute x2, starting transfers between devices, along_y(): below = lax.ppermute(up, 'gy', upward)  6.64 us
    unnamed x12, local copies, waits for them, and re-layouts  4.29 us
    ppermute x1, waiting for transfers between devices, on_device(): lax.ppermute(odd, 'gx', [(i, (i - 1 ^ 1) + 1) for i in range(1, size - 1)])  4.04 us
    ppermute x2, waiting for transfers between devices, along_y(): above = lax.ppermute(down, 'gy', downward)  3.92 us
    ppermute x1, starting transfers between devices, on_device(): even = lax.ppermute(even, 'gx', [(i, i ^ 1) for i in range(size)])  1.92 us
  transfers between devices with their start and end apart: 6, of which 2 were waited for; matrix products, arithmetic and copies ran while one was open for 0% of the time, Pallas kernels for 14%

profile of v1, /device:TPU:56, one launch (start us, length us, event | category | flops | bytes accessed | tf_op | source)
XLA Modules:
  0.0 49.5 jit_solution(15011483865449193125)
XLA Ops:
  0.6 0.0 copy-start
  0.6 0.9 %copy-done = f32[3,8,8,128]{3,2,1,0:T(8,128)S(1)} copy-done((f32[3,8,8,128]{3,2,1,0:T(8,128)S(1)}, f32[3,8,8,128]{3,2,1,0:T(8,128)}, u32[]{:S(2)}) %copy-start) | copy-done | bytes 98328
  1.5 0.0 copy-start.1
  1.5 1.0 %copy-done.1 = s32[11,8,8,128]{3,2,1,0:T(8,128)S(1)} copy-done((s32[11,8,8,128]{3,2,1,0:T(8,128)S(1)}, s32[11,8,8,128]{3,2,1,0:T(8,128)}, u32[]{:S(2)}) %copy-start.1) | copy-done | bytes 360472
  2.5 0.0 copy-start.3
  2.5 0.8 %copy-done.3 = s32[8,8,128]{2,1,0:T(8,128)S(1)} copy-done((s32[8,8,128]{2,1,0:T(8,128)S(1)}, s32[8,8,128]{2,1,0:T(8,128)}, u32[]{:S(2)}) %copy-start.3) | copy-done | bytes 32792
  3.3 1.9 %collective-permute-start = (f32[54,8,128]{2,1,0:T(8,128)S(1)}, f32[54,8,128]{2,1,0:T(8,128)S(1)}, u32[]{:S(2)}, u32[]{:S(2)}) collective-permute-start(f32[54,8,128]{2,1,0:T(8,128)S(1)} %get-tuple-element.15), channel_id=1, source_target_pairs={{0,16},{16,0},{32,48},{48,32},{64,80},{80,64},{96,112},{112,96},{1... | collective-permute-start | bytes 663560 | tf_op jit(solution)/shard_map/ppermute | solution.py:452
  5.2 11.8 %collective-permute-start.1 = (f32[54,8,128]{2,1,0:T(8,128)S(1)}, f32[54,8,128]{2,1,0:T(8,128)S(1)}, u32[]{:S(2)}, u32[]{:S(2)}) collective-permute-start(f32[54,8,128]{2,1,0:T(8,128)S(1)} %get-tuple-element.16), channel_id=1, source_target_pairs={{16,32},{32,16},{48,64},{64,48},{80,96},{96,80},{112,128},{128,112... | collective-permute-start | bytes 663560 | tf_op jit(solution)/shard_map/ppermute | solution.py:453
  17.1 0.0 collective-permute-done
  17.1 4.0 %collective-permute-done.1 = f32[54,8,128]{2,1,0:T(8,128)S(1)} collective-permute-done((f32[54,8,128]{2,1,0:T(8,128)S(1)}, f32[54,8,128]{2,1,0:T(8,128)S(1)}, u32[]{:S(2)}, u32[]{:S(2)}) %collective-permute-start.1) | collective-permute-done | bytes 221216 | tf_op jit(solution)/shard_map/ppermute | solution.py:453
  21.1 0.1 slabs_y.1
  21.2 2.3 %collective-permute-start.2 = (f32[162,128]{1,0:T(8,128)S(1)}, f32[162,128]{1,0:T(8,128)S(1)}, u32[]{:S(2)}, u32[]{:S(2)}) collective-permute-start(f32[162,128]{1,0:T(8,128)S(1)} %get-tuple-element.17), channel_id=1, source_target_pairs={{0,1},{1,2},{2,3},{3,4},{4,5},{5,6},{6,7},{7,8},{8,9},{9,10},{10,1... | collective-permute-start | bytes 248840 | tf_op jit(solution)/shard_map/ppermute | solution.py:439
  23.5 4.5 %collective-permute-start.3 = (f32[162,128]{1,0:T(8,128)S(1)}, f32[162,128]{1,0:T(8,128)S(1)}, u32[]{:S(2)}, u32[]{:S(2)}) collective-permute-start(f32[162,128]{1,0:T(8,128)S(1)} %get-tuple-element.18), channel_id=1, source_target_pairs={{1,0},{2,1},{3,2},{4,3},{5,4},{6,5},{7,6},{8,7},{9,8},{10,9},{11,1... | collective-permute-start | bytes 248840 | tf_op jit(solution)/shard_map/ppermute | solution.py:440
  28.0 0.0 copy-start.2
  28.0 1.0 %copy-done.2 = s32[11,8,8,128]{3,2,1,0:T(8,128)S(1)} copy-done((s32[11,8,8,128]{3,2,1,0:T(8,128)S(1)}, s32[11,8,8,128]{3,2,1,0:T(8,128)}, u32[]{:S(2)}) %copy-start.2) | copy-done | bytes 360472
  28.9 0.0 copy-start.5
  28.9 0.7 %copy-done.5 = f32[3,4]{1,0:T(4,128)S(1)} copy-done((f32[3,4]{1,0:T(4,128)S(1)}, f32[3,4]{1,0:T(4,128)}, u32[]{:S(2)}) %copy-start.5) | copy-done | bytes 72
  29.6 4.2 %inner_dilatation.1 = (f32[21,336,128]{2,1,0:T(8,128)S(1)}, s32[12,216,128]{2,1,0:T(8,128)S(1)}, f32[48,8,128]{2,1,0:T(8,128)S(1)}) custom-call(f32[192,128]{1,0:T(8,128)S(1)} %bitcast.9, s32[704,128]{1,0:T(8,128)S(1)} %bitcast.11, s32[64,128]{1,0:T(8,128)S(1)} %bitcast.16, f32[3,4]{1,0:T(4,128)S(1)} %copy-done.5, f32[432,128]{1,0:T(8,128)S(1)} %bitcast.13, ...), custom_call_target="tpu_custom_call" | custom-call | flops 40000000 | bytes 100000 | tf_op jit(solution)/shard_map/inner_dilatation/pallas_call | solution.py:423
  33.9 0.0 collective-permute-done.2.below_ref
  33.9 0.0 collective-permute-done.3.above_ref
  33.9 0.6 %outer_dilatation.1 = (f32[21,140,128]{2,1,0:T(8,128)S(1)}, f32[2,144,128]{2,1,0:T(8,128)S(1)}, f32[72,128]{1,0:T(8,128)S(1)}, f32[72,128]{1,0:T(8,128)S(1)}) custom-call(f32[162,128]{1,0:T(8,128)S(1)} %collective-permute-done.2.below_ref, f32[162,128]{1,0:T(8,128)S(1)} %collective-permute-done.3.above_ref, s32[12,216,128]{2,1,0:T(8,128)S(1)} %get-tuple-element.19.wx_ref, ...), custom_call_target="tpu_custom_call" | custom-call | flops 4000000 | bytes 100000 | tf_op jit(solution)/shard_map/outer_dilatation/pallas_call | solution.py:423
  34.5 4.4 %collective-permute-start.4 = (f32[72,128]{1,0:T(8,128)S(1)}, f32[72,128]{1,0:T(8,128)S(1)}, u32[]{:S(2)}, u32[]{:S(2)}) collective-permute-start(f32[72,128]{1,0:T(8,128)S(1)} %get-tuple-element.21), channel_id=1, source_target_pairs={{0,1},{1,2},{2,3},{3,4},{4,5},{5,6},{6,7},{7,8},{8,9},{9,10},{10,1... | collective-permute-start | bytes 110600 | tf_op jit(solution)/shard_map/ppermute | solution.py:439
  38.9 2.4 %collective-permute-start.5 = (f32[72,128]{1,0:T(8,128)S(1)}, f32[72,128]{1,0:T(8,128)S(1)}, u32[]{:S(2)}, u32[]{:S(2)}) collective-permute-start(f32[72,128]{1,0:T(8,128)S(1)} %get-tuple-element.22), channel_id=1, source_target_pairs={{1,0},{2,1},{3,2},{4,3},{5,4},{6,5},{7,6},{8,7},{9,8},{10,9},{11,1... | collective-permute-start | bytes 110600 | tf_op jit(solution)/shard_map/ppermute | solution.py:440
  41.3 0.0 copy-start.4
  41.3 2.5 %inner_force.1.part_ref = f32[24,8,128]{2,1,0:T(8,128)S(1)} custom-call(f32[21,336,128]{2,1,0:T(8,128)S(1)} %get-tuple-element.23.ux_ref, s32[12,216,128]{2,1,0:T(8,128)S(1)} %get-tuple-element.19.wx_ref, f32[2,144,128]{2,1,0:T(8,128)S(1)} %get-tuple-element.25.ps_ref), custom_call_target="tpu_custom_call" | custom-call | flops 40000000 | bytes 100000 | tf_op jit(solution)/shard_map/inner_force/pallas_call | solution.py:423
  43.8 0.0 collective-permute-done.4.below_ref
  43.8 3.9 %collective-permute-done.5.above_ref = f32[72,128]{1,0:T(8,128)S(1)} collective-permute-done((f32[72,128]{1,0:T(8,128)S(1)}, f32[72,128]{1,0:T(8,128)S(1)}, u32[]{:S(2)}, u32[]{:S(2)}) %collective-permute-start.5) | collective-permute-done | bytes 36896 | tf_op jit(solution)/shard_map/ppermute | solution.py:440
  47.8 0.0 copy-done.4
  47.8 1.8 %outer_force.1 = (f32[192,128]{1,0:T(8,128)}, f32[192,128]{1,0:T(8,128)}) custom-call(f32[72,128]{1,0:T(8,128)S(1)} %collective-permute-done.4.below_ref, f32[72,128]{1,0:T(8,128)S(1)} %collective-permute-done.5.above_ref, f32[21,336,128]{2,1,0:T(8,128)S(1)} %get-tuple-element.23.ux_ref, f32[21,140,128]{2,1,0:T(8,128)S(1)} %get-tuple-element.24.uh_ref, ...), custom_call_target="tpu_custom_call" | custom-call | flops 4000000 | bytes 100000 | tf_op jit(solution)/shard_map/outer_force/pallas_call | solution.py:423
  (1 shorter events, 0.0 us)
Async XLA Ops:
  0.6 0.9 %copy-start = (f32[3,8,8,128]{3,2,1,0:T(8,128)S(1)}, f32[3,8,8,128]{3,2,1,0:T(8,128)}, u32[]{:S(2)}) copy-start(f32[3,8,8,128]{3,2,1,0:T(8,128)} %u_ref.1) | copy-start | bytes 294916
  1.5 1.0 %copy-start.1 = (s32[11,8,8,128]{3,2,1,0:T(8,128)S(1)}, s32[11,8,8,128]{3,2,1,0:T(8,128)}, u32[]{:S(2)}) copy-start(s32[11,8,8,128]{3,2,1,0:T(8,128)} %w_ref.1) | copy-start | bytes 1081348
  2.5 0.8 %copy-start.3 = (s32[8,8,128]{2,1,0:T(8,128)S(1)}, s32[8,8,128]{2,1,0:T(8,128)}, u32[]{:S(2)}) copy-start(s32[8,8,128]{2,1,0:T(8,128)} %r_ref.1) | copy-start | bytes 98308
  3.3 13.8 %collective-permute-start = (f32[54,8,128]{2,1,0:T(8,128)S(1)}, f32[54,8,128]{2,1,0:T(8,128)S(1)}, u32[]{:S(2)}, u32[]{:S(2)}) collective-permute-start(f32[54,8,128]{2,1,0:T(8,128)S(1)} %get-tuple-element.15), channel_id=1, source_target_pairs={{0,16},{16,0},{32,48},{48,32},{64,80},{80,64},{96,112},{112,96},{1... | collective-permute-start | bytes 663560 | tf_op jit(solution)/shard_map/ppermute | solution.py:452
  5.2 15.9 %collective-permute-start.1 = (f32[54,8,128]{2,1,0:T(8,128)S(1)}, f32[54,8,128]{2,1,0:T(8,128)S(1)}, u32[]{:S(2)}, u32[]{:S(2)}) collective-permute-start(f32[54,8,128]{2,1,0:T(8,128)S(1)} %get-tuple-element.16), channel_id=1, source_target_pairs={{16,32},{32,16},{48,64},{64,48},{80,96},{96,80},{112,128},{128,112... | collective-permute-start | bytes 663560 | tf_op jit(solution)/shard_map/ppermute | solution.py:453
  21.2 12.7 %collective-permute-start.2 = (f32[162,128]{1,0:T(8,128)S(1)}, f32[162,128]{1,0:T(8,128)S(1)}, u32[]{:S(2)}, u32[]{:S(2)}) collective-permute-start(f32[162,128]{1,0:T(8,128)S(1)} %get-tuple-element.17), channel_id=1, source_target_pairs={{0,1},{1,2},{2,3},{3,4},{4,5},{5,6},{6,7},{7,8},{8,9},{9,10},{10,1... | collective-permute-start | bytes 248840 | tf_op jit(solution)/shard_map/ppermute | solution.py:439
  23.5 10.4 %collective-permute-start.3 = (f32[162,128]{1,0:T(8,128)S(1)}, f32[162,128]{1,0:T(8,128)S(1)}, u32[]{:S(2)}, u32[]{:S(2)}) collective-permute-start(f32[162,128]{1,0:T(8,128)S(1)} %get-tuple-element.18), channel_id=1, source_target_pairs={{1,0},{2,1},{3,2},{4,3},{5,4},{6,5},{7,6},{8,7},{9,8},{10,9},{11,1... | collective-permute-start | bytes 248840 | tf_op jit(solution)/shard_map/ppermute | solution.py:440
  28.0 1.0 %copy-start.2 = (s32[11,8,8,128]{3,2,1,0:T(8,128)S(1)}, s32[11,8,8,128]{3,2,1,0:T(8,128)}, u32[]{:S(2)}) copy-start(s32[11,8,8,128]{3,2,1,0:T(8,128)} %w_ref.1) | copy-start | bytes 1081348
  28.9 0.7 %copy-start.5 = (f32[3,4]{1,0:T(4,128)S(1)}, f32[3,4]{1,0:T(4,128)}, u32[]{:S(2)}) copy-start(f32[3,4]{1,0:T(4,128)} %moduli_ref.3) | copy-start | bytes 148
  34.5 9.3 %collective-permute-start.4 = (f32[72,128]{1,0:T(8,128)S(1)}, f32[72,128]{1,0:T(8,128)S(1)}, u32[]{:S(2)}, u32[]{:S(2)}) collective-permute-start(f32[72,128]{1,0:T(8,128)S(1)} %get-tuple-element.21), channel_id=1, source_target_pairs={{0,1},{1,2},{2,3},{3,4},{4,5},{5,6},{6,7},{7,8},{8,9},{9,10},{10,1... | collective-permute-start | bytes 110600 | tf_op jit(solution)/shard_map/ppermute | solution.py:439
  38.9 8.9 %collective-permute-start.5 = (f32[72,128]{1,0:T(8,128)S(1)}, f32[72,128]{1,0:T(8,128)S(1)}, u32[]{:S(2)}, u32[]{:S(2)}) collective-permute-start(f32[72,128]{1,0:T(8,128)S(1)} %get-tuple-element.22), channel_id=1, source_target_pairs={{1,0},{2,1},{3,2},{4,3},{5,4},{6,5},{7,6},{8,7},{9,8},{10,9},{11,1... | collective-permute-start | bytes 110600 | tf_op jit(solution)/shard_map/ppermute | solution.py:440
  41.3 6.5 %copy-start.4 = (f32[3,8,8,128]{3,2,1,0:T(8,128)S(1)}, f32[3,8,8,128]{3,2,1,0:T(8,128)}, u32[]{:S(2)}) copy-start(f32[3,8,8,128]{3,2,1,0:T(8,128)} %param.6) | copy-start | bytes 294916

commit v2 on v1

--- a/solution.py
+++ b/solution.py
@@ -6,6 +6,7 @@
 from jax.experimental import pallas as pl
 from jax.experimental.pallas import tpu as pltpu
 from jax.sharding import PartitionSpec as P
+
 
 HORIZON = 3
 time_step = 0.3
@@ -109,8 +110,19 @@
     return found
 
 
-def slabs_x(u_ref, w_ref, r_ref, even_ref, odd_ref):
+def slabs_x(
+    u_hbm, w_hbm, r_hbm, odd_ref, even_ref, u_ref, w_ref, r_ref, u_sem, w_sem, r_sem
+):
     parity = lax.axis_index("gx") % 2
+    copies = [
+        pltpu.make_async_copy(w_hbm, w_ref, w_sem),
+        pltpu.make_async_copy(u_hbm, u_ref, u_sem),
+        pltpu.make_async_copy(r_hbm, r_ref, r_sem),
+    ]
+    for copy in copies:
+        copy.start()
+    for copy in copies:
+        copy.wait()
     for ref, right in ((even_ref, 1 - parity), (odd_ref, parity)):
         w_start = right * 5
         u_start = right * 2
@@ -151,8 +163,21 @@
 
 
 def inner_dilatation(
-    u_ref, w_ref, r_ref, moduli_ref, even_ref, odd_ref, ux_ref, wx_ref, out_ref
+    u_ref,
+    w_ref,
+    r_ref,
+    moduli_hbm,
+    even_ref,
+    odd_ref,
+    ux_ref,
+    wx_ref,
+    out_ref,
+    step_ref,
+    moduli_ref,
+    moduli_sem,
 ):
+    fetch = pltpu.make_async_copy(moduli_hbm, moduli_ref, moduli_sem)
+    fetch.start()
     parity = lax.axis_index("gx") % 2
     zero = jnp.zeros((8, LANES), F32)
     for y in (-3, -2, -1, 8, 9, 10):
@@ -184,6 +209,10 @@
             ):
                 wx_ref[k, pl.ds((x + 8) * SW + y, 8, stride=SW), :] = value
 
+    fetch.wait()
+    for y in range(8):
+        region = r_ref[pl.ds(y, 8, stride=8), :]
+        step_ref[y] = time_step / chosen(region, moduli_ref, 2)
     for index, x0 in enumerate(BLOCKS):
 
         def row(y, carry, index=index, x0=x0):
@@ -361,7 +390,7 @@
     part_ref,
     u_ref,
     v_ref,
-    moduli_ref,
+    step_ref,
     new_u_ref,
     new_v_ref,
     ph_ref,
@@ -408,8 +437,7 @@
             if position + 1 == len(bonds) or bonds[position + 1][1][:2] != (a, b):
                 force = fold(force, column, a, b)
                 column = {}
-        density = chosen(word_at(wx_ref, WORDS, 0, y), moduli_ref, 2)
-        step = time_step / density
+        step = step_ref[y]
         for i in range(3):
             rows = pl.ds(i * 64 + y, 8, stride=8)
             velocity = v_ref[rows, :] + force[i] * step
@@ -417,19 +445,23 @@
             new_u_ref[rows, :] = u_ref[rows, :] + time_step * velocity
 
 
-def call(body, name, outs, args, scalars=(), scratch=(), flops=1000):
+def call(body, outs, args, unplaced=(), scratch=(), flops=1000):
     vmem = pl.BlockSpec(memory_space=pltpu.VMEM)
-    smem = pl.BlockSpec(memory_space=pltpu.SMEM)
+    unmoved = pl.BlockSpec(memory_space=pltpu.HBM)
     return pl.pallas_call(
         body,
-        name=name,
         out_shape=[jax.ShapeDtypeStruct(shape, dtype) for shape, dtype in outs],
-        in_specs=[smem if position in scalars else vmem for position in range(len(args))],
+        in_specs=[unmoved if position in unplaced else vmem for position in range(len(args))],
         out_specs=[vmem for _ in outs],
-        scratch_shapes=[pltpu.VMEM(shape, dtype) for shape, dtype in scratch],
+        scratch_shapes=scratch,
         cost_estimate=pl.CostEstimate(flops=flops, bytes_accessed=100000, transcendentals=0),
         compiler_params=pltpu.CompilerParams(vmem_limit_bytes=16 * 1024 * 1024),
-    )(*args)
+    )(
+        *[
+            pltpu.with_memory_space_constraint(arg, pltpu.HBM) if position in unplaced else arg
+            for position, arg in enumerate(args)
+        ]
+    )
 
 
 def along_y(down, up):
@@ -442,33 +474,33 @@
 
 
 def on_device(displacement, velocity, region, bond_words, moduli):
-    even, odd = call(
+    copy = pltpu.SemaphoreType.DMA(())
+    odd, even, u, words, region = call(
         slabs_x,
-        "slabs_x",
-        [((SLAB, 8, LANES), F32)] * 2,
+        [((SLAB, 8, LANES), F32)] * 2
+        + [(x.shape, x.dtype) for x in (displacement, bond_words, region)],
         (displacement, bond_words, region),
+        unplaced=(0, 1, 2),
+        scratch=[copy, copy, copy],
     )
     size = lax.axis_size("gx")
+    odd = lax.ppermute(odd, "gx", [(i, ((i - 1) ^ 1) + 1) for i in range(1, size - 1)])
     even = lax.ppermute(even, "gx", [(i, i ^ 1) for i in range(size)])
-    odd = lax.ppermute(
-        odd, "gx", [(i, ((i - 1) ^ 1) + 1) for i in range(1, size - 1)]
-    )
     even = even.reshape(SLAB * 8, LANES)
     odd = odd.reshape(SLAB * 8, LANES)
-    u = displacement.reshape(192, LANES)
-    down, up = call(slabs_y, "slabs_y", [((162, LANES), F32)] * 2, (u, even, odd))
+    u = u.reshape(192, LANES)
+    down, up = call(slabs_y, [((162, LANES), F32)] * 2, (u, even, odd))
     below, above = along_y(down, up)
-    ux, wx, part = call(
+    ux, wx, part, step = call(
         inner_dilatation,
-        "inner_dilatation",
-        [((21, 24 * SU, LANES), F32), ((12, 24 * SW, LANES), jnp.int32), ((48, 8, LANES), F32)],
-        (u, bond_words.reshape(704, LANES), region.reshape(64, LANES), moduli, even, odd),
-        scalars=(3,),
+        [((21, 24 * SU, LANES), F32), ((12, 24 * SW, LANES), jnp.int32), ((48, 8, LANES), F32), ((8, 8, LANES), F32)],
+        (u, words.reshape(704, LANES), region.reshape(64, LANES), moduli, even, odd),
+        unplaced=(3,),
+        scratch=[pltpu.SMEM(moduli.shape, F32), copy],
         flops=40_000_000,
     )
     uh, ps, down, up = call(
         outer_dilatation,
-        "outer_dilatation",
         [
             ((21, 20 * SH, LANES), F32),
             ((2, 16 * SP, LANES), F32),
@@ -481,19 +513,16 @@
     below, above = along_y(down, up)
     (force,) = call(
         inner_force,
-        "inner_force",
         [((24, 8, LANES), F32)],
         (ux, wx, ps),
-        scratch=[((14, 16 * SU, LANES), F32)],
+        scratch=[pltpu.VMEM((14, 16 * SU, LANES), F32)],
         flops=40_000_000,
     )
     new_u, new_v = call(
         outer_force,
-        "outer_force",
         [((192, LANES), F32)] * 2,
-        (below, above, ux, uh, wx, ps, force, u, velocity.reshape(192, LANES), moduli),
-        scalars=(9,),
-        scratch=[((14, 12 * SH, LANES), F32)],
+        (below, above, ux, uh, wx, ps, force, u, velocity.reshape(192, LANES), step),
+        scratch=[pltpu.VMEM((14, 12 * SH, LANES), F32)],
         flops=4_000_000,
     )
     return new_u.reshape(displacement.shape), new_v.reshape(velocity.shape)

time: 50.2 us -> 45.8 us (0.912)
  local copies, waits for them, and re-layouts: 4.29 us -> 0.01 us
    unnamed x12 -> x2, local copies, waits for them, and re-layouts: 4.29 us -> 0.01 us
    ppermute x2, starting transfers between devices: 6.85 us -> 8.03 us  [along_y(): above = lax.ppermute(down, 'gy', downward)]
    ppermute x2, starting transfers between devices: 6.64 us -> 5.45 us  [along_y(): below = lax.ppermute(up, 'gy', upward)]
  transfers between devices with their start and end apart: 6 -> 6, of which waited for: 2 -> 3; matrix products, arithmetic and copies ran while one was open for 0% -> 0% of each run, Pallas kernels for 14% -> 14%
where the time goes in v2:
time: 45.8 us; the launch traced here: 45.5 us
  starting transfers between devices  27.2 us (59%)
  Pallas kernels  9.16 us (20%)
  waiting for transfers between devices  8.35 us (18%)
  between operations  0.73 us (2%)
    ppermute x1, starting transfers between devices, on_device(): lax.ppermute(odd, 'gx', [(i, (i - 1 ^ 1) + 1) for i in range(1, size - 1)])  11.8 us
    pallas_call x6, Pallas kernels, call(): pl.pallas_call(body, out_shape=[jax.ShapeDtypeStruct(shape, dtype) for sh...  9.16 us
    ppermute x2, starting transfers between devices, along_y(): above = lax.ppermute(down, 'gy', downward)  8.03 us
    ppermute x2, starting transfers between devices, along_y(): below = lax.ppermute(up, 'gy', upward)  5.45 us
    ppermute x2, waiting for transfers between devices, along_y(): above = lax.ppermute(down, 'gy', downward)  4.3 us
    ppermute x1, waiting for transfers between devices, on_device(): lax.ppermute(odd, 'gx', [(i, (i - 1 ^ 1) + 1) for i in range(1, size - 1)])  4.04 us
    ppermute x1, starting transfers between devices, on_device(): even = lax.ppermute(even, 'gx', [(i, i ^ 1) for i in range(size)])  1.92 us
  transfers between devices with their start and end apart: 6, of which 3 were waited for; matrix products, arithmetic and copies ran while one was open for 0% of the time, Pallas kernels for 14%

profile of v2, /device:TPU:56, one launch (start us, length us, event | category | flops | bytes accessed | tf_op | source)
XLA Modules:
  0.0 45.5 jit_solution(5763980201357523700)
XLA Ops:
  0.6 1.1 %shard_map.68 = (f32[54,8,128]{2,1,0:T(8,128)S(1)}, f32[54,8,128]{2,1,0:T(8,128)S(1)}, f32[3,8,8,128]{3,2,1,0:T(8,128)S(1)}, s32[11,8,8,128]{3,2,1,0:T(8,128)S(1)}, s32[8,8,128]{2,1,0:T(8,128)S(1)}) custom-call(f32[3,8,8,128]{3,2,1,0:T(8,128)} %u_hbm.1, s32[11,8,8,128]{3,2,1,0:T(8,128)} %w_hbm.1, s32[8,8,128]{2,1,0:T(8,128)} %r_hbm.1), custom_call_target="tpu_custom_call" | custom-call | flops 1000 | bytes 100000 | tf_op jit(solution)/shard_map/pallas_call | solution.py:451
  1.7 1.9 %collective-permute-start = (f32[54,8,128]{2,1,0:T(8,128)S(1)}, f32[54,8,128]{2,1,0:T(8,128)S(1)}, u32[]{:S(2)}, u32[]{:S(2)}) collective-permute-start(f32[54,8,128]{2,1,0:T(8,128)S(1)} %get-tuple-element.20), channel_id=1, source_target_pairs={{0,16},{16,0},{32,48},{48,32},{64,80},{80,64},{96,112},{112,96},{1... | collective-permute-start | bytes 663560 | tf_op jit(solution)/shard_map/ppermute | solution.py:488
  3.6 11.8 %collective-permute-start.1 = (f32[54,8,128]{2,1,0:T(8,128)S(1)}, f32[54,8,128]{2,1,0:T(8,128)S(1)}, u32[]{:S(2)}, u32[]{:S(2)}) collective-permute-start(f32[54,8,128]{2,1,0:T(8,128)S(1)} %get-tuple-element.21), channel_id=1, source_target_pairs={{16,32},{32,16},{48,64},{64,48},{80,96},{96,80},{112,128},{128,112... | collective-permute-start | bytes 663560 | tf_op jit(solution)/shard_map/ppermute | solution.py:487
  15.5 0.0 collective-permute-done
  15.5 4.0 %collective-permute-done.1 = f32[54,8,128]{2,1,0:T(8,128)S(1)} collective-permute-done((f32[54,8,128]{2,1,0:T(8,128)S(1)}, f32[54,8,128]{2,1,0:T(8,128)S(1)}, u32[]{:S(2)}, u32[]{:S(2)}) %collective-permute-start.1) | collective-permute-done | bytes 221216 | tf_op jit(solution)/shard_map/ppermute | solution.py:487
  19.5 0.1 shard_map.69
  19.6 2.3 %collective-permute-start.2 = (f32[162,128]{1,0:T(8,128)S(1)}, f32[162,128]{1,0:T(8,128)S(1)}, u32[]{:S(2)}, u32[]{:S(2)}) collective-permute-start(f32[162,128]{1,0:T(8,128)S(1)} %get-tuple-element.22), channel_id=1, source_target_pairs={{0,1},{1,2},{2,3},{3,4},{4,5},{5,6},{6,7},{7,8},{8,9},{9,10},{10,1... | collective-permute-start | bytes 248840 | tf_op jit(solution)/shard_map/ppermute | solution.py:471
  21.9 4.5 %collective-permute-start.3 = (f32[162,128]{1,0:T(8,128)S(1)}, f32[162,128]{1,0:T(8,128)S(1)}, u32[]{:S(2)}, u32[]{:S(2)}) collective-permute-start(f32[162,128]{1,0:T(8,128)S(1)} %get-tuple-element.23), channel_id=1, source_target_pairs={{1,0},{2,1},{3,2},{4,3},{5,4},{6,5},{7,6},{8,7},{9,8},{10,9},{11,1... | collective-permute-start | bytes 248840 | tf_op jit(solution)/shard_map/ppermute | solution.py:472
  26.4 3.7 %shard_map.70 = (f32[21,336,128]{2,1,0:T(8,128)S(1)}, s32[12,216,128]{2,1,0:T(8,128)S(1)}, f32[48,8,128]{2,1,0:T(8,128)S(1)}, f32[8,8,128]{2,1,0:T(8,128)S(1)}) custom-call(f32[192,128]{1,0:T(8,128)S(1)} %bitcast.13, s32[704,128]{1,0:T(8,128)S(1)} %bitcast.15, s32[64,128]{1,0:T(8,128)S(1)} %bitcast.17, f32[3,4]{1,0:T(4,128)} %moduli_hbm.1, ...), custom_call_target="tpu_custom_call" | custom-call | flops 40000000 | bytes 100000 | tf_op jit(solution)/shard_map/pallas_call | solution.py:451
  30.1 0.0 collective-permute-done.2.below_ref
  30.1 1.6 %collective-permute-done.3.above_ref = f32[162,128]{1,0:T(8,128)S(1)} collective-permute-done((f32[162,128]{1,0:T(8,128)S(1)}, f32[162,128]{1,0:T(8,128)S(1)}, u32[]{:S(2)}, u32[]{:S(2)}) %collective-permute-start.3) | collective-permute-done | bytes 82976 | tf_op jit(solution)/shard_map/ppermute | solution.py:472
  31.7 0.6 %shard_map.71 = (f32[21,140,128]{2,1,0:T(8,128)S(1)}, f32[2,144,128]{2,1,0:T(8,128)S(1)}, f32[72,128]{1,0:T(8,128)S(1)}, f32[72,128]{1,0:T(8,128)S(1)}) custom-call(f32[162,128]{1,0:T(8,128)S(1)} %collective-permute-done.2.below_ref, f32[162,128]{1,0:T(8,128)S(1)} %collective-permute-done.3.above_ref, s32[12,216,128]{2,1,0:T(8,128)S(1)} %get-tuple-element.26.wx_ref, ...), custom_call_target="tpu_custom_call" | custom-call | flops 4000000 | bytes 100000 | tf_op jit(solution)/shard_map/pallas_call | solution.py:451
  32.3 3.2 %collective-permute-start.4 = (f32[72,128]{1,0:T(8,128)S(1)}, f32[72,128]{1,0:T(8,128)S(1)}, u32[]{:S(2)}, u32[]{:S(2)}) collective-permute-start(f32[72,128]{1,0:T(8,128)S(1)} %get-tuple-element.28), channel_id=1, source_target_pairs={{0,1},{1,2},{2,3},{3,4},{4,5},{5,6},{6,7},{7,8},{8,9},{9,10},{10,1... | collective-permute-start | bytes 110600 | tf_op jit(solution)/shard_map/ppermute | solution.py:471
  35.5 3.6 %collective-permute-start.5 = (f32[72,128]{1,0:T(8,128)S(1)}, f32[72,128]{1,0:T(8,128)S(1)}, u32[]{:S(2)}, u32[]{:S(2)}) collective-permute-start(f32[72,128]{1,0:T(8,128)S(1)} %get-tuple-element.29), channel_id=1, source_target_pairs={{1,0},{2,1},{3,2},{4,3},{5,4},{6,5},{7,6},{8,7},{9,8},{10,9},{11,1... | collective-permute-start | bytes 110600 | tf_op jit(solution)/shard_map/ppermute | solution.py:472
  39.0 0.0 copy-start
  39.0 2.5 %shard_map.72.part_ref = f32[24,8,128]{2,1,0:T(8,128)S(1)} custom-call(f32[21,336,128]{2,1,0:T(8,128)S(1)} %get-tuple-element.30.ux_ref, s32[12,216,128]{2,1,0:T(8,128)S(1)} %get-tuple-element.26.wx_ref, f32[2,144,128]{2,1,0:T(8,128)S(1)} %get-tuple-element.32.ps_ref), custom_call_target="tpu_custom_call" | custom-call | flops 40000000 | bytes 100000 | tf_op jit(solution)/shard_map/pallas_call | solution.py:451
  41.6 0.0 collective-permute-done.4.below_ref
  41.6 2.7 %collective-permute-done.5.above_ref = f32[72,128]{1,0:T(8,128)S(1)} collective-permute-done((f32[72,128]{1,0:T(8,128)S(1)}, f32[72,128]{1,0:T(8,128)S(1)}, u32[]{:S(2)}, u32[]{:S(2)}) %collective-permute-start.5) | collective-permute-done | bytes 36896 | tf_op jit(solution)/shard_map/ppermute | solution.py:472
  44.3 0.0 copy-done
  44.3 1.2 %shard_map.73 = (f32[192,128]{1,0:T(8,128)}, f32[192,128]{1,0:T(8,128)}) custom-call(f32[72,128]{1,0:T(8,128)S(1)} %collective-permute-done.4.below_ref, f32[72,128]{1,0:T(8,128)S(1)} %collective-permute-done.5.above_ref, f32[21,336,128]{2,1,0:T(8,128)S(1)} %get-tuple-element.30.ux_ref, f32[21,140,128]{2,1,0:T(8,128)S(1)} %get-tuple-element.31.uh_ref, ...), custom_call_target="tpu_custom_call" | custom-call | flops 4000000 | bytes 100000 | tf_op jit(solution)/shard_map/pallas_call | solution.py:451
Async XLA Ops:
  1.7 13.8 %collective-permute-start = (f32[54,8,128]{2,1,0:T(8,128)S(1)}, f32[54,8,128]{2,1,0:T(8,128)S(1)}, u32[]{:S(2)}, u32[]{:S(2)}) collective-permute-start(f32[54,8,128]{2,1,0:T(8,128)S(1)} %get-tuple-element.20), channel_id=1, source_target_pairs={{0,16},{16,0},{32,48},{48,32},{64,80},{80,64},{96,112},{112,96},{1... | collective-permute-start | bytes 663560 | tf_op jit(solution)/shard_map/ppermute | solution.py:488
  3.6 15.9 %collective-permute-start.1 = (f32[54,8,128]{2,1,0:T(8,128)S(1)}, f32[54,8,128]{2,1,0:T(8,128)S(1)}, u32[]{:S(2)}, u32[]{:S(2)}) collective-permute-start(f32[54,8,128]{2,1,0:T(8,128)S(1)} %get-tuple-element.21), channel_id=1, source_target_pairs={{16,32},{32,16},{48,64},{64,48},{80,96},{96,80},{112,128},{128,112... | collective-permute-start | bytes 663560 | tf_op jit(solution)/shard_map/ppermute | solution.py:487
  19.6 10.5 %collective-permute-start.2 = (f32[162,128]{1,0:T(8,128)S(1)}, f32[162,128]{1,0:T(8,128)S(1)}, u32[]{:S(2)}, u32[]{:S(2)}) collective-permute-start(f32[162,128]{1,0:T(8,128)S(1)} %get-tuple-element.22), channel_id=1, source_target_pairs={{0,1},{1,2},{2,3},{3,4},{4,5},{5,6},{6,7},{7,8},{8,9},{9,10},{10,1... | collective-permute-start | bytes 248840 | tf_op jit(solution)/shard_map/ppermute | solution.py:471
  21.9 9.8 %collective-permute-start.3 = (f32[162,128]{1,0:T(8,128)S(1)}, f32[162,128]{1,0:T(8,128)S(1)}, u32[]{:S(2)}, u32[]{:S(2)}) collective-permute-start(f32[162,128]{1,0:T(8,128)S(1)} %get-tuple-element.23), channel_id=1, source_target_pairs={{1,0},{2,1},{3,2},{4,3},{5,4},{6,5},{7,6},{8,7},{9,8},{10,9},{11,1... | collective-permute-start | bytes 248840 | tf_op jit(solution)/shard_map/ppermute | solution.py:472
  32.3 9.3 %collective-permute-start.4 = (f32[72,128]{1,0:T(8,128)S(1)}, f32[72,128]{1,0:T(8,128)S(1)}, u32[]{:S(2)}, u32[]{:S(2)}) collective-permute-start(f32[72,128]{1,0:T(8,128)S(1)} %get-tuple-element.28), channel_id=1, source_target_pairs={{0,1},{1,2},{2,3},{3,4},{4,5},{5,6},{6,7},{7,8},{8,9},{9,10},{10,1... | collective-permute-start | bytes 110600 | tf_op jit(solution)/shard_map/ppermute | solution.py:471
  35.5 8.9 %collective-permute-start.5 = (f32[72,128]{1,0:T(8,128)S(1)}, f32[72,128]{1,0:T(8,128)S(1)}, u32[]{:S(2)}, u32[]{:S(2)}) collective-permute-start(f32[72,128]{1,0:T(8,128)S(1)} %get-tuple-element.29), channel_id=1, source_target_pairs={{1,0},{2,1},{3,2},{4,3},{5,4},{6,5},{7,6},{8,7},{9,8},{10,9},{11,1... | collective-permute-start | bytes 110600 | tf_op jit(solution)/shard_map/ppermute | solution.py:472
  39.0 5.3 %copy-start = (f32[3,8,8,128]{3,2,1,0:T(8,128)S(1)}, f32[3,8,8,128]{3,2,1,0:T(8,128)}, u32[]{:S(2)}) copy-start(f32[3,8,8,128]{3,2,1,0:T(8,128)} %param.6) | copy-start | bytes 294916

commit v3 on v2

v3 whole, which is shorter than its diff:
```python
import math

import jax
import jax.numpy as jnp
from jax import lax
from jax.experimental import pallas as pl
from jax.experimental.pallas import tpu as pltpu
from jax.sharding import PartitionSpec as P


HORIZON = 3
time_step = 0.3
bits_per_word = 12
F32 = jnp.float32
LANES = 128

OFFSETS = [
    (a, b, c)
    for a in range(-HORIZON, HORIZON + 1)
    for b in range(-HORIZON, HORIZON + 1)
    for c in range(-HORIZON, HORIZON + 1)
    if 0 < a * a + b * b + c * c <= HORIZON * HORIZON
]
CLASSES = sorted({a * a + b * b + c * c for a, b, c in OFFSETS})
NUMBERS = {offset: number for number, offset in enumerate(OFFSETS)}
WORDS = (len(OFFSETS) + bits_per_word - 1) // bits_per_word


def square(offset):
    return offset[0] * offset[0] + offset[1] * offset[1] + offset[2] * offset[2]


SU = 14
SW = 9
SH = 7
SF = 9
BLOCKS = (-4, 4)
U_TILE = 44
R_TILE = 62
SLAB = 65
FIELDS = 162
EDGE_ROWS = (0, 1, 2, 5, 6, 7)


def rolled(value, shift):
    return value if shift == 0 else pltpu.roll(value, (-shift) % LANES, 1)


def u_at(ref, component, shift, x, y):
    return ref[component * 7 + shift + 3, pl.ds((x + 8) * SU + y + 3, 8, stride=SU), :]


def word_at(ref, k, x, y):
    return ref[k, pl.ds((x + 8) * SW + y, 8, stride=SW), :]


def uh_at(ref, component, shift, x, h):
    return ref[component * 7 + shift + 3, pl.ds((x + 6) * SH + h, 8, stride=SH), :]


def scaled(value, factor):
    if factor == 1:
        return value
    if factor == -1:
        return -value
    return value * float(factor)


def combined(values, offset):
    total = None
    for value, factor in zip(values, offset):
        if factor == 0:
            continue
        if total is None:
            total = scaled(value, factor)
        elif factor == 1:
            total = total + value
        elif factor == -1:
            total = total - value
        else:
            total = total + value * float(factor)
    return total


def bit(word, number):
    return (word & (1 << (number % bits_per_word))) != 0


def add_to(store, key, value):
    store[key] = value if store.get(key) is None else store[key] + value


def by_class(store):
    total = None
    for cls, value in store.items():
        term = value * (1.0 / math.sqrt(cls))
        total = term if total is None else total + term
    return total


def chosen(region, moduli_ref, row):
    value = jnp.where(region == 1, moduli_ref[row, 1], moduli_ref[row, 0])
    value = jnp.where(region == 2, moduli_ref[row, 2], value)
    return jnp.where(region == 3, moduli_ref[row, 3], value)


def px_at(ref, shift, x, y):
    return ref[shift + 3, pl.ds((x + 4) * SU + y + 3, 8, stride=SU), :]


def field_at(ref, field, x, y):
    return ref[field, pl.ds((x + 4) * SF + y, 8, stride=SF), :]


def crossing(y):
    found = []
    for number, offset in enumerate(OFFSETS):
        target = y + offset[1]
        if target < 0:
            found.append((number, offset, target + 3))
        elif target > 7:
            found.append((number, offset, target - 8 + 3))
    return found


def slabs_x(
    u_hbm, w_hbm, r_hbm, odd_ref, even_ref, u_ref, w_ref, r_ref, u_sem, w_sem, r_sem
):
    parity = lax.axis_index("gx") % 2
    copies = [
        pltpu.make_async_copy(w_hbm, w_ref, w_sem),
        pltpu.make_async_copy(u_hbm, u_ref, u_sem),
        pltpu.make_async_copy(r_hbm, r_ref, r_sem),
    ]
    for copy in copies:
        copy.start()
    for copy in copies:
        copy.wait()
    for ref, right in ((even_ref, 1 - parity), (odd_ref, parity)):
        for k in range(WORDS):
            for d in range(4):
                ref[k * 4 + d] = w_ref[k, right * 4 + d].astype(F32)
        for c in range(3):
            for d in range(6):
                ref[U_TILE + c * 6 + d] = u_ref[c, right * 2 + d]
        for d in range(3):
            ref[R_TILE + d] = r_ref[right * 5 + d].astype(F32)


def halves(even_ref, odd_ref, parity, tile_left, tile_right, y):
    def pick(tile, left):
        rows = pl.ds(tile * 8 + y, 8, stride=8)
        even, odd = (even_ref[rows, :], odd_ref[rows, :])
        return jnp.where(parity == 0, odd, even) if left else jnp.where(parity == 0, even, odd)

    return pick(tile_left, True), pick(tile_right, False)


def inner_sum(ux_ref, wx_ref, x0, y):
    own = [u_at(ux_ref, c, 0, x0, y) for c in range(3)]
    sums = {}
    word = None
    for number, offset in enumerate(OFFSETS):
        if number % bits_per_word == 0:
            word = word_at(wx_ref, number // bits_per_word, x0, y)
        difference = [
            u_at(ux_ref, c, offset[2], x0 + offset[0], y + offset[1]) - own[c]
            if offset[c] != 0
            else None
            for c in range(3)
        ]
        along = combined(difference, offset)
        add_to(sums, square(offset), jnp.where(bit(word, number), along, 0.0))
    return by_class(sums)


def ratios(wx_ref, moduli_ref, x0, y):
    counts = {}
    for k in range(WORDS):
        word = word_at(wx_ref, k, x0, y)
        group = OFFSETS[k * bits_per_word : (k + 1) * bits_per_word]
        for cls in CLASSES:
            held = sum(1 << i for i, offset in enumerate(group) if square(offset) == cls)
            if held:
                add_to(counts, cls, lax.population_count(word & held))
    volume = None
    for cls in CLASSES:
        term = counts[cls].astype(F32) * math.sqrt(cls)
        volume = term if volume is None else volume + term
    inverse = 1.0 / jnp.where(volume > 0.0, volume, 1.0)
    region = word_at(wx_ref, WORDS, x0, y)
    bulk = chosen(region, moduli_ref, 0)
    shear = chosen(region, moduli_ref, 1)
    return (3.0 * inverse) * ((3.0 * bulk - 5.0 * shear) * inverse), 15.0 * shear * inverse


def slabs_y(
    u_ref,
    w_ref,
    r_ref,
    moduli_hbm,
    even_ref,
    odd_ref,
    ux_ref,
    wx_ref,
    field_ref,
    down_ref,
    up_ref,
    moduli_ref,
    moduli_sem,
):
    fetch = pltpu.make_async_copy(moduli_hbm, moduli_ref, moduli_sem)
    fetch.start()
    parity = lax.axis_index("gx") % 2
    zero = jnp.zeros((8, LANES), F32)
    for y in (-3, -2, -1, 8, 9, 10):
        for lead in range(21):
            for x in (-8, 0, 8):
                ux_ref[lead, pl.ds((x + 8) * SU + y + 3, 8, stride=SU), :] = zero
    for y in range(8):
        for c in range(3):
            tile = U_TILE + c * 6
            left, right = halves(even_ref, odd_ref, parity, tile - 2, tile, y)
            own = u_ref[pl.ds(c * 64 + y, 8, stride=8), :]
            for x, value in ((-8, left), (8, right), (0, own)):
                for shift in range(-3, 4):
                    ux_ref[
                        c * 7 + shift + 3, pl.ds((x + 8) * SU + y + 3, 8, stride=SU), :
                    ] = rolled(value, shift)
        for k in range(WORDS + 1):
            if k < WORDS:
                left, right = halves(even_ref, odd_ref, parity, k * 4, k * 4, y)
                own = w_ref[pl.ds(k * 64 + y, 8, stride=8), :]
                places = (-4, 8)
            else:
                left, right = halves(even_ref, odd_ref, parity, R_TILE - 5, R_TILE - 5, y)
                own = r_ref[pl.ds(y, 8, stride=8), :]
                places = (-8, 3)
            for x, value in (
                (places[0], left.astype(jnp.int32)),
                (places[1], right.astype(jnp.int32)),
                (0, own),
            ):
                wx_ref[k, pl.ds((x + 8) * SW + y, 8, stride=SW), :] = value

    def row(index, carry):
        y = index + jnp.where(index < 3, 0, 2)
        for x0 in BLOCKS:
            field_ref[0, pl.ds((x0 + 4) * SF + y, 8, stride=SF), :] = inner_sum(
                ux_ref, wx_ref, x0, y
            )
        return carry

    lax.fori_loop(0, 6, row, 0)
    fetch.wait()
    for y in EDGE_ROWS:
        for x0 in BLOCKS:
            rows = pl.ds((x0 + 4) * SF + y, 8, stride=SF)
            field_ref[1, rows, :], field_ref[2, rows, :] = ratios(wx_ref, moduli_ref, x0, y)
    for ref, first in ((down_ref, 0), (up_ref, 5)):
        for i in range(3):
            for d in range(3):
                y = first + d
                j = i * 3 + d
                for x in (-5, 3, 5):
                    ref[pl.ds((x + 5) * 9 + j, 8, stride=9), :] = u_at(ux_ref, i, 0, x, y)
                for x in (-2, 2):
                    ref[pl.ds(FIELDS + (x + 2) * 9 + j, 8, stride=9), :] = field_at(
                        field_ref, i, x, y
                    )


def fold(force, column, a, b):
    force = list(force)
    total = None
    for value in column.values():
        total = value if total is None else total + value
    for i, factor in ((0, a), (1, b)):
        if factor != 0:
            term = scaled(total, factor)
            force[i] = term if force[i] is None else force[i] + term
    for c, value in column.items():
        if c > 0:
            term = scaled(value - column[-c], c)
            force[2] = term if force[2] is None else force[2] + term
    return force


def inner_force(
    ux_ref,
    wx_ref,
    field_ref,
    moduli_hbm,
    middle_ref,
    part_ref,
    sum_ref,
    step_ref,
    sx_ref,
    moduli_ref,
    moduli_sem,
):
    fetch = pltpu.make_async_copy(moduli_hbm, moduli_ref, moduli_sem)
    fetch.start()
    zero = jnp.zeros((8, LANES), F32)
    for x in BLOCKS:
        for y in (-3, -2, -1, 8, 9, 10):
            for lead in range(7):
                sx_ref[lead, pl.ds((x + 4) * SU + y + 3, 8, stride=SU), :] = zero
    fetch.wait()
    for y in range(8):
        step_ref[y] = time_step / chosen(word_at(wx_ref, WORDS, 0, y), moduli_ref, 2)
        for index, x in enumerate(BLOCKS):
            if y in EDGE_ROWS:
                shear = field_at(field_ref, 2, x, y)
            else:
                place = (index * 2 + y - 3) * 3
                middle_ref[place] = inner_sum(ux_ref, wx_ref, x, y)
                middle_ref[place + 1], shear = ratios(wx_ref, moduli_ref, x, y)
                middle_ref[place + 2] = shear
            for shift in range(-3, 4):
                sx_ref[
                    shift + 3, pl.ds((x + 4) * SU + y + 3, 8, stride=SU), :
                ] = rolled(shear, shift)

    def row(y, carry):
        own = [u_at(ux_ref, c, 0, 0, y) for c in range(3)]
        shear = px_at(sx_ref, 0, 0, y)
        force = [None, None, None]
        balance = [None, None, None]
        word = None
        column = {}
        count = {}
        for number, offset in enumerate(OFFSETS):
            if number % bits_per_word == 0:
                word = word_at(wx_ref, number // bits_per_word, 0, y)
            a, b, c = offset
            difference = [
                u_at(ux_ref, i, c, a, y + b) - own[i] if offset[i] != 0 else None
                for i in range(3)
            ]
            cls = square(offset)
            value = (shear + px_at(sx_ref, c, a, y + b)) * combined(difference, offset)
            held = bit(word, number)
            column[c] = jnp.where(held, value * (1.0 / (cls * math.sqrt(cls))), 0.0)
            count[c] = jnp.where(held, F32(1.0 / math.sqrt(cls)), F32(0.0))
            if number + 1 == len(OFFSETS) or OFFSETS[number + 1][:2] != (a, b):
                force = fold(force, column, a, b)
                balance = fold(balance, count, a, b)
                column = {}
                count = {}
        for i in range(3):
            part_ref[i * 8 + y] = force[i]
            sum_ref[i * 8 + y] = balance[i]
        return carry

    lax.fori_loop(0, 8, row, 0)


def halo_y(h):
    return h - 3 if h < 3 else h + 5


def outer_force(
    below_ref,
    above_ref,
    ux_ref,
    wx_ref,
    field_ref,
    middle_ref,
    part_ref,
    sum_ref,
    step_ref,
    u_ref,
    v_ref,
    new_u_ref,
    new_v_ref,
    uh_ref,
    hd_ref,
    sh_ref,
    px_ref,
    force_ref,
):
    halo = (below_ref, above_ref)
    zero = jnp.zeros((8, LANES), F32)
    for h in range(6):
        for i in range(3):
            for x in (-5, 3, 5):
                value = halo[h // 3][pl.ds((x + 5) * 9 + i * 3 + h % 3, 8, stride=9), :]
                for shift in range(-3, 4):
                    uh_ref[
                        i * 7 + shift + 3, pl.ds((x + 6) * SH + h, 8, stride=SH), :
                    ] = rolled(value, shift)
        for x in (-6, 2, 6):
            hd_ref[pl.ds((x + 6) * SH + h, 8, stride=SH), :] = zero

    for index, x0 in enumerate(BLOCKS):
        rest = {}
        for h in range(6):
            for a in range(-2, 3):
                spread = None
                for c in range(-2, 3):
                    gathered = None
                    for y in range(8):
                        offset = (a, halo_y(h) - y, c)
                        if offset not in NUMBERS:
                            continue
                        number = NUMBERS[offset]
                        factor = 1.0 / math.sqrt(square(offset))
                        held = bit(word_at(wx_ref, number // bits_per_word, x0, y), number)
                        far = [
                            uh_at(uh_ref, i, c, x0 + a, h) if offset[i] != 0 else None
                            for i in range(3)
                        ]
                        own = [
                            u_at(ux_ref, i, 0, x0, y) if offset[i] != 0 else None
                            for i in range(3)
                        ]
                        add_to(
                            rest, y, jnp.where(held, combined(far, offset) * factor, 0.0)
                        )
                        term = jnp.where(held, combined(own, offset) * factor, 0.0)
                        gathered = term if gathered is None else gathered + term
                    if gathered is not None:
                        value = rolled(gathered, -c)
                        spread = value if spread is None else spread + value
                if spread is not None:
                    rows = pl.ds((x0 + a + 6) * SH + h, 8, stride=SH)
                    hd_ref[rows, :] = hd_ref[rows, :] - spread
        for y in range(8):
            if y in EDGE_ROWS:
                total = field_at(field_ref, 0, x0, y) + rest[y]
                pressure = total * field_at(field_ref, 1, x0, y)
            else:
                place = (index * 2 + y - 3) * 3
                pressure = middle_ref[place] * middle_ref[place + 1]
            for shift in range(-3, 4):
                px_ref[
                    shift + 3, pl.ds((x0 + 4) * SU + y + 3, 8, stride=SU), :
                ] = rolled(pressure, shift)
    for h in range(6):
        for x in (-2, 2):
            part, ratio, shear = [
                halo[h // 3][pl.ds(FIELDS + (x + 2) * 9 + i * 3 + h % 3, 8, stride=9), :]
                for i in range(3)
            ]
            pressure = (part + hd_ref[pl.ds((x + 6) * SH + h, 8, stride=SH), :]) * ratio
            for shift in range(-3, 4):
                px_ref[
                    shift + 3, pl.ds((x + 4) * SU + halo_y(h) + 3, 8, stride=SU), :
                ] = rolled(pressure, shift)
                sh_ref[shift + 3, pl.ds((x + 2) * SH + h, 8, stride=SH), :] = rolled(
                    shear, shift
                )

    def row(y, carry):
        pressure = px_at(px_ref, 0, 0, y)
        force = [part_ref[i * 8 + y] + pressure * sum_ref[i * 8 + y] for i in range(3)]
        word = None
        column = {}
        for number, offset in enumerate(OFFSETS):
            if number % bits_per_word == 0:
                word = word_at(wx_ref, number // bits_per_word, 0, y)
            a, b, c = offset
            column[c] = jnp.where(
                bit(word, number),
                px_at(px_ref, c, a, y + b) * (1.0 / math.sqrt(square(offset))),
                0.0,
            )
            if number + 1 == len(OFFSETS) or OFFSETS[number + 1][:2] != (a, b):
                force = fold(force, column, a, b)
                column = {}
        for i in range(3):
            force_ref[i * 8 + y] = force[i]
        return carry

    lax.fori_loop(0, 8, row, 0)

    for y in range(8):
        force = [force_ref[i * 8 + y] for i in range(3)]
        own = [u_at(ux_ref, c, 0, 0, y) for c in range(3)]
        if y in EDGE_ROWS:
            shear = field_at(field_ref, 2, 0, y)
        column = {}
        bonds = crossing(y)
        for position, (number, offset, h) in enumerate(bonds):
            word = word_at(wx_ref, number // bits_per_word, 0, y)
            a, b, c = offset
            cls = square(offset)
            far = [
                uh_at(uh_ref, i, c, a, h) if offset[i] != 0 else None for i in range(3)
            ]
            reach = combined(far, offset)
            along = combined(
                [far[i] - own[i] if offset[i] != 0 else None for i in range(3)], offset
            )
            far_shear = sh_ref[c + 3, pl.ds((a + 2) * SH + h, 8, stride=SH), :]
            value = (far_shear * along + shear * reach) * (1.0 / (cls * math.sqrt(cls)))
            column[c] = jnp.where(bit(word, number), value, 0.0)
            if position + 1 == len(bonds) or bonds[position + 1][1][:2] != (a, b):
                force = fold(force, column, a, b)
                column = {}
        step = step_ref[y]
        for i in range(3):
            rows = pl.ds(i * 64 + y, 8, stride=8)
            velocity = v_ref[rows, :] + force[i] * step
            new_v_ref[rows, :] = velocity
            new_u_ref[rows, :] = u_ref[rows, :] + time_step * velocity


def call(body, outs, args, unplaced=(), scratch=(), flops=1000):
    vmem = pl.BlockSpec(memory_space=pltpu.VMEM)
    unmoved = pl.BlockSpec(memory_space=pltpu.HBM)
    return pl.pallas_call(
        body,
        out_shape=[jax.ShapeDtypeStruct(shape, dtype) for shape, dtype in outs],
        in_specs=[unmoved if position in unplaced else vmem for position in range(len(args))],
        out_specs=[vmem for _ in outs],
        scratch_shapes=scratch,
        cost_estimate=pl.CostEstimate(flops=flops, bytes_accessed=100000, transcendentals=0),
        compiler_params=pltpu.CompilerParams(vmem_limit_bytes=16 * 1024 * 1024),
    )(
        *[
            pltpu.with_memory_space_constraint(arg, pltpu.HBM) if position in unplaced else arg
            for position, arg in enumerate(args)
        ]
    )


def along_y(down, up):
    size = lax.axis_size("gy")
    upward = [(i, i + 1) for i in range(size - 1)]
    downward = [(i + 1, i) for i in range(size - 1)]
    below = lax.ppermute(up, "gy", upward)
    above = lax.ppermute(down, "gy", downward)
    return below, above


def on_device(displacement, velocity, region, bond_words, moduli):
    copy = pltpu.SemaphoreType.DMA(())
    odd, even, u, words, region = call(
        slabs_x,
        [((SLAB, 8, LANES), F32)] * 2
        + [(x.shape, x.dtype) for x in (displacement, bond_words, region)],
        (displacement, bond_words, region),
        unplaced=(0, 1, 2),
        scratch=[copy, copy, copy],
    )
    size = lax.axis_size("gx")
    odd = lax.ppermute(
        odd, "gx", [(i, ((i - 1) ^ 1) + 1) for i in range(1, size - 1)]
    )
    even = lax.ppermute(even, "gx", [(i, i ^ 1) for i in range(size)])
    even = even.reshape(SLAB * 8, LANES)
    odd = odd.reshape(SLAB * 8, LANES)
    u = u.reshape(192, LANES)
    ux, wx, fields, down, up = call(
        slabs_y,
        [
            ((21, 24 * SU, LANES), F32),
            ((12, 24 * SW, LANES), jnp.int32),
            ((3, 16 * SF, LANES), F32),
            ((FIELDS + 108, LANES), F32),
            ((FIELDS + 108, LANES), F32),
        ],
        (u, words.reshape(704, LANES), region.reshape(64, LANES), moduli, even, odd),
        unplaced=(3,),
        scratch=[pltpu.SMEM(moduli.shape, F32), copy],
        flops=20_000_000,
    )
    below, above = along_y(down, up)
    middle, part, balance, step = call(
        inner_force,
        [
            ((12, 8, LANES), F32),
            ((24, 8, LANES), F32),
            ((24, 8, LANES), F32),
            ((8, 8, LANES), F32),
        ],
        (ux, wx, fields, moduli),
        unplaced=(3,),
        scratch=[
            pltpu.VMEM((7, 16 * SU, LANES), F32),
            pltpu.SMEM(moduli.shape, F32),
            copy,
        ],
        flops=40_000_000,
    )
    new_u, new_v = call(
        outer_force,
        [((192, LANES), F32)] * 2,
        (
            below,
            above,
            ux,
            wx,
            fields,
            middle,
            part,
            balance,
            step,
            u,
            velocity.reshape(192, LANES),
        ),
        scratch=[
            pltpu.VMEM((21, 20 * SH, LANES), F32),
            pltpu.VMEM((20 * SH, LANES), F32),
            pltpu.VMEM((7, 12 * SH, LANES), F32),
            pltpu.VMEM((7, 16 * SU, LANES), F32),
            pltpu.VMEM((24, 8, LANES), F32),
        ],
        flops=10_000_000,
    )
    return new_u.reshape(displacement.shape), new_v.reshape(velocity.shape)


def solution(mesh):
    placed = (
        P(None, "gx", "gy", None),
        P(None, "gx", "gy", None),
        P("gx", "gy", None),
        P(None, "gx", "gy", None),
        P(),
    )
    return jax.shard_map(
        on_device,
        mesh=mesh,
        in_specs=placed,
        out_specs=(P(None, "gx", "gy", None), P(None, "gx", "gy", None)),
        check_vma=False,
    )
```

time: 45.8 us -> 40.6 us (0.89)
  the two profiles are of different devices: /device:TPU:56 before, /device:TPU:28 now
where the time goes in v3:
time: 40.6 us; the launch traced here: 40.3 us
  starting transfers between devices  21.3 us (52%)
  Pallas kernels  11 us (27%)
  waiting for transfers between devices  7.29 us (18%)
  between operations  0.71 us (2%)
    pallas_call x4, Pallas kernels, call(): pl.pallas_call(body, out_shape=[jax.ShapeDtypeStruct(shape, dtype) for sh...  11 us
    ppermute x1, starting transfers between devices, on_device(): lax.ppermute(odd, 'gx', [(i, (i - 1 ^ 1) + 1) for i in range(1, size - 1)])  10.9 us
    ppermute x1, starting transfers between devices, along_y(): below = lax.ppermute(up, 'gy', upward)  6.53 us
    ppermute x1, waiting for transfers between devices, on_device(): lax.ppermute(odd, 'gx', [(i, (i - 1 ^ 1) + 1) for i in range(1, size - 1)])  4.07 us
    ppermute x1, waiting for transfers between devices, along_y(): above = lax.ppermute(down, 'gy', downward)  3.21 us
    ppermute x1, starting transfers between devices, along_y(): above = lax.ppermute(down, 'gy', downward)  1.92 us
    ppermute x1, starting transfers between devices, on_device(): even = lax.ppermute(even, 'gx', [(i, i ^ 1) for i in range(size)])  1.92 us
  transfers between devices with their start and end apart: 4, of which 2 were waited for; matrix products, arithmetic and copies ran while one was open for 0% of the time, Pallas kernels for 10%

profile of v3, /device:TPU:28, one launch (start us, length us, event | category | flops | bytes accessed | tf_op | source)
XLA Modules:
  0.0 40.3 jit_solution(11028357924069996436)
XLA Ops:
  0.6 0.0 copy-start
  0.6 1.1 %shard_map.68 = (f32[65,8,128]{2,1,0:T(8,128)S(1)}, f32[65,8,128]{2,1,0:T(8,128)S(1)}, f32[3,8,8,128]{3,2,1,0:T(8,128)S(1)}, s32[11,8,8,128]{3,2,1,0:T(8,128)S(1)}, s32[8,8,128]{2,1,0:T(8,128)S(1)}) custom-call(f32[3,8,8,128]{3,2,1,0:T(8,128)} %u_hbm.1, s32[11,8,8,128]{3,2,1,0:T(8,128)} %w_hbm.1, s32[8,8,128]{2,1,0:T(8,128)} %r_hbm.1), custom_call_target="tpu_custom_call" | custom-call | flops 1000 | bytes 100000 | tf_op jit(solution)/shard_map/pallas_call | solution.py:513
  1.7 1.9 %collective-permute-start = (f32[65,8,128]{2,1,0:T(8,128)S(1)}, f32[65,8,128]{2,1,0:T(8,128)S(1)}, u32[]{:S(2)}, u32[]{:S(2)}) collective-permute-start(f32[65,8,128]{2,1,0:T(8,128)S(1)} %get-tuple-element.21), channel_id=1, source_target_pairs={{0,16},{16,0},{32,48},{48,32},{64,80},{80,64},{96,112},{112,96},{1... | collective-permute-start | bytes 798728 | tf_op jit(solution)/shard_map/ppermute | solution.py:552
  3.7 10.9 %collective-permute-start.1 = (f32[65,8,128]{2,1,0:T(8,128)S(1)}, f32[65,8,128]{2,1,0:T(8,128)S(1)}, u32[]{:S(2)}, u32[]{:S(2)}) collective-permute-start(f32[65,8,128]{2,1,0:T(8,128)S(1)} %get-tuple-element.22), channel_id=1, source_target_pairs={{16,32},{32,16},{48,64},{64,48},{80,96},{96,80},{112,128},{128,112... | collective-permute-start | bytes 798728 | tf_op jit(solution)/shard_map/ppermute | solution.py:549
  14.6 0.0 collective-permute-done
  14.6 4.1 %collective-permute-done.1 = f32[65,8,128]{2,1,0:T(8,128)S(1)} collective-permute-done((f32[65,8,128]{2,1,0:T(8,128)S(1)}, f32[65,8,128]{2,1,0:T(8,128)S(1)}, u32[]{:S(2)}, u32[]{:S(2)}) %collective-permute-start.1) | collective-permute-done | bytes 266272 | tf_op jit(solution)/shard_map/ppermute | solution.py:549
  18.7 3.0 %shard_map.69 = (f32[21,336,128]{2,1,0:T(8,128)S(1)}, s32[12,216,128]{2,1,0:T(8,128)S(1)}, f32[3,144,128]{2,1,0:T(8,128)S(1)}, f32[270,128]{1,0:T(8,128)S(1)}, f32[270,128]{1,0:T(8,128)S(1)}) custom-call(f32[192,128]{1,0:T(8,128)S(1)} %bitcast.8, s32[704,128]{1,0:T(8,128)S(1)} %bitcast.10, s32[64,128]{1,0:T(8,128)S(1)} %bitcast.14, f32[3,4]{1,0:T(4,128)} %moduli_hbm.3, ...), custom_call_target="tpu_custom_call" | custom-call | flops 20000000 | bytes 100000 | tf_op jit(solution)/shard_map/pallas_call | solution.py:513
  21.7 6.5 %collective-permute-start.2 = (f32[270,128]{1,0:T(8,128)S(1)}, f32[270,128]{1,0:T(8,128)S(1)}, u32[]{:S(2)}, u32[]{:S(2)}) collective-permute-start(f32[270,128]{1,0:T(8,128)S(1)} %get-tuple-element.23), channel_id=1, source_target_pairs={{0,1},{1,2},{2,3},{3,4},{4,5},{5,6},{6,7},{7,8},{8,9},{9,10},{10,1... | collective-permute-start | bytes 414728 | tf_op jit(solution)/shard_map/ppermute | solution.py:533
  28.2 1.9 %collective-permute-start.3 = (f32[270,128]{1,0:T(8,128)S(1)}, f32[270,128]{1,0:T(8,128)S(1)}, u32[]{:S(2)}, u32[]{:S(2)}) collective-permute-start(f32[270,128]{1,0:T(8,128)S(1)} %get-tuple-element.24), channel_id=1, source_target_pairs={{1,0},{2,1},{3,2},{4,3},{5,4},{6,5},{7,6},{8,7},{9,8},{10,9},{11,1... | collective-permute-start | bytes 414728 | tf_op jit(solution)/shard_map/ppermute | solution.py:534
  30.1 3.9 %shard_map.70 = (f32[12,8,128]{2,1,0:T(8,128)S(1)}, f32[24,8,128]{2,1,0:T(8,128)S(1)}, f32[24,8,128]{2,1,0:T(8,128)S(1)}, f32[8,8,128]{2,1,0:T(8,128)S(1)}) custom-call(f32[21,336,128]{2,1,0:T(8,128)S(1)} %get-tuple-element.25.ux_ref, s32[12,216,128]{2,1,0:T(8,128)S(1)} %get-tuple-element.26.wx_ref, f32[3,144,128]{2,1,0:T(8,128)S(1)} %get-tuple-element.27.field_ref, ...), custom_call_target="tpu_custom_call" | custom-call | flops 40000000 | bytes 100000 | tf_op jit(solution)/shard_map/pallas_call | solution.py:513
  34.1 0.0 collective-permute-done.2.below_ref
  34.1 3.2 %collective-permute-done.3.above_ref = f32[270,128]{1,0:T(8,128)S(1)} collective-permute-done((f32[270,128]{1,0:T(8,128)S(1)}, f32[270,128]{1,0:T(8,128)S(1)}, u32[]{:S(2)}, u32[]{:S(2)}) %collective-permute-start.3) | collective-permute-done | bytes 138272 | tf_op jit(solution)/shard_map/ppermute | solution.py:534
  37.3 0.0 copy-done
  37.3 3.1 %shard_map.71 = (f32[192,128]{1,0:T(8,128)}, f32[192,128]{1,0:T(8,128)}) custom-call(f32[270,128]{1,0:T(8,128)S(1)} %collective-permute-done.2.below_ref, f32[270,128]{1,0:T(8,128)S(1)} %collective-permute-done.3.above_ref, f32[21,336,128]{2,1,0:T(8,128)S(1)} %get-tuple-element.25.ux_ref, s32[12,216,128]{2,1,0:T(8,128)S(1)} %get-tuple-element.26.wx_ref, ...), custom_call_target="tpu_custom_call" | custom-call | flops 10000000 | bytes 100000 | tf_op jit(solution)/shard_map/pallas_call | solution.py:513
Async XLA Ops:
  0.6 36.6 %copy-start = (f32[3,8,8,128]{3,2,1,0:T(8,128)S(1)}, f32[3,8,8,128]{3,2,1,0:T(8,128)}, u32[]{:S(2)}) copy-start(f32[3,8,8,128]{3,2,1,0:T(8,128)} %param.6) | copy-start | bytes 294916
  1.7 12.9 %collective-permute-start = (f32[65,8,128]{2,1,0:T(8,128)S(1)}, f32[65,8,128]{2,1,0:T(8,128)S(1)}, u32[]{:S(2)}, u32[]{:S(2)}) collective-permute-start(f32[65,8,128]{2,1,0:T(8,128)S(1)} %get-tuple-element.21), channel_id=1, source_target_pairs={{0,16},{16,0},{32,48},{48,32},{64,80},{80,64},{96,112},{112,96},{1... | collective-permute-start | bytes 798728 | tf_op jit(solution)/shard_map/ppermute | solution.py:552
  3.7 15.0 %collective-permute-start.1 = (f32[65,8,128]{2,1,0:T(8,128)S(1)}, f32[65,8,128]{2,1,0:T(8,128)S(1)}, u32[]{:S(2)}, u32[]{:S(2)}) collective-permute-start(f32[65,8,128]{2,1,0:T(8,128)S(1)} %get-tuple-element.22), channel_id=1, source_target_pairs={{16,32},{32,16},{48,64},{64,48},{80,96},{96,80},{112,128},{128,112... | collective-permute-start | bytes 798728 | tf_op jit(solution)/shard_map/ppermute | solution.py:549
  21.7 12.4 %collective-permute-start.2 = (f32[270,128]{1,0:T(8,128)S(1)}, f32[270,128]{1,0:T(8,128)S(1)}, u32[]{:S(2)}, u32[]{:S(2)}) collective-permute-start(f32[270,128]{1,0:T(8,128)S(1)} %get-tuple-element.23), channel_id=1, source_target_pairs={{0,1},{1,2},{2,3},{3,4},{4,5},{5,6},{6,7},{7,8},{8,9},{9,10},{10,1... | collective-permute-start | bytes 414728 | tf_op jit(solution)/shard_map/ppermute | solution.py:533
  28.2 9.1 %collective-permute-start.3 = (f32[270,128]{1,0:T(8,128)S(1)}, f32[270,128]{1,0:T(8,128)S(1)}, u32[]{:S(2)}, u32[]{:S(2)}) collective-permute-start(f32[270,128]{1,0:T(8,128)S(1)} %get-tuple-element.24), channel_id=1, source_target_pairs={{1,0},{2,1},{3,2},{4,3},{5,4},{6,5},{7,6},{8,7},{9,8},{10,9},{11,1... | collective-permute-start | bytes 414728 | tf_op jit(solution)/shard_map/ppermute | solution.py:534

commit v4 on v3

--- a/solution.py
+++ b/solution.py
@@ -30,15 +30,17 @@
     return offset[0] * offset[0] + offset[1] * offset[1] + offset[2] * offset[2]
 
 
+UX_ROWS = 20 * 28
+WX_ROWS = 16 * 18
+FX_ROWS = 16 * 18
 SU = 14
-SW = 9
 SH = 7
-SF = 9
 BLOCKS = (-4, 4)
-U_TILE = 44
-R_TILE = 62
-SLAB = 65
-FIELDS = 162
+EXTRA_TILE = 33
+U_TILE = 36
+R_TILE = 54
+SLAB = 57
+SLAB_Y = 246
 EDGE_ROWS = (0, 1, 2, 5, 6, 7)
 
 
@@ -46,16 +48,48 @@
     return value if shift == 0 else pltpu.roll(value, (-shift) % LANES, 1)
 
 
+def ux_rows(x, y):
+    return pl.ds(((x + 6) * 14 + y + 3) * 2, 8, stride=28)
+
+
+def ux_column(x, y=0):
+    return pl.ds(((x + 6) * 14 + y + 3) * 2, 8, stride=2)
+
+
+def fx_rows(x, y):
+    return pl.ds(((x + 4) * 9 + y) * 2, 8, stride=18)
+
+
+def fx_column(x):
+    return pl.ds((x + 4) * 18, 8, stride=2)
+
+
 def u_at(ref, component, shift, x, y):
-    return ref[component * 7 + shift + 3, pl.ds((x + 8) * SU + y + 3, 8, stride=SU), :]
+    return ref[component * 7 + shift + 3, ux_rows(x, y), :]
 
 
 def word_at(ref, k, x, y):
-    return ref[k, pl.ds((x + 8) * SW + y, 8, stride=SW), :]
+    return ref[k, fx_rows(x, y), :]
 
 
 def uh_at(ref, component, shift, x, h):
-    return ref[component * 7 + shift + 3, pl.ds((x + 6) * SH + h, 8, stride=SH), :]
+    return ref[component * 5 + shift + 2, pl.ds((x + 6) * SH + h, 8, stride=SH), :]
+
+
+def slab_u(component, depth, x):
+    if depth < 2:
+        return pl.ds((x + 5) * 6 + component * 2 + depth, 8, stride=6)
+    return pl.ds(108 + (x + 3) * 3 + component, 8, stride=3)
+
+
+def slab_field(field, depth, x):
+    if depth < 2:
+        return pl.ds(150 + (x + 2) * 6 + field * 2 + depth, 8, stride=6)
+    return pl.ds(222 + x * 3 + field, 8, stride=3)
+
+
+def slab_places(depth):
+    return ((-5, 3, 5), (-2, 2)) if depth < 2 else ((-3, 3), (0,))
 
 
 def scaled(value, factor):
@@ -109,7 +143,7 @@
 
 
 def field_at(ref, field, x, y):
-    return ref[field, pl.ds((x + 4) * SF + y, 8, stride=SF), :]
+    return ref[field, fx_rows(x, y), :]
 
 
 def crossing(y):
@@ -138,8 +172,10 @@
         copy.wait()
     for ref, right in ((even_ref, 1 - parity), (odd_ref, parity)):
         for k in range(WORDS):
-            for d in range(4):
-                ref[k * 4 + d] = w_ref[k, right * 4 + d].astype(F32)
+            for d in range(3):
+                ref[k * 3 + d] = w_ref[k, right * 5 + d].astype(F32)
+        for d in range(3):
+            ref[EXTRA_TILE + d] = w_ref[right * 8 + d, right + 3].astype(F32)
         for c in range(3):
             for d in range(6):
                 ref[U_TILE + c * 6 + d] = u_ref[c, right * 2 + d]
@@ -147,37 +183,31 @@
             ref[R_TILE + d] = r_ref[right * 5 + d].astype(F32)
 
 
-def halves(even_ref, odd_ref, parity, tile_left, tile_right, y):
-    def pick(tile, left):
-        rows = pl.ds(tile * 8 + y, 8, stride=8)
-        even, odd = (even_ref[rows, :], odd_ref[rows, :])
-        return jnp.where(parity == 0, odd, even) if left else jnp.where(parity == 0, even, odd)
-
-    return pick(tile_left, True), pick(tile_right, False)
-
-
-def inner_sum(ux_ref, wx_ref, x0, y):
-    own = [u_at(ux_ref, c, 0, x0, y) for c in range(3)]
+def column_sum(ux_ref, words, x, inside):
+    own = [ux_ref[i * 7 + 3, ux_column(x), :] for i in range(3)]
     sums = {}
-    word = None
+    loaded = None
     for number, offset in enumerate(OFFSETS):
-        if number % bits_per_word == 0:
-            word = word_at(wx_ref, number // bits_per_word, x0, y)
+        if not inside(x + offset[0]):
+            continue
+        if loaded != number // bits_per_word:
+            loaded = number // bits_per_word
+            word = words(loaded)
         difference = [
-            u_at(ux_ref, c, offset[2], x0 + offset[0], y + offset[1]) - own[c]
-            if offset[c] != 0
+            ux_ref[i * 7 + offset[2] + 3, ux_column(x + offset[0], offset[1]), :] - own[i]
+            if offset[i] != 0
             else None
-            for c in range(3)
+            for i in range(3)
         ]
         along = combined(difference, offset)
         add_to(sums, square(offset), jnp.where(bit(word, number), along, 0.0))
     return by_class(sums)
 
 
-def ratios(wx_ref, moduli_ref, x0, y):
+def ratios(words, region, moduli_ref):
     counts = {}
     for k in range(WORDS):
-        word = word_at(wx_ref, k, x0, y)
+        word = words(k)
         group = OFFSETS[k * bits_per_word : (k + 1) * bits_per_word]
         for cls in CLASSES:
             held = sum(1 << i for i, offset in enumerate(group) if square(offset) == cls)
@@ -188,21 +218,71 @@
         term = counts[cls].astype(F32) * math.sqrt(cls)
         volume = term if volume is None else volume + term
     inverse = 1.0 / jnp.where(volume > 0.0, volume, 1.0)
-    region = word_at(wx_ref, WORDS, x0, y)
     bulk = chosen(region, moduli_ref, 0)
     shear = chosen(region, moduli_ref, 1)
     return (3.0 * inverse) * ((3.0 * bulk - 5.0 * shear) * inverse), 15.0 * shear * inverse
 
 
+def spread_column(ux_ref, component, x, value):
+    for shift in range(-3, 4):
+        ux_ref[component * 7 + shift + 3, ux_column(x), :] = rolled(value, shift)
+
+
+def own_part(u_ref, w_ref, r_ref, moduli_hbm, ux_ref, own_ref, moduli_ref, moduli_sem):
+    fetch = pltpu.make_async_copy(moduli_hbm, moduli_ref, moduli_sem)
+    fetch.start()
+    zero = jnp.zeros((8, LANES), F32)
+    for i in range(3):
+        for x in range(8):
+            spread_column(ux_ref, i, x, u_ref[pl.ds(i * 64 + x * 8, 8), :])
+        for shift in range(-2, 3):
+            for y in (-3, -2, -1, 8, 9, 10):
+                for x in (-6, 2, 6):
+                    ux_ref[i * 7 + shift + 3, ux_rows(x, y), :] = zero
+    for x in range(8):
+        own_ref[x] = column_sum(
+            ux_ref,
+            lambda k, x=x: w_ref[pl.ds(k * 64 + x * 8, 8), :],
+            x,
+            lambda far: 0 <= far < 8,
+        )
+    fetch.wait()
+    for x in range(8):
+        own_ref[8 + x], own_ref[16 + x] = ratios(
+            lambda k, x=x: w_ref[pl.ds(k * 64 + x * 8, 8), :],
+            r_ref[pl.ds(x * 8, 8), :],
+            moduli_ref,
+        )
+
+
+def halo_reader(even_ref, odd_ref):
+    parity = lax.axis_index("gx") % 2
+
+    def tile(index, left):
+        rows = pl.ds(index * 8, 8)
+        even, odd = (even_ref[rows, :], odd_ref[rows, :])
+        return jnp.where(parity == 0, odd, even) if left else jnp.where(parity == 0, even, odd)
+
+    def word(k, x):
+        d = x + 3 if x < 0 else x - 8
+        return tile(k * 3 + d, x < 0).astype(jnp.int32)
+
+    def region(x):
+        d = x + 3 if x < 0 else x - 8
+        return tile(R_TILE + d, x < 0).astype(jnp.int32)
+
+    return tile, word, region
+
+
 def slabs_y(
     u_ref,
     w_ref,
-    r_ref,
+    own_ref,
     moduli_hbm,
     even_ref,
     odd_ref,
+    ux_in_ref,
     ux_ref,
-    wx_ref,
     field_ref,
     down_ref,
     up_ref,
@@ -211,63 +291,41 @@
 ):
     fetch = pltpu.make_async_copy(moduli_hbm, moduli_ref, moduli_sem)
     fetch.start()
-    parity = lax.axis_index("gx") % 2
-    zero = jnp.zeros((8, LANES), F32)
-    for y in (-3, -2, -1, 8, 9, 10):
-        for lead in range(21):
-            for x in (-8, 0, 8):
-                ux_ref[lead, pl.ds((x + 8) * SU + y + 3, 8, stride=SU), :] = zero
-    for y in range(8):
-        for c in range(3):
-            tile = U_TILE + c * 6
-            left, right = halves(even_ref, odd_ref, parity, tile - 2, tile, y)
-            own = u_ref[pl.ds(c * 64 + y, 8, stride=8), :]
-            for x, value in ((-8, left), (8, right), (0, own)):
-                for shift in range(-3, 4):
-                    ux_ref[
-                        c * 7 + shift + 3, pl.ds((x + 8) * SU + y + 3, 8, stride=SU), :
-                    ] = rolled(value, shift)
-        for k in range(WORDS + 1):
-            if k < WORDS:
-                left, right = halves(even_ref, odd_ref, parity, k * 4, k * 4, y)
-                own = w_ref[pl.ds(k * 64 + y, 8, stride=8), :]
-                places = (-4, 8)
-            else:
-                left, right = halves(even_ref, odd_ref, parity, R_TILE - 5, R_TILE - 5, y)
-                own = r_ref[pl.ds(y, 8, stride=8), :]
-                places = (-8, 3)
-            for x, value in (
-                (places[0], left.astype(jnp.int32)),
-                (places[1], right.astype(jnp.int32)),
-                (0, own),
-            ):
-                wx_ref[k, pl.ds((x + 8) * SW + y, 8, stride=SW), :] = value
-
-    def row(index, carry):
-        y = index + jnp.where(index < 3, 0, 2)
-        for x0 in BLOCKS:
-            field_ref[0, pl.ds((x0 + 4) * SF + y, 8, stride=SF), :] = inner_sum(
-                ux_ref, wx_ref, x0, y
+    tile, halo_word, halo_region = halo_reader(even_ref, odd_ref)
+    for i in range(3):
+        for d in range(6):
+            spread_column(ux_ref, i, d - 6, tile(U_TILE + i * 6 + d, True))
+            spread_column(ux_ref, i, d + 8, tile(U_TILE + i * 6 + d, False))
+    for x in range(8):
+        value = own_ref[x]
+        if x < 3 or x > 4:
+            value = value + column_sum(
+                ux_ref,
+                lambda k, x=x: w_ref[pl.ds(k * 64 + x * 8, 8), :],
+                x,
+                lambda far: far < 0 or far > 7,
             )
-        return carry
-
-    lax.fori_loop(0, 6, row, 0)
+        field_ref[0, fx_column(x), :] = value
+        field_ref[1, fx_column(x), :] = own_ref[8 + x]
+        field_ref[2, fx_column(x), :] = own_ref[16 + x]
+    for x in (-2, -1, 8, 9):
+        field_ref[0, fx_column(x), :] = column_sum(
+            ux_ref, lambda k, x=x: halo_word(k, x), x, lambda far: True
+        )
     fetch.wait()
-    for y in EDGE_ROWS:
-        for x0 in BLOCKS:
-            rows = pl.ds((x0 + 4) * SF + y, 8, stride=SF)
-            field_ref[1, rows, :], field_ref[2, rows, :] = ratios(wx_ref, moduli_ref, x0, y)
-    for ref, first in ((down_ref, 0), (up_ref, 5)):
+    for x in (-2, -1, 8, 9):
+        field_ref[1, fx_column(x), :], field_ref[2, fx_column(x), :] = ratios(
+            lambda k, x=x: halo_word(k, x), halo_region(x), moduli_ref
+        )
+    for ref, first, step in ((down_ref, 0, 1), (up_ref, 7, -1)):
         for i in range(3):
-            for d in range(3):
-                y = first + d
-                j = i * 3 + d
-                for x in (-5, 3, 5):
-                    ref[pl.ds((x + 5) * 9 + j, 8, stride=9), :] = u_at(ux_ref, i, 0, x, y)
-                for x in (-2, 2):
-                    ref[pl.ds(FIELDS + (x + 2) * 9 + j, 8, stride=9), :] = field_at(
-                        field_ref, i, x, y
-                    )
+            for depth in range(3):
+                y = first + step * depth
+                places, field_places = slab_places(depth)
+                for x in places:
+                    ref[slab_u(i, depth, x), :] = u_at(ux_ref, i, 0, x, y)
+                for x in field_places:
+                    ref[slab_field(i, depth, x), :] = field_at(field_ref, i, x, y)
 
 
 def fold(force, column, a, b):
@@ -288,10 +346,14 @@
 
 def inner_force(
     ux_ref,
+    w_ref,
+    r_ref,
+    moduli_hbm,
+    even_ref,
+    odd_ref,
+    field_in_ref,
+    field_ref,
     wx_ref,
-    field_ref,
-    moduli_hbm,
-    middle_ref,
     part_ref,
     sum_ref,
     step_ref,
@@ -301,22 +363,33 @@
 ):
     fetch = pltpu.make_async_copy(moduli_hbm, moduli_ref, moduli_sem)
     fetch.start()
+    tile, halo_word, halo_region = halo_reader(even_ref, odd_ref)
+    for k in range(WORDS):
+        for x in range(8):
+            wx_ref[k, fx_column(x), :] = w_ref[pl.ds(k * 64 + x * 8, 8), :]
+        for x in (-3, -2, -1, 8, 9, 10):
+            wx_ref[k, fx_column(x), :] = halo_word(k, x)
+    for d in range(3):
+        wx_ref[8 + d, fx_column(-4), :] = tile(EXTRA_TILE + d, True).astype(jnp.int32)
+        wx_ref[d, fx_column(11), :] = tile(EXTRA_TILE + d, False).astype(jnp.int32)
     zero = jnp.zeros((8, LANES), F32)
     for x in BLOCKS:
         for y in (-3, -2, -1, 8, 9, 10):
-            for lead in range(7):
+            for lead in range(1, 6):
                 sx_ref[lead, pl.ds((x + 4) * SU + y + 3, 8, stride=SU), :] = zero
+    for x in (-3, 10):
+        field_ref[0, fx_column(x), :] = column_sum(
+            ux_ref, lambda k, x=x: halo_word(k, x), x, lambda far: True
+        )
     fetch.wait()
+    for x in (-3, 10):
+        field_ref[1, fx_column(x), :], field_ref[2, fx_column(x), :] = ratios(
+            lambda k, x=x: halo_word(k, x), halo_region(x), moduli_ref
+        )
     for y in range(8):
-        step_ref[y] = time_step / chosen(word_at(wx_ref, WORDS, 0, y), moduli_ref, 2)
-        for index, x in enumerate(BLOCKS):
-            if y in EDGE_ROWS:
-                shear = field_at(field_ref, 2, x, y)
-            else:
-                place = (index * 2 + y - 3) * 3
-                middle_ref[place] = inner_sum(ux_ref, wx_ref, x, y)
-                middle_ref[place + 1], shear = ratios(wx_ref, moduli_ref, x, y)
-                middle_ref[place + 2] = shear
+        step_ref[y] = time_step / chosen(r_ref[pl.ds(y, 8, stride=8), :], moduli_ref, 2)
+        for x in BLOCKS:
+            shear = field_at(field_ref, 2, x, y)
             for shift in range(-3, 4):
                 sx_ref[
                     shift + 3, pl.ds((x + 4) * SU + y + 3, 8, stride=SU), :
@@ -366,7 +439,6 @@
     ux_ref,
     wx_ref,
     field_ref,
-    middle_ref,
     part_ref,
     sum_ref,
     step_ref,
@@ -380,20 +452,21 @@
     px_ref,
     force_ref,
 ):
-    halo = (below_ref, above_ref)
     zero = jnp.zeros((8, LANES), F32)
-    for h in range(6):
+    halo = [(below_ref, depth, 2 - depth) for depth in range(3)]
+    halo += [(above_ref, depth, 3 + depth) for depth in range(3)]
+    for ref, depth, h in halo:
         for i in range(3):
-            for x in (-5, 3, 5):
-                value = halo[h // 3][pl.ds((x + 5) * 9 + i * 3 + h % 3, 8, stride=9), :]
-                for shift in range(-3, 4):
+            for x in slab_places(depth)[0]:
+                value = ref[slab_u(i, depth, x), :]
+                for shift in range(-2, 3) if depth < 2 else (0,):
                     uh_ref[
-                        i * 7 + shift + 3, pl.ds((x + 6) * SH + h, 8, stride=SH), :
+                        i * 5 + shift + 2, pl.ds((x + 6) * SH + h, 8, stride=SH), :
                     ] = rolled(value, shift)
         for x in (-6, 2, 6):
             hd_ref[pl.ds((x + 6) * SH + h, 8, stride=SH), :] = zero
 
-    for index, x0 in enumerate(BLOCKS):
+    for x0 in BLOCKS:
         rest = {}
         for h in range(6):
             for a in range(-2, 3):
@@ -427,28 +500,23 @@
                     rows = pl.ds((x0 + a + 6) * SH + h, 8, stride=SH)
                     hd_ref[rows, :] = hd_ref[rows, :] - spread
         for y in range(8):
+            total = field_at(field_ref, 0, x0, y)
             if y in EDGE_ROWS:
-                total = field_at(field_ref, 0, x0, y) + rest[y]
-                pressure = total * field_at(field_ref, 1, x0, y)
-            else:
-                place = (index * 2 + y - 3) * 3
-                pressure = middle_ref[place] * middle_ref[place + 1]
+                total = total + rest[y]
+            pressure = total * field_at(field_ref, 1, x0, y)
             for shift in range(-3, 4):
                 px_ref[
                     shift + 3, pl.ds((x0 + 4) * SU + y + 3, 8, stride=SU), :
                 ] = rolled(pressure, shift)
-    for h in range(6):
-        for x in (-2, 2):
-            part, ratio, shear = [
-                halo[h // 3][pl.ds(FIELDS + (x + 2) * 9 + i * 3 + h % 3, 8, stride=9), :]
-                for i in range(3)
-            ]
+    for ref, depth, h in halo:
+        for x in slab_places(depth)[1]:
+            part, ratio, shear = [ref[slab_field(i, depth, x), :] for i in range(3)]
             pressure = (part + hd_ref[pl.ds((x + 6) * SH + h, 8, stride=SH), :]) * ratio
-            for shift in range(-3, 4):
+            for shift in range(-2, 3) if depth < 2 else (0,):
                 px_ref[
                     shift + 3, pl.ds((x + 4) * SU + halo_y(h) + 3, 8, stride=SU), :
                 ] = rolled(pressure, shift)
-                sh_ref[shift + 3, pl.ds((x + 2) * SH + h, 8, stride=SH), :] = rolled(
+                sh_ref[shift + 2, pl.ds((x + 2) * SH + h, 8, stride=SH), :] = rolled(
                     shear, shift
                 )
 
@@ -493,7 +561,7 @@
             along = combined(
                 [far[i] - own[i] if offset[i] != 0 else None for i in range(3)], offset
             )
-            far_shear = sh_ref[c + 3, pl.ds((a + 2) * SH + h, 8, stride=SH), :]
+            far_shear = sh_ref[c + 2, pl.ds((a + 2) * SH + h, 8, stride=SH), :]
             value = (far_shear * along + shear * reach) * (1.0 / (cls * math.sqrt(cls)))
             column[c] = jnp.where(bit(word, number), value, 0.0)
             if position + 1 == len(bonds) or bonds[position + 1][1][:2] != (a, b):
@@ -507,7 +575,7 @@
             new_u_ref[rows, :] = u_ref[rows, :] + time_step * velocity
 
 
-def call(body, outs, args, unplaced=(), scratch=(), flops=1000):
+def call(body, outs, args, unplaced=(), scratch=(), flops=1000, aliases=None):
     vmem = pl.BlockSpec(memory_space=pltpu.VMEM)
     unmoved = pl.BlockSpec(memory_space=pltpu.HBM)
     return pl.pallas_call(
@@ -516,6 +584,7 @@
         in_specs=[unmoved if position in unplaced else vmem for position in range(len(args))],
         out_specs=[vmem for _ in outs],
         scratch_shapes=scratch,
+        input_output_aliases=aliases or {},
         cost_estimate=pl.CostEstimate(flops=flops, bytes_accessed=100000, transcendentals=0),
         compiler_params=pltpu.CompilerParams(vmem_limit_bytes=16 * 1024 * 1024),
     )(
@@ -546,44 +615,48 @@
         scratch=[copy, copy, copy],
     )
     size = lax.axis_size("gx")
-    odd = lax.ppermute(
-        odd, "gx", [(i, ((i - 1) ^ 1) + 1) for i in range(1, size - 1)]
-    )
+    odd = lax.ppermute(odd, "gx", [(i, ((i - 1) ^ 1) + 1) for i in range(1, size - 1)])
     even = lax.ppermute(even, "gx", [(i, i ^ 1) for i in range(size)])
     even = even.reshape(SLAB * 8, LANES)
     odd = odd.reshape(SLAB * 8, LANES)
     u = u.reshape(192, LANES)
-    ux, wx, fields, down, up = call(
+    words = words.reshape(704, LANES)
+    region = region.reshape(64, LANES)
+    scalars = [pltpu.SMEM(moduli.shape, F32), copy]
+    displaced = ((21, UX_ROWS, LANES), F32)
+    per_node = ((3, FX_ROWS, LANES), F32)
+    ux, own = call(
+        own_part,
+        [displaced, ((24, 8, LANES), F32)],
+        (u, words, region, moduli),
+        unplaced=(3,),
+        scratch=scalars,
+        flops=10_000_000,
+    )
+    ux, fields, down, up = call(
         slabs_y,
-        [
-            ((21, 24 * SU, LANES), F32),
-            ((12, 24 * SW, LANES), jnp.int32),
-            ((3, 16 * SF, LANES), F32),
-            ((FIELDS + 108, LANES), F32),
-            ((FIELDS + 108, LANES), F32),
-        ],
-        (u, words.reshape(704, LANES), region.reshape(64, LANES), moduli, even, odd),
+        [displaced, per_node, ((SLAB_Y, LANES), F32), ((SLAB_Y, LANES), F32)],
+        (u, words, own, moduli, even, odd, ux),
         unplaced=(3,),
-        scratch=[pltpu.SMEM(moduli.shape, F32), copy],
-        flops=20_000_000,
+        scratch=scalars,
+        flops=10_000_000,
+        aliases={6: 0},
     )
     below, above = along_y(down, up)
-    middle, part, balance, step = call(
+    fields, wx, part, balance, step = call(
         inner_force,
         [
-            ((12, 8, LANES), F32),
+            per_node,
+            ((WORDS, WX_ROWS, LANES), jnp.int32),
             ((24, 8, LANES), F32),
             ((24, 8, LANES), F32),
             ((8, 8, LANES), F32),
         ],
-        (ux, wx, fields, moduli),
+        (ux, words, region, moduli, even, odd, fields),
         unplaced=(3,),
-        scratch=[
-            pltpu.VMEM((7, 16 * SU, LANES), F32),
-            pltpu.SMEM(moduli.shape, F32),
-            copy,
-        ],
+        scratch=[pltpu.VMEM((7, 16 * SU, LANES), F32)] + scalars,
         flops=40_000_000,
+        aliases={6: 0},
     )
     new_u, new_v = call(
         outer_force,
@@ -594,7 +667,6 @@
             ux,
             wx,
             fields,
-            middle,
             part,
             balance,
             step,
@@ -602,9 +674,9 @@
             velocity.reshape(192, LANES),
         ),
         scratch=[
-            pltpu.VMEM((21, 20 * SH, LANES), F32),
+            pltpu.VMEM((15, 20 * SH, LANES), F32),
             pltpu.VMEM((20 * SH, LANES), F32),
-            pltpu.VMEM((7, 12 * SH, LANES), F32),
+            pltpu.VMEM((5, 12 * SH, LANES), F32),
             pltpu.VMEM((7, 16 * SU, LANES), F32),
             pltpu.VMEM((24, 8, LANES), F32),
         ],

time: 40.6 us -> 37.3 us (0.919)
  the two profiles are of different devices: /device:TPU:28 before, /device:TPU:56 now
where the time goes in v4:
time: 37.3 us; the launch traced here: 37 us
  starting transfers between devices  20.5 us (55%)
  Pallas kernels  10.2 us (27%)
  waiting for transfers between devices  5.6 us (15%)
  between operations  0.71 us (2%)
    ppermute x1, starting transfers between devices, on_device(): lax.ppermute(odd, 'gx', [(i, (i - 1 ^ 1) + 1) for i in range(1, size - 1)])  11.8 us
    pallas_call x5, Pallas kernels, call(): pl.pallas_call(body, out_shape=[jax.ShapeDtypeStruct(shape, dtype) for sh...  10.2 us
    ppermute x1, starting transfers between devices, along_y(): below = lax.ppermute(up, 'gy', upward)  3.9 us
    ppermute x1, waiting for transfers between devices, along_y(): above = lax.ppermute(down, 'gy', downward)  3.43 us
    ppermute x1, starting transfers between devices, along_y(): above = lax.ppermute(down, 'gy', downward)  2.84 us
    ppermute x1, waiting for transfers between devices, on_device(): lax.ppermute(odd, 'gx', [(i, (i - 1 ^ 1) + 1) for i in range(1, size - 1)])  2.17 us
    ppermute x1, starting transfers between devices, on_device(): even = lax.ppermute(even, 'gx', [(i, i ^ 1) for i in range(size)])  1.92 us
  transfers between devices with their start and end apart: 4, of which 2 were waited for; matrix products, arithmetic and copies ran while one was open for 0% of the time, Pallas kernels for 14%

profile of v4, /device:TPU:56, one launch (start us, length us, event | category | flops | bytes accessed | tf_op | source)
XLA Modules:
  0.0 37.0 jit_solution(13699503825285813657)
XLA Ops:
  0.6 1.1 %shard_map.68 = (f32[57,8,128]{2,1,0:T(8,128)S(1)}, f32[57,8,128]{2,1,0:T(8,128)S(1)}, f32[3,8,8,128]{3,2,1,0:T(8,128)S(1)}, s32[11,8,8,128]{3,2,1,0:T(8,128)S(1)}, s32[8,8,128]{2,1,0:T(8,128)S(1)}) custom-call(f32[3,8,8,128]{3,2,1,0:T(8,128)} %u_hbm.1, s32[11,8,8,128]{3,2,1,0:T(8,128)} %w_hbm.1, s32[8,8,128]{2,1,0:T(8,128)} %r_hbm.1), custom_call_target="tpu_custom_call" | custom-call | flops 1000 | bytes 100000 | tf_op jit(solution)/shard_map/pallas_call | solution.py:581
  1.7 1.9 %collective-permute-start = (f32[57,8,128]{2,1,0:T(8,128)S(1)}, f32[57,8,128]{2,1,0:T(8,128)S(1)}, u32[]{:S(2)}, u32[]{:S(2)}) collective-permute-start(f32[57,8,128]{2,1,0:T(8,128)S(1)} %get-tuple-element.24), channel_id=1, source_target_pairs={{0,16},{16,0},{32,48},{48,32},{64,80},{80,64},{96,112},{112,96},{1... | collective-permute-start | bytes 700424 | tf_op jit(solution)/shard_map/ppermute | solution.py:619
  3.6 11.8 %collective-permute-start.1 = (f32[57,8,128]{2,1,0:T(8,128)S(1)}, f32[57,8,128]{2,1,0:T(8,128)S(1)}, u32[]{:S(2)}, u32[]{:S(2)}) collective-permute-start(f32[57,8,128]{2,1,0:T(8,128)S(1)} %get-tuple-element.25), channel_id=1, source_target_pairs={{16,32},{32,16},{48,64},{64,48},{80,96},{96,80},{112,128},{128,112... | collective-permute-start | bytes 700424 | tf_op jit(solution)/shard_map/ppermute | solution.py:618
  15.5 1.6 %shard_map.69 = (f32[21,560,128]{2,1,0:T(8,128)S(1)}, f32[24,8,128]{2,1,0:T(8,128)S(1)}) custom-call(f32[192,128]{1,0:T(8,128)S(1)} %bitcast.15, s32[704,128]{1,0:T(8,128)S(1)} %bitcast.8, s32[64,128]{1,0:T(8,128)S(1)} %bitcast.18, f32[3,4]{1,0:T(4,128)} %moduli_hbm.5), custom_call_target="tpu_custom_call" | custom-call | flops 10000000 | bytes 100000 | tf_op jit(solution)/shard_map/pallas_call | solution.py:581
  17.0 0.0 collective-permute-done
  17.0 2.2 %collective-permute-done.1 = f32[57,8,128]{2,1,0:T(8,128)S(1)} collective-permute-done((f32[57,8,128]{2,1,0:T(8,128)S(1)}, f32[57,8,128]{2,1,0:T(8,128)S(1)}, u32[]{:S(2)}, u32[]{:S(2)}) %collective-permute-start.1) | collective-permute-done | bytes 233504 | tf_op jit(solution)/shard_map/ppermute | solution.py:618
  19.2 0.0 copy-start
  19.2 1.2 %shard_map.70 = (f32[21,560,128]{2,1,0:T(8,128)S(1)}, f32[3,288,128]{2,1,0:T(8,128)S(1)}, f32[246,128]{1,0:T(8,128)S(1)}, f32[246,128]{1,0:T(8,128)S(1)}) custom-call(f32[192,128]{1,0:T(8,128)S(1)} %bitcast.16, s32[704,128]{1,0:T(8,128)S(1)} %bitcast.9, f32[24,8,128]{2,1,0:T(8,128)S(1)} %get-tuple-element.23.own_ref, ...), custom_call_target="tpu_custom_call", output_to_operand_aliasing={{0}: (6, {})} | custom-call | flops 10000000 | bytes 100000 | tf_op jit(solution)/shard_map/pallas_call | solution.py:581
  20.4 3.9 %collective-permute-start.2 = (f32[246,128]{1,0:T(8,128)S(1)}, f32[246,128]{1,0:T(8,128)S(1)}, u32[]{:S(2)}, u32[]{:S(2)}) collective-permute-start(f32[246,128]{1,0:T(8,128)S(1)} %get-tuple-element.27), channel_id=1, source_target_pairs={{0,1},{1,2},{2,3},{3,4},{4,5},{5,6},{6,7},{7,8},{8,9},{9,10},{10,1... | collective-permute-start | bytes 377864 | tf_op jit(solution)/shard_map/ppermute | solution.py:602
  24.3 2.8 %collective-permute-start.3 = (f32[246,128]{1,0:T(8,128)S(1)}, f32[246,128]{1,0:T(8,128)S(1)}, u32[]{:S(2)}, u32[]{:S(2)}) collective-permute-start(f32[246,128]{1,0:T(8,128)S(1)} %get-tuple-element.28), channel_id=1, source_target_pairs={{1,0},{2,1},{3,2},{4,3},{5,4},{6,5},{7,6},{8,7},{9,8},{10,9},{11,1... | collective-permute-start | bytes 377864 | tf_op jit(solution)/shard_map/ppermute | solution.py:603
  27.2 3.5 %shard_map.71 = (f32[3,288,128]{2,1,0:T(8,128)S(1)}, s32[11,288,128]{2,1,0:T(8,128)S(1)}, f32[24,8,128]{2,1,0:T(8,128)S(1)}, f32[24,8,128]{2,1,0:T(8,128)S(1)}, f32[8,8,128]{2,1,0:T(8,128)S(1)}) custom-call(f32[21,560,128]{2,1,0:T(8,128)S(1)} %get-tuple-element.29.ux_ref, s32[704,128]{1,0:T(8,128)S(1)} %bitcast.10, ...), custom_call_target="tpu_custom_call", output_to_operand_aliasing={{0}: (6, {})} | custom-call | flops 40000000 | bytes 100000 | tf_op jit(solution)/shard_map/pallas_call | solution.py:581
  30.7 0.0 collective-permute-done.2.below_ref
  30.7 3.4 %collective-permute-done.3.above_ref = f32[246,128]{1,0:T(8,128)S(1)} collective-permute-done((f32[246,128]{1,0:T(8,128)S(1)}, f32[246,128]{1,0:T(8,128)S(1)}, u32[]{:S(2)}, u32[]{:S(2)}) %collective-permute-start.3) | collective-permute-done | bytes 125984 | tf_op jit(solution)/shard_map/ppermute | solution.py:603
  34.2 0.0 copy-done
  34.2 2.9 %shard_map.72 = (f32[192,128]{1,0:T(8,128)}, f32[192,128]{1,0:T(8,128)}) custom-call(f32[246,128]{1,0:T(8,128)S(1)} %collective-permute-done.2.below_ref, f32[246,128]{1,0:T(8,128)S(1)} %collective-permute-done.3.above_ref, f32[21,560,128]{2,1,0:T(8,128)S(1)} %get-tuple-element.29.ux_ref, s32[11,288,128]{2,1,0:T(8,128)S(1)} %get-tuple-element.31.wx_ref, ...), custom_call_target="tpu_custom_call" | custom-call | flops 10000000 | bytes 100000 | tf_op jit(solution)/shard_map/pallas_call | solution.py:581
Async XLA Ops:
  1.7 15.3 %collective-permute-start = (f32[57,8,128]{2,1,0:T(8,128)S(1)}, f32[57,8,128]{2,1,0:T(8,128)S(1)}, u32[]{:S(2)}, u32[]{:S(2)}) collective-permute-start(f32[57,8,128]{2,1,0:T(8,128)S(1)} %get-tuple-element.24), channel_id=1, source_target_pairs={{0,16},{16,0},{32,48},{48,32},{64,80},{80,64},{96,112},{112,96},{1... | collective-permute-start | bytes 700424 | tf_op jit(solution)/shard_map/ppermute | solution.py:619
  3.6 15.6 %collective-permute-start.1 = (f32[57,8,128]{2,1,0:T(8,128)S(1)}, f32[57,8,128]{2,1,0:T(8,128)S(1)}, u32[]{:S(2)}, u32[]{:S(2)}) collective-permute-start(f32[57,8,128]{2,1,0:T(8,128)S(1)} %get-tuple-element.25), channel_id=1, source_target_pairs={{16,32},{32,16},{48,64},{64,48},{80,96},{96,80},{112,128},{128,112... | collective-permute-start | bytes 700424 | tf_op jit(solution)/shard_map/ppermute | solution.py:618
  19.2 15.0 %copy-start = (f32[3,8,8,128]{3,2,1,0:T(8,128)S(1)}, f32[3,8,8,128]{3,2,1,0:T(8,128)}, u32[]{:S(2)}) copy-start(f32[3,8,8,128]{3,2,1,0:T(8,128)} %param.6) | copy-start | bytes 294916
  20.4 10.3 %collective-permute-start.2 = (f32[246,128]{1,0:T(8,128)S(1)}, f32[246,128]{1,0:T(8,128)S(1)}, u32[]{:S(2)}, u32[]{:S(2)}) collective-permute-start(f32[246,128]{1,0:T(8,128)S(1)} %get-tuple-element.27), channel_id=1, source_target_pairs={{0,1},{1,2},{2,3},{3,4},{4,5},{5,6},{6,7},{7,8},{8,9},{9,10},{10,1... | collective-permute-start | bytes 377864 | tf_op jit(solution)/shard_map/ppermute | solution.py:602
  24.3 9.8 %collective-permute-start.3 = (f32[246,128]{1,0:T(8,128)S(1)}, f32[246,128]{1,0:T(8,128)S(1)}, u32[]{:S(2)}, u32[]{:S(2)}) collective-permute-start(f32[246,128]{1,0:T(8,128)S(1)} %get-tuple-element.28), channel_id=1, source_target_pairs={{1,0},{2,1},{3,2},{4,3},{5,4},{6,5},{7,6},{8,7},{9,8},{10,9},{11,1... | collective-permute-start | bytes 377864 | tf_op jit(solution)/shard_map/ppermute | solution.py:603

commit v5 on v4

--- a/solution.py
+++ b/solution.py
@@ -41,7 +41,6 @@
 R_TILE = 54
 SLAB = 57
 SLAB_Y = 246
-EDGE_ROWS = (0, 1, 2, 5, 6, 7)
 
 
 def rolled(value, shift):
@@ -344,6 +343,10 @@
     return force
 
 
+def halo_y(h):
+    return h - 3 if h < 3 else h + 5
+
+
 def inner_force(
     ux_ref,
     w_ref,
@@ -357,6 +360,8 @@
     part_ref,
     sum_ref,
     step_ref,
+    hd_ref,
+    weight_ref,
     sx_ref,
     moduli_ref,
     moduli_sem,
@@ -395,6 +400,35 @@
                     shift + 3, pl.ds((x + 4) * SU + y + 3, 8, stride=SU), :
                 ] = rolled(shear, shift)
 
+    for h in range(6):
+        for x in (-6, 2, 6):
+            hd_ref[pl.ds((x + 6) * SH + h, 8, stride=SH), :] = zero
+    for x0 in BLOCKS:
+        for h in range(6):
+            for a in range(-2, 3):
+                spread = None
+                for c in range(-2, 3):
+                    gathered = None
+                    for y in range(8):
+                        offset = (a, halo_y(h) - y, c)
+                        if offset not in NUMBERS:
+                            continue
+                        number = NUMBERS[offset]
+                        factor = 1.0 / math.sqrt(square(offset))
+                        held = bit(word_at(wx_ref, number // bits_per_word, x0, y), number)
+                        own = [
+                            u_at(ux_ref, i, 0, x0, y) if offset[i] != 0 else None
+                            for i in range(3)
+                        ]
+                        term = jnp.where(held, combined(own, offset) * factor, 0.0)
+                        gathered = term if gathered is None else gathered + term
+                    if gathered is not None:
+                        value = rolled(gathered, -c)
+                        spread = value if spread is None else spread + value
+                if spread is not None:
+                    rows = pl.ds((x0 + a + 6) * SH + h, 8, stride=SH)
+                    hd_ref[rows, :] = hd_ref[rows, :] - spread
+
     def row(y, carry):
         own = [u_at(ux_ref, c, 0, 0, y) for c in range(3)]
         shear = px_at(sx_ref, 0, 0, y)
@@ -416,6 +450,7 @@
             held = bit(word, number)
             column[c] = jnp.where(held, value * (1.0 / (cls * math.sqrt(cls))), 0.0)
             count[c] = jnp.where(held, F32(1.0 / math.sqrt(cls)), F32(0.0))
+            weight_ref[number * 8 + y] = count[c]
             if number + 1 == len(OFFSETS) or OFFSETS[number + 1][:2] != (a, b):
                 force = fold(force, column, a, b)
                 balance = fold(balance, count, a, b)
@@ -429,88 +464,26 @@
     lax.fori_loop(0, 8, row, 0)
 
 
-def halo_y(h):
-    return h - 3 if h < 3 else h + 5
-
-
-def outer_force(
-    below_ref,
-    above_ref,
-    ux_ref,
-    wx_ref,
-    field_ref,
-    part_ref,
-    sum_ref,
-    step_ref,
-    u_ref,
-    v_ref,
-    new_u_ref,
-    new_v_ref,
-    uh_ref,
-    hd_ref,
-    sh_ref,
-    px_ref,
-    force_ref,
+def side_of(low):
+    return ((0, 1, 2), -3, 4) if low else ((5, 6, 7), 5, 10)
+
+
+def add_side(
+    low, slab_ref, ux_ref, wx_ref, field_ref, hd_ref, weight_ref, sum_ref, uh_ref, sh_ref, px_ref
 ):
-    zero = jnp.zeros((8, LANES), F32)
-    halo = [(below_ref, depth, 2 - depth) for depth in range(3)]
-    halo += [(above_ref, depth, 3 + depth) for depth in range(3)]
-    for ref, depth, h in halo:
+    edge, first, last = side_of(low)
+    halo = [(depth, 2 - depth if low else 3 + depth) for depth in range(3)]
+    for depth, h in halo:
         for i in range(3):
             for x in slab_places(depth)[0]:
-                value = ref[slab_u(i, depth, x), :]
+                value = slab_ref[slab_u(i, depth, x), :]
                 for shift in range(-2, 3) if depth < 2 else (0,):
                     uh_ref[
                         i * 5 + shift + 2, pl.ds((x + 6) * SH + h, 8, stride=SH), :
                     ] = rolled(value, shift)
-        for x in (-6, 2, 6):
-            hd_ref[pl.ds((x + 6) * SH + h, 8, stride=SH), :] = zero
-
-    for x0 in BLOCKS:
-        rest = {}
-        for h in range(6):
-            for a in range(-2, 3):
-                spread = None
-                for c in range(-2, 3):
-                    gathered = None
-                    for y in range(8):
-                        offset = (a, halo_y(h) - y, c)
-                        if offset not in NUMBERS:
-                            continue
-                        number = NUMBERS[offset]
-                        factor = 1.0 / math.sqrt(square(offset))
-                        held = bit(word_at(wx_ref, number // bits_per_word, x0, y), number)
-                        far = [
-                            uh_at(uh_ref, i, c, x0 + a, h) if offset[i] != 0 else None
-                            for i in range(3)
-                        ]
-                        own = [
-                            u_at(ux_ref, i, 0, x0, y) if offset[i] != 0 else None
-                            for i in range(3)
-                        ]
-                        add_to(
-                            rest, y, jnp.where(held, combined(far, offset) * factor, 0.0)
-                        )
-                        term = jnp.where(held, combined(own, offset) * factor, 0.0)
-                        gathered = term if gathered is None else gathered + term
-                    if gathered is not None:
-                        value = rolled(gathered, -c)
-                        spread = value if spread is None else spread + value
-                if spread is not None:
-                    rows = pl.ds((x0 + a + 6) * SH + h, 8, stride=SH)
-                    hd_ref[rows, :] = hd_ref[rows, :] - spread
-        for y in range(8):
-            total = field_at(field_ref, 0, x0, y)
-            if y in EDGE_ROWS:
-                total = total + rest[y]
-            pressure = total * field_at(field_ref, 1, x0, y)
-            for shift in range(-3, 4):
-                px_ref[
-                    shift + 3, pl.ds((x0 + 4) * SU + y + 3, 8, stride=SU), :
-                ] = rolled(pressure, shift)
-    for ref, depth, h in halo:
+    for depth, h in halo:
         for x in slab_places(depth)[1]:
-            part, ratio, shear = [ref[slab_field(i, depth, x), :] for i in range(3)]
+            part, ratio, shear = [slab_ref[slab_field(i, depth, x), :] for i in range(3)]
             pressure = (part + hd_ref[pl.ds((x + 6) * SH + h, 8, stride=SH), :]) * ratio
             for shift in range(-2, 3) if depth < 2 else (0,):
                 px_ref[
@@ -519,58 +492,114 @@
                 sh_ref[shift + 2, pl.ds((x + 2) * SH + h, 8, stride=SH), :] = rolled(
                     shear, shift
                 )
-
-    def row(y, carry):
-        pressure = px_at(px_ref, 0, 0, y)
-        force = [part_ref[i * 8 + y] + pressure * sum_ref[i * 8 + y] for i in range(3)]
-        word = None
+    for y in range(max(first, 0), min(last, 7) + 1):
+        for x0 in BLOCKS:
+            total = field_at(field_ref, 0, x0, y)
+            if y in edge:
+                sums = {}
+                for number, offset, h in crossing(y):
+                    far = [
+                        uh_at(uh_ref, i, offset[2], x0 + offset[0], h)
+                        if offset[i] != 0
+                        else None
+                        for i in range(3)
+                    ]
+                    held = bit(word_at(wx_ref, number // bits_per_word, x0, y), number)
+                    add_to(sums, square(offset), jnp.where(held, combined(far, offset), 0.0))
+                total = total + by_class(sums)
+            pressure = total * field_at(field_ref, 1, x0, y)
+            for shift in range(-3, 4):
+                px_ref[
+                    shift + 3, pl.ds((x0 + 4) * SU + y + 3, 8, stride=SU), :
+                ] = rolled(pressure, shift)
+
+    def row(y, force):
+        force = list(force)
+        if y in edge:
+            own = [u_at(ux_ref, c, 0, 0, y) for c in range(3)]
+            shear = field_at(field_ref, 2, 0, y)
+            column = {}
+            bonds = crossing(y)
+            for position, (number, (a, b, c), h) in enumerate(bonds):
+                offset = (a, b, c)
+                far = [
+                    uh_at(uh_ref, i, c, a, h) if offset[i] != 0 else None for i in range(3)
+                ]
+                reach = combined(far, offset)
+                near = combined(
+                    [own[i] if offset[i] != 0 else None for i in range(3)], offset
+                )
+                far_shear = sh_ref[c + 2, pl.ds((a + 2) * SH + h, 8, stride=SH), :]
+                value = far_shear * (reach - near) + shear * reach
+                column[c] = (value * (1.0 / square(offset))) * weight_ref[number * 8 + y]
+                if position + 1 == len(bonds) or bonds[position + 1][1][:2] != (a, b):
+                    force = fold(force, column, a, b)
+                    column = {}
+        if first <= y <= last:
+            pressure = px_at(px_ref, 0, 0, y)
+            force = [force[i] + pressure * sum_ref[i * 8 + y] for i in range(3)]
         column = {}
-        for number, offset in enumerate(OFFSETS):
-            if number % bits_per_word == 0:
-                word = word_at(wx_ref, number // bits_per_word, 0, y)
-            a, b, c = offset
-            column[c] = jnp.where(
-                bit(word, number),
-                px_at(px_ref, c, a, y + b) * (1.0 / math.sqrt(square(offset))),
-                0.0,
-            )
+        for number, (a, b, c) in enumerate(OFFSETS):
+            if not first <= y + b <= last:
+                continue
+            column[c] = px_at(px_ref, c, a, y + b) * weight_ref[number * 8 + y]
             if number + 1 == len(OFFSETS) or OFFSETS[number + 1][:2] != (a, b):
                 force = fold(force, column, a, b)
                 column = {}
+        return force
+
+    return row
+
+
+def lower_force(
+    slab_ref,
+    ux_ref,
+    wx_ref,
+    field_ref,
+    hd_ref,
+    weight_ref,
+    sum_ref,
+    part_ref,
+    force_ref,
+    uh_ref,
+    sh_ref,
+    px_ref,
+):
+    row = add_side(
+        True, slab_ref, ux_ref, wx_ref, field_ref, hd_ref, weight_ref, sum_ref, uh_ref, sh_ref, px_ref
+    )
+    for y in range(8):
+        force = row(y, [part_ref[i * 8 + y] for i in range(3)])
         for i in range(3):
             force_ref[i * 8 + y] = force[i]
-        return carry
-
-    lax.fori_loop(0, 8, row, 0)
-
+
+
+def outer_force(
+    slab_ref,
+    ux_ref,
+    wx_ref,
+    field_ref,
+    hd_ref,
+    weight_ref,
+    sum_ref,
+    force_ref,
+    step_ref,
+    u_ref,
+    v_ref,
+    new_u_ref,
+    new_v_ref,
+    uh_ref,
+    sh_ref,
+    px_ref,
+):
+    row = add_side(
+        False, slab_ref, ux_ref, wx_ref, field_ref, hd_ref, weight_ref, sum_ref, uh_ref, sh_ref, px_ref
+    )
     for y in range(8):
-        force = [force_ref[i * 8 + y] for i in range(3)]
-        own = [u_at(ux_ref, c, 0, 0, y) for c in range(3)]
-        if y in EDGE_ROWS:
-            shear = field_at(field_ref, 2, 0, y)
-        column = {}
-        bonds = crossing(y)
-        for position, (number, offset, h) in enumerate(bonds):
-            word = word_at(wx_ref, number // bits_per_word, 0, y)
-            a, b, c = offset
-            cls = square(offset)
-            far = [
-                uh_at(uh_ref, i, c, a, h) if offset[i] != 0 else None for i in range(3)
-            ]
-            reach = combined(far, offset)
-            along = combined(
-                [far[i] - own[i] if offset[i] != 0 else None for i in range(3)], offset
-            )
-            far_shear = sh_ref[c + 2, pl.ds((a + 2) * SH + h, 8, stride=SH), :]
-            value = (far_shear * along + shear * reach) * (1.0 / (cls * math.sqrt(cls)))
-            column[c] = jnp.where(bit(word, number), value, 0.0)
-            if position + 1 == len(bonds) or bonds[position + 1][1][:2] != (a, b):
-                force = fold(force, column, a, b)
-                column = {}
-        step = step_ref[y]
+        force = row(y, [force_ref[i * 8 + y] for i in range(3)])
         for i in range(3):
             rows = pl.ds(i * 64 + y, 8, stride=8)
-            velocity = v_ref[rows, :] + force[i] * step
+            velocity = v_ref[rows, :] + force[i] * step_ref[y]
             new_v_ref[rows, :] = velocity
             new_u_ref[rows, :] = u_ref[rows, :] + time_step * velocity
 
@@ -615,7 +644,9 @@
         scratch=[copy, copy, copy],
     )
     size = lax.axis_size("gx")
-    odd = lax.ppermute(odd, "gx", [(i, ((i - 1) ^ 1) + 1) for i in range(1, size - 1)])
+    odd = lax.ppermute(
+        odd, "gx", [(i, ((i - 1) ^ 1) + 1) for i in range(1, size - 1)]
+    )
     even = lax.ppermute(even, "gx", [(i, i ^ 1) for i in range(size)])
     even = even.reshape(SLAB * 8, LANES)
     odd = odd.reshape(SLAB * 8, LANES)
@@ -643,7 +674,7 @@
         aliases={6: 0},
     )
     below, above = along_y(down, up)
-    fields, wx, part, balance, step = call(
+    fields, wx, part, balance, step, halo, weights = call(
         inner_force,
         [
             per_node,
@@ -651,6 +682,8 @@
             ((24, 8, LANES), F32),
             ((24, 8, LANES), F32),
             ((8, 8, LANES), F32),
+            ((20 * SH, LANES), F32),
+            ((len(OFFSETS) * 8, 8, LANES), F32),
         ],
         (ux, words, region, moduli, even, odd, fields),
         unplaced=(3,),
@@ -658,28 +691,24 @@
         flops=40_000_000,
         aliases={6: 0},
     )
+    shared = (ux, wx, fields, halo, weights, balance)
+    working = [
+        pltpu.VMEM((15, 20 * SH, LANES), F32),
+        pltpu.VMEM((5, 12 * SH, LANES), F32),
+        pltpu.VMEM((7, 16 * SU, LANES), F32),
+    ]
+    (force,) = call(
+        lower_force,
+        [((24, 8, LANES), F32)],
+        (below,) + shared + (part,),
+        scratch=working,
+        flops=10_000_000,
+    )
     new_u, new_v = call(
         outer_force,
         [((192, LANES), F32)] * 2,
-        (
-            below,
-            above,
-            ux,
-            wx,
-            fields,
-            part,
-            balance,
-            step,
-            u,
-            velocity.reshape(192, LANES),
-        ),
-        scratch=[
-            pltpu.VMEM((15, 20 * SH, LANES), F32),
-            pltpu.VMEM((20 * SH, LANES), F32),
-            pltpu.VMEM((5, 12 * SH, LANES), F32),
-            pltpu.VMEM((7, 16 * SU, LANES), F32),
-            pltpu.VMEM((24, 8, LANES), F32),
-        ],
+        (above,) + shared + (force, step, u, velocity.reshape(192, LANES)),
+        scratch=working,
         flops=10_000_000,
     )
     return new_u.reshape(displacement.shape), new_v.reshape(velocity.shape)

time: 37.3 us -> 36 us (0.965)
  waiting for transfers between devices: 5.6 us -> 4.76 us
  Pallas kernels: 10.2 us -> 9.75 us
    ppermute x1, waiting for transfers between devices: 3.43 us -> 2.66 us  [along_y(): above = lax.ppermute(down, 'gy', downward)]
    pallas_call x5 -> x6, Pallas kernels: 10.2 us -> 9.75 us  [call(): pl.pallas_call(body, out_shape=[jax.ShapeDtypeStruct(shape, dtype) for sh...]
  transfers between devices with their start and end apart: 4 -> 4, of which waited for: 2 -> 2; matrix products, arithmetic and copies ran while one was open for 0% -> 0% of each run, Pallas kernels for 14% -> 17%
where the time goes in v5:
time: 36 us; the launch traced here: 35.7 us
  starting transfers between devices  20.5 us (57%)
  Pallas kernels  9.75 us (27%)
  waiting for transfers between devices  4.76 us (13%)
  between operations  0.72 us (2%)
    ppermute x1, starting transfers between devices, on_device(): lax.ppermute(odd, 'gx', [(i, (i - 1 ^ 1) + 1) for i in range(1, size - 1)])  11.8 us
    pallas_call x6, Pallas kernels, call(): pl.pallas_call(body, out_shape=[jax.ShapeDtypeStruct(shape, dtype) for sh...  9.75 us
    ppermute x1, starting transfers between devices, along_y(): below = lax.ppermute(up, 'gy', upward)  3.9 us
    ppermute x1, starting transfers between devices, along_y(): above = lax.ppermute(down, 'gy', downward)  2.84 us
    ppermute x1, waiting for transfers between devices, along_y(): above = lax.ppermute(down, 'gy', downward)  2.66 us
    ppermute x1, waiting for transfers between devices, on_device(): lax.ppermute(odd, 'gx', [(i, (i - 1 ^ 1) + 1) for i in range(1, size - 1)])  2.1 us
    ppermute x1, starting transfers between devices, on_device(): even = lax.ppermute(even, 'gx', [(i, i ^ 1) for i in range(size)])  1.92 us
  transfers between devices with their start and end apart: 4, of which 2 were waited for; matrix products, arithmetic and copies ran while one was open for 0% of the time, Pallas kernels for 17%

profile of v5, /device:TPU:56, one launch (start us, length us, event | category | flops | bytes accessed | tf_op | source)
XLA Modules:
  0.0 35.7 jit_solution(17985992956647931624)
XLA Ops:
  0.6 1.1 %shard_map.68 = (f32[57,8,128]{2,1,0:T(8,128)S(1)}, f32[57,8,128]{2,1,0:T(8,128)S(1)}, f32[3,8,8,128]{3,2,1,0:T(8,128)S(1)}, s32[11,8,8,128]{3,2,1,0:T(8,128)S(1)}, s32[8,8,128]{2,1,0:T(8,128)S(1)}) custom-call(f32[3,8,8,128]{3,2,1,0:T(8,128)} %u_hbm.1, s32[11,8,8,128]{3,2,1,0:T(8,128)} %w_hbm.1, s32[8,8,128]{2,1,0:T(8,128)} %r_hbm.1), custom_call_target="tpu_custom_call" | custom-call | flops 1000 | bytes 100000 | tf_op jit(solution)/shard_map/pallas_call | solution.py:610
  1.7 1.9 %collective-permute-start = (f32[57,8,128]{2,1,0:T(8,128)S(1)}, f32[57,8,128]{2,1,0:T(8,128)S(1)}, u32[]{:S(2)}, u32[]{:S(2)}) collective-permute-start(f32[57,8,128]{2,1,0:T(8,128)S(1)} %get-tuple-element.26), channel_id=1, source_target_pairs={{0,16},{16,0},{32,48},{48,32},{64,80},{80,64},{96,112},{112,96},{1... | collective-permute-start | bytes 700424 | tf_op jit(solution)/shard_map/ppermute | solution.py:650
  3.6 11.8 %collective-permute-start.1 = (f32[57,8,128]{2,1,0:T(8,128)S(1)}, f32[57,8,128]{2,1,0:T(8,128)S(1)}, u32[]{:S(2)}, u32[]{:S(2)}) collective-permute-start(f32[57,8,128]{2,1,0:T(8,128)S(1)} %get-tuple-element.27), channel_id=1, source_target_pairs={{16,32},{32,16},{48,64},{64,48},{80,96},{96,80},{112,128},{128,112... | collective-permute-start | bytes 700424 | tf_op jit(solution)/shard_map/ppermute | solution.py:647
  15.5 1.6 %shard_map.69 = (f32[21,560,128]{2,1,0:T(8,128)S(1)}, f32[24,8,128]{2,1,0:T(8,128)S(1)}) custom-call(f32[192,128]{1,0:T(8,128)S(1)} %bitcast.15, s32[704,128]{1,0:T(8,128)S(1)} %bitcast.8, s32[64,128]{1,0:T(8,128)S(1)} %bitcast.18, f32[3,4]{1,0:T(4,128)} %moduli_hbm.5), custom_call_target="tpu_custom_call" | custom-call | flops 10000000 | bytes 100000 | tf_op jit(solution)/shard_map/pallas_call | solution.py:610
  17.1 0.0 collective-permute-done
  17.1 2.1 %collective-permute-done.1 = f32[57,8,128]{2,1,0:T(8,128)S(1)} collective-permute-done((f32[57,8,128]{2,1,0:T(8,128)S(1)}, f32[57,8,128]{2,1,0:T(8,128)S(1)}, u32[]{:S(2)}, u32[]{:S(2)}) %collective-permute-start.1) | collective-permute-done | bytes 233504 | tf_op jit(solution)/shard_map/ppermute | solution.py:647
  19.2 1.3 %shard_map.70 = (f32[21,560,128]{2,1,0:T(8,128)S(1)}, f32[3,288,128]{2,1,0:T(8,128)S(1)}, f32[246,128]{1,0:T(8,128)S(1)}, f32[246,128]{1,0:T(8,128)S(1)}) custom-call(f32[192,128]{1,0:T(8,128)S(1)} %bitcast.16, s32[704,128]{1,0:T(8,128)S(1)} %bitcast.9, f32[24,8,128]{2,1,0:T(8,128)S(1)} %get-tuple-element.25.own_ref, ...), custom_call_target="tpu_custom_call", output_to_operand_aliasing={{0}: (6, {})} | custom-call | flops 10000000 | bytes 100000 | tf_op jit(solution)/shard_map/pallas_call | solution.py:610
  20.5 3.9 %collective-permute-start.3 = (f32[246,128]{1,0:T(8,128)S(1)}, f32[246,128]{1,0:T(8,128)S(1)}, u32[]{:S(2)}, u32[]{:S(2)}) collective-permute-start(f32[246,128]{1,0:T(8,128)S(1)} %get-tuple-element.37), channel_id=1, source_target_pairs={{0,1},{1,2},{2,3},{3,4},{4,5},{5,6},{6,7},{7,8},{8,9},{9,10},{10,1... | collective-permute-start | bytes 377864 | tf_op jit(solution)/shard_map/ppermute | solution.py:631
  24.4 2.8 %collective-permute-start.2 = (f32[246,128]{1,0:T(8,128)S(1)}, f32[246,128]{1,0:T(8,128)S(1)}, u32[]{:S(2)}, u32[]{:S(2)}) collective-permute-start(f32[246,128]{1,0:T(8,128)S(1)} %get-tuple-element.29), channel_id=1, source_target_pairs={{1,0},{2,1},{3,2},{4,3},{5,4},{6,5},{7,6},{8,7},{9,8},{10,9},{11,1... | collective-permute-start | bytes 377864 | tf_op jit(solution)/shard_map/ppermute | solution.py:632
  27.3 3.4 %shard_map.71 = (f32[3,288,128]{2,1,0:T(8,128)S(1)}, s32[11,288,128]{2,1,0:T(8,128)S(1)}, f32[24,8,128]{2,1,0:T(8,128)S(1)}, f32[24,8,128]{2,1,0:T(8,128)S(1)}, ...) custom-call(f32[21,560,128]{2,1,0:T(8,128)S(1)} %get-tuple-element.3, ...), custom_call_target="tpu_custom_call", output_to_operand_aliasing={{0}: (6, {})} | custom-call | flops 40000000 | bytes 100000 | tf_op jit(solution)/shard_map/pallas_call | solution.py:610
  30.7 0.0 collective-permute-done.3.slab_ref
  30.7 0.0 copy-start
  30.7 0.9 %shard_map.72.force_ref = f32[24,8,128]{2,1,0:T(8,128)S(1)} custom-call(f32[246,128]{1,0:T(8,128)S(1)} %collective-permute-done.3.slab_ref, f32[21,560,128]{2,1,0:T(8,128)S(1)} %get-tuple-element.30.ux_ref, s32[11,288,128]{2,1,0:T(8,128)S(1)} %get-tuple-element.32.wx_ref, f32[3,288,128]{2,1,0:T(8,128)S(1)} %get-tuple-element.33.field_ref, ...), custom_call_target="tpu_custom_call" | custom-call | flops 10000000 | bytes 100000 | tf_op jit(solution)/shard_map/pallas_call | solution.py:610
  31.6 2.7 %collective-permute-done.2.slab_ref = f32[246,128]{1,0:T(8,128)S(1)} collective-permute-done((f32[246,128]{1,0:T(8,128)S(1)}, f32[246,128]{1,0:T(8,128)S(1)}, u32[]{:S(2)}, u32[]{:S(2)}) %collective-permute-start.2) | collective-permute-done | bytes 125984 | tf_op jit(solution)/shard_map/ppermute | solution.py:632
  34.3 0.0 copy-done
  34.3 1.5 %shard_map.73 = (f32[192,128]{1,0:T(8,128)}, f32[192,128]{1,0:T(8,128)}) custom-call(f32[246,128]{1,0:T(8,128)S(1)} %collective-permute-done.2.slab_ref, f32[21,560,128]{2,1,0:T(8,128)S(1)} %get-tuple-element.30.ux_ref, s32[11,288,128]{2,1,0:T(8,128)S(1)} %get-tuple-element.32.wx_ref, f32[3,288,128]{2,1,0:T(8,128)S(1)} %get-tuple-element.33.field_ref, ...), custom_call_target="tpu_custom_call" | custom-call | flops 10000000 | bytes 100000 | tf_op jit(solution)/shard_map/pallas_call | solution.py:610
Async XLA Ops:
  1.7 15.4 %collective-permute-start = (f32[57,8,128]{2,1,0:T(8,128)S(1)}, f32[57,8,128]{2,1,0:T(8,128)S(1)}, u32[]{:S(2)}, u32[]{:S(2)}) collective-permute-start(f32[57,8,128]{2,1,0:T(8,128)S(1)} %get-tuple-element.26), channel_id=1, source_target_pairs={{0,16},{16,0},{32,48},{48,32},{64,80},{80,64},{96,112},{112,96},{1... | collective-permute-start | bytes 700424 | tf_op jit(solution)/shard_map/ppermute | solution.py:650
  3.6 15.6 %collective-permute-start.1 = (f32[57,8,128]{2,1,0:T(8,128)S(1)}, f32[57,8,128]{2,1,0:T(8,128)S(1)}, u32[]{:S(2)}, u32[]{:S(2)}) collective-permute-start(f32[57,8,128]{2,1,0:T(8,128)S(1)} %get-tuple-element.27), channel_id=1, source_target_pairs={{16,32},{32,16},{48,64},{64,48},{80,96},{96,80},{112,128},{128,112... | collective-permute-start | bytes 700424 | tf_op jit(solution)/shard_map/ppermute | solution.py:647
  20.5 10.2 %collective-permute-start.3 = (f32[246,128]{1,0:T(8,128)S(1)}, f32[246,128]{1,0:T(8,128)S(1)}, u32[]{:S(2)}, u32[]{:S(2)}) collective-permute-start(f32[246,128]{1,0:T(8,128)S(1)} %get-tuple-element.37), channel_id=1, source_target_pairs={{0,1},{1,2},{2,3},{3,4},{4,5},{5,6},{6,7},{7,8},{8,9},{9,10},{10,1... | collective-permute-start | bytes 377864 | tf_op jit(solution)/shard_map/ppermute | solution.py:631
  24.4 9.8 %collective-permute-start.2 = (f32[246,128]{1,0:T(8,128)S(1)}, f32[246,128]{1,0:T(8,128)S(1)}, u32[]{:S(2)}, u32[]{:S(2)}) collective-permute-start(f32[246,128]{1,0:T(8,128)S(1)} %get-tuple-element.29), channel_id=1, source_target_pairs={{1,0},{2,1},{3,2},{4,3},{5,4},{6,5},{7,6},{8,7},{9,8},{10,9},{11,1... | collective-permute-start | bytes 377864 | tf_op jit(solution)/shard_map/ppermute | solution.py:632
  30.7 3.6 %copy-start = (f32[3,8,8,128]{3,2,1,0:T(8,128)S(1)}, f32[3,8,8,128]{3,2,1,0:T(8,128)}, u32[]{:S(2)}) copy-start(f32[3,8,8,128]{3,2,1,0:T(8,128)} %param.6) | copy-start | bytes 294916

commit v6 on v5

--- a/solution.py
+++ b/solution.py
@@ -38,9 +38,9 @@
 BLOCKS = (-4, 4)
 EXTRA_TILE = 33
 U_TILE = 36
-R_TILE = 54
-SLAB = 57
-SLAB_Y = 246
+R_TILE = 52
+SLAB = 55
+SLAB_Y = 218
 
 
 def rolled(value, shift):
@@ -78,13 +78,17 @@
 def slab_u(component, depth, x):
     if depth < 2:
         return pl.ds((x + 5) * 6 + component * 2 + depth, 8, stride=6)
-    return pl.ds(108 + (x + 3) * 3 + component, 8, stride=3)
+    return pl.ds(108 + x + 3, 8)
 
 
 def slab_field(field, depth, x):
     if depth < 2:
-        return pl.ds(150 + (x + 2) * 6 + field * 2 + depth, 8, stride=6)
-    return pl.ds(222 + x * 3 + field, 8, stride=3)
+        return pl.ds(122 + (x + 2) * 6 + field * 2 + depth, 8, stride=6)
+    return pl.ds(194 + x * 3 + field, 8, stride=3)
+
+
+def slab_components(depth):
+    return range(3) if depth < 2 else (1,)
 
 
 def slab_places(depth):
@@ -154,6 +158,14 @@
         elif target > 7:
             found.append((number, offset, target - 8 + 3))
     return found
+
+
+def u_depth(component):
+    return 6 if component == 0 else 5
+
+
+def u_tile(component):
+    return U_TILE + (0 if component == 0 else 1 + component * 5)
 
 
 def slabs_x(
@@ -176,8 +188,8 @@
         for d in range(3):
             ref[EXTRA_TILE + d] = w_ref[right * 8 + d, right + 3].astype(F32)
         for c in range(3):
-            for d in range(6):
-                ref[U_TILE + c * 6 + d] = u_ref[c, right * 2 + d]
+            for d in range(u_depth(c)):
+                ref[u_tile(c) + d] = u_ref[c, right * (8 - u_depth(c)) + d]
         for d in range(3):
             ref[R_TILE + d] = r_ref[right * 5 + d].astype(F32)
 
@@ -205,9 +217,15 @@
 
 def ratios(words, region, moduli_ref):
     counts = {}
-    for k in range(WORDS):
-        word = words(k)
+    for k in range((WORDS + 1) // 2):
+        word = words(k) if k < WORDS // 2 else words(WORDS - 1)
         group = OFFSETS[k * bits_per_word : (k + 1) * bits_per_word]
+        if k < WORDS // 2:
+            other = WORDS - 2 - k
+            word = word | (words(other) << bits_per_word)
+            group = group + OFFSETS[other * bits_per_word : (other + 1) * bits_per_word]
+        else:
+            group = OFFSETS[(WORDS - 1) * bits_per_word :]
         for cls in CLASSES:
             held = sum(1 << i for i, offset in enumerate(group) if square(offset) == cls)
             if held:
@@ -223,7 +241,9 @@
 
 
 def spread_column(ux_ref, component, x, value):
-    for shift in range(-3, 4):
+    depth = max(-x, x - 7, 0)
+    reach = 3 if depth < 4 else 2 if depth < 6 else 0
+    for shift in range(-reach, reach + 1):
         ux_ref[component * 7 + shift + 3, ux_column(x), :] = rolled(value, shift)
 
 
@@ -292,9 +312,10 @@
     fetch.start()
     tile, halo_word, halo_region = halo_reader(even_ref, odd_ref)
     for i in range(3):
-        for d in range(6):
-            spread_column(ux_ref, i, d - 6, tile(U_TILE + i * 6 + d, True))
-            spread_column(ux_ref, i, d + 8, tile(U_TILE + i * 6 + d, False))
+        size = u_depth(i)
+        for d in range(size):
+            spread_column(ux_ref, i, d - size, tile(u_tile(i) + d, True))
+            spread_column(ux_ref, i, d + 8, tile(u_tile(i) + d, False))
     for x in range(8):
         value = own_ref[x]
         if x < 3 or x > 4:
@@ -317,12 +338,13 @@
             lambda k, x=x: halo_word(k, x), halo_region(x), moduli_ref
         )
     for ref, first, step in ((down_ref, 0, 1), (up_ref, 7, -1)):
-        for i in range(3):
-            for depth in range(3):
-                y = first + step * depth
-                places, field_places = slab_places(depth)
+        for depth in range(3):
+            y = first + step * depth
+            places, field_places = slab_places(depth)
+            for i in slab_components(depth):
                 for x in places:
                     ref[slab_u(i, depth, x), :] = u_at(ux_ref, i, 0, x, y)
+            for i in range(3):
                 for x in field_places:
                     ref[slab_field(i, depth, x), :] = field_at(field_ref, i, x, y)
 
@@ -474,7 +496,7 @@
     edge, first, last = side_of(low)
     halo = [(depth, 2 - depth if low else 3 + depth) for depth in range(3)]
     for depth, h in halo:
-        for i in range(3):
+        for i in slab_components(depth):
             for x in slab_places(depth)[0]:
                 value = slab_ref[slab_u(i, depth, x), :]
                 for shift in range(-2, 3) if depth < 2 else (0,):

time: 36 us -> 35.7 us (level)
  transfers between devices with their start and end apart: 4 -> 4, of which waited for: 2 -> 2; matrix products, arithmetic and copies ran while one was open for 0% -> 0% of each run, Pallas kernels for 17% -> 16%
where the time goes in v6:
time: 35.7 us; the launch traced here: 35.3 us
  starting transfers between devices  20.5 us (57%)
  Pallas kernels  9.6 us (27%)
  waiting for transfers between devices  4.49 us (13%)
  between operations  0.72 us (2%)
    ppermute x1, starting transfers between devices, on_device(): lax.ppermute(odd, 'gx', [(i, (i - 1 ^ 1) + 1) for i in range(1, size - 1)])  11.8 us
    pallas_call x6, Pallas kernels, call(): pl.pallas_call(body, out_shape=[jax.ShapeDtypeStruct(shape, dtype) for sh...  9.6 us
    ppermute x1, starting transfers between devices, along_y(): below = lax.ppermute(up, 'gy', upward)  3.77 us
    ppermute x1, starting transfers between devices, along_y(): above = lax.ppermute(down, 'gy', downward)  2.97 us
    ppermute x1, waiting for transfers between devices, along_y(): above = lax.ppermute(down, 'gy', downward)  2.41 us
    ppermute x1, waiting for transfers between devices, on_device(): lax.ppermute(odd, 'gx', [(i, (i - 1 ^ 1) + 1) for i in range(1, size - 1)])  2.08 us
    ppermute x1, starting transfers between devices, on_device(): even = lax.ppermute(even, 'gx', [(i, i ^ 1) for i in range(size)])  1.92 us
  transfers between devices with their start and end apart: 4, of which 2 were waited for; matrix products, arithmetic and copies ran while one was open for 0% of the time, Pallas kernels for 16%

profile of v6, /device:TPU:56, one launch (start us, length us, event | category | flops | bytes accessed | tf_op | source)
XLA Modules:
  0.0 35.3 jit_solution(11281153261496145899)
XLA Ops:
  0.6 1.1 %shard_map.68 = (f32[55,8,128]{2,1,0:T(8,128)S(1)}, f32[55,8,128]{2,1,0:T(8,128)S(1)}, f32[3,8,8,128]{3,2,1,0:T(8,128)S(1)}, s32[11,8,8,128]{3,2,1,0:T(8,128)S(1)}, s32[8,8,128]{2,1,0:T(8,128)S(1)}) custom-call(f32[3,8,8,128]{3,2,1,0:T(8,128)} %u_hbm.1, s32[11,8,8,128]{3,2,1,0:T(8,128)} %w_hbm.1, s32[8,8,128]{2,1,0:T(8,128)} %r_hbm.1), custom_call_target="tpu_custom_call" | custom-call | flops 1000 | bytes 100000 | tf_op jit(solution)/shard_map/pallas_call | solution.py:632
  1.7 1.9 %collective-permute-start = (f32[55,8,128]{2,1,0:T(8,128)S(1)}, f32[55,8,128]{2,1,0:T(8,128)S(1)}, u32[]{:S(2)}, u32[]{:S(2)}) collective-permute-start(f32[55,8,128]{2,1,0:T(8,128)S(1)} %get-tuple-element.26), channel_id=1, source_target_pairs={{0,16},{16,0},{32,48},{48,32},{64,80},{80,64},{96,112},{112,96},{1... | collective-permute-start | bytes 675848 | tf_op jit(solution)/shard_map/ppermute | solution.py:672
  3.6 11.8 %collective-permute-start.1 = (f32[55,8,128]{2,1,0:T(8,128)S(1)}, f32[55,8,128]{2,1,0:T(8,128)S(1)}, u32[]{:S(2)}, u32[]{:S(2)}) collective-permute-start(f32[55,8,128]{2,1,0:T(8,128)S(1)} %get-tuple-element.27), channel_id=1, source_target_pairs={{16,32},{32,16},{48,64},{64,48},{80,96},{96,80},{112,128},{128,112... | collective-permute-start | bytes 675848 | tf_op jit(solution)/shard_map/ppermute | solution.py:669
  15.5 1.5 %shard_map.69 = (f32[21,560,128]{2,1,0:T(8,128)S(1)}, f32[24,8,128]{2,1,0:T(8,128)S(1)}) custom-call(f32[192,128]{1,0:T(8,128)S(1)} %bitcast.15, s32[704,128]{1,0:T(8,128)S(1)} %bitcast.8, s32[64,128]{1,0:T(8,128)S(1)} %bitcast.18, f32[3,4]{1,0:T(4,128)} %moduli_hbm.5), custom_call_target="tpu_custom_call" | custom-call | flops 10000000 | bytes 100000 | tf_op jit(solution)/shard_map/pallas_call | solution.py:632
  17.0 0.0 collective-permute-done
  17.0 2.1 %collective-permute-done.1 = f32[55,8,128]{2,1,0:T(8,128)S(1)} collective-permute-done((f32[55,8,128]{2,1,0:T(8,128)S(1)}, f32[55,8,128]{2,1,0:T(8,128)S(1)}, u32[]{:S(2)}, u32[]{:S(2)}) %collective-permute-start.1) | collective-permute-done | bytes 225312 | tf_op jit(solution)/shard_map/ppermute | solution.py:669
  19.1 1.3 %shard_map.70 = (f32[21,560,128]{2,1,0:T(8,128)S(1)}, f32[3,288,128]{2,1,0:T(8,128)S(1)}, f32[218,128]{1,0:T(8,128)S(1)}, f32[218,128]{1,0:T(8,128)S(1)}) custom-call(f32[192,128]{1,0:T(8,128)S(1)} %bitcast.16, s32[704,128]{1,0:T(8,128)S(1)} %bitcast.9, f32[24,8,128]{2,1,0:T(8,128)S(1)} %get-tuple-element.25.own_ref, ...), custom_call_target="tpu_custom_call", output_to_operand_aliasing={{0}: (6, {})} | custom-call | flops 10000000 | bytes 100000 | tf_op jit(solution)/shard_map/pallas_call | solution.py:632
  20.4 3.8 %collective-permute-start.3 = (f32[218,128]{1,0:T(8,128)S(1)}, f32[218,128]{1,0:T(8,128)S(1)}, u32[]{:S(2)}, u32[]{:S(2)}) collective-permute-start(f32[218,128]{1,0:T(8,128)S(1)} %get-tuple-element.37), channel_id=1, source_target_pairs={{0,1},{1,2},{2,3},{3,4},{4,5},{5,6},{6,7},{7,8},{8,9},{9,10},{10,1... | collective-permute-start | bytes 334856 | tf_op jit(solution)/shard_map/ppermute | solution.py:653
  24.2 3.0 %collective-permute-start.2 = (f32[218,128]{1,0:T(8,128)S(1)}, f32[218,128]{1,0:T(8,128)S(1)}, u32[]{:S(2)}, u32[]{:S(2)}) collective-permute-start(f32[218,128]{1,0:T(8,128)S(1)} %get-tuple-element.29), channel_id=1, source_target_pairs={{1,0},{2,1},{3,2},{4,3},{5,4},{6,5},{7,6},{8,7},{9,8},{10,9},{11,1... | collective-permute-start | bytes 334856 | tf_op jit(solution)/shard_map/ppermute | solution.py:654
  27.1 3.4 %shard_map.71 = (f32[3,288,128]{2,1,0:T(8,128)S(1)}, s32[11,288,128]{2,1,0:T(8,128)S(1)}, f32[24,8,128]{2,1,0:T(8,128)S(1)}, f32[24,8,128]{2,1,0:T(8,128)S(1)}, ...) custom-call(f32[21,560,128]{2,1,0:T(8,128)S(1)} %get-tuple-element.3, ...), custom_call_target="tpu_custom_call", output_to_operand_aliasing={{0}: (6, {})} | custom-call | flops 40000000 | bytes 100000 | tf_op jit(solution)/shard_map/pallas_call | solution.py:632
  30.5 0.0 collective-permute-done.3.slab_ref
  30.5 0.0 copy-start
  30.5 0.9 %shard_map.72.force_ref = f32[24,8,128]{2,1,0:T(8,128)S(1)} custom-call(f32[218,128]{1,0:T(8,128)S(1)} %collective-permute-done.3.slab_ref, f32[21,560,128]{2,1,0:T(8,128)S(1)} %get-tuple-element.30.ux_ref, s32[11,288,128]{2,1,0:T(8,128)S(1)} %get-tuple-element.32.wx_ref, f32[3,288,128]{2,1,0:T(8,128)S(1)} %get-tuple-element.33.field_ref, ...), custom_call_target="tpu_custom_call" | custom-call | flops 10000000 | bytes 100000 | tf_op jit(solution)/shard_map/pallas_call | solution.py:632
  31.4 2.4 %collective-permute-done.2.slab_ref = f32[218,128]{1,0:T(8,128)S(1)} collective-permute-done((f32[218,128]{1,0:T(8,128)S(1)}, f32[218,128]{1,0:T(8,128)S(1)}, u32[]{:S(2)}, u32[]{:S(2)}) %collective-permute-start.2) | collective-permute-done | bytes 111648 | tf_op jit(solution)/shard_map/ppermute | solution.py:654
  33.9 0.0 copy-done
  33.9 1.5 %shard_map.73 = (f32[192,128]{1,0:T(8,128)}, f32[192,128]{1,0:T(8,128)}) custom-call(f32[218,128]{1,0:T(8,128)S(1)} %collective-permute-done.2.slab_ref, f32[21,560,128]{2,1,0:T(8,128)S(1)} %get-tuple-element.30.ux_ref, s32[11,288,128]{2,1,0:T(8,128)S(1)} %get-tuple-element.32.wx_ref, f32[3,288,128]{2,1,0:T(8,128)S(1)} %get-tuple-element.33.field_ref, ...), custom_call_target="tpu_custom_call" | custom-call | flops 10000000 | bytes 100000 | tf_op jit(solution)/shard_map/pallas_call | solution.py:632
Async XLA Ops:
  1.7 15.3 %collective-permute-start = (f32[55,8,128]{2,1,0:T(8,128)S(1)}, f32[55,8,128]{2,1,0:T(8,128)S(1)}, u32[]{:S(2)}, u32[]{:S(2)}) collective-permute-start(f32[55,8,128]{2,1,0:T(8,128)S(1)} %get-tuple-element.26), channel_id=1, source_target_pairs={{0,16},{16,0},{32,48},{48,32},{64,80},{80,64},{96,112},{112,96},{1... | collective-permute-start | bytes 675848 | tf_op jit(solution)/shard_map/ppermute | solution.py:672
  3.6 15.5 %collective-permute-start.1 = (f32[55,8,128]{2,1,0:T(8,128)S(1)}, f32[55,8,128]{2,1,0:T(8,128)S(1)}, u32[]{:S(2)}, u32[]{:S(2)}) collective-permute-start(f32[55,8,128]{2,1,0:T(8,128)S(1)} %get-tuple-element.27), channel_id=1, source_target_pairs={{16,32},{32,16},{48,64},{64,48},{80,96},{96,80},{112,128},{128,112... | collective-permute-start | bytes 675848 | tf_op jit(solution)/shard_map/ppermute | solution.py:669
  20.4 10.1 %collective-permute-start.3 = (f32[218,128]{1,0:T(8,128)S(1)}, f32[218,128]{1,0:T(8,128)S(1)}, u32[]{:S(2)}, u32[]{:S(2)}) collective-permute-start(f32[218,128]{1,0:T(8,128)S(1)} %get-tuple-element.37), channel_id=1, source_target_pairs={{0,1},{1,2},{2,3},{3,4},{4,5},{5,6},{6,7},{7,8},{8,9},{9,10},{10,1... | collective-permute-start | bytes 334856 | tf_op jit(solution)/shard_map/ppermute | solution.py:653
  24.2 9.7 %collective-permute-start.2 = (f32[218,128]{1,0:T(8,128)S(1)}, f32[218,128]{1,0:T(8,128)S(1)}, u32[]{:S(2)}, u32[]{:S(2)}) collective-permute-start(f32[218,128]{1,0:T(8,128)S(1)} %get-tuple-element.29), channel_id=1, source_target_pairs={{1,0},{2,1},{3,2},{4,3},{5,4},{6,5},{7,6},{8,7},{9,8},{10,9},{11,1... | collective-permute-start | bytes 334856 | tf_op jit(solution)/shard_map/ppermute | solution.py:654
  30.5 3.3 %copy-start = (f32[3,8,8,128]{3,2,1,0:T(8,128)S(1)}, f32[3,8,8,128]{3,2,1,0:T(8,128)}, u32[]{:S(2)}) copy-start(f32[3,8,8,128]{3,2,1,0:T(8,128)} %param.6) | copy-start | bytes 294916

commit v7 on v6

--- a/solution.py
+++ b/solution.py
@@ -303,8 +303,8 @@
     ux_in_ref,
     ux_ref,
     field_ref,
-    down_ref,
-    up_ref,
+    odd_rows_ref,
+    even_rows_ref,
     moduli_ref,
     moduli_sem,
 ):
@@ -337,9 +337,10 @@
         field_ref[1, fx_column(x), :], field_ref[2, fx_column(x), :] = ratios(
             lambda k, x=x: halo_word(k, x), halo_region(x), moduli_ref
         )
-    for ref, first, step in ((down_ref, 0, 1), (up_ref, 7, -1)):
+    parity_y = lax.axis_index("gy") % 2
+    for ref, upward in ((odd_rows_ref, parity_y), (even_rows_ref, 1 - parity_y)):
         for depth in range(3):
-            y = first + step * depth
+            y = depth + upward * (7 - 2 * depth)
             places, field_places = slab_places(depth)
             for i in slab_components(depth):
                 for x in places:
@@ -486,14 +487,16 @@
     lax.fori_loop(0, 8, row, 0)
 
 
-def side_of(low):
-    return ((0, 1, 2), -3, 4) if low else ((5, 6, 7), 5, 10)
+def side_of(low, early):
+    if low:
+        return (0, 1, 2), -3, 4 if early else 2
+    return (5, 6, 7), 3 if early else 5, 10
 
 
 def add_side(
-    low, slab_ref, ux_ref, wx_ref, field_ref, hd_ref, weight_ref, sum_ref, uh_ref, sh_ref, px_ref
+    low, early, slab_ref, ux_ref, wx_ref, field_ref, hd_ref, weight_ref, sum_ref, uh_ref, sh_ref, px_ref
 ):
-    edge, first, last = side_of(low)
+    edge, first, last = side_of(low, early)
     halo = [(depth, 2 - depth if low else 3 + depth) for depth in range(3)]
     for depth, h in halo:
         for i in slab_components(depth):
@@ -573,7 +576,7 @@
     return row
 
 
-def lower_force(
+def early_force(
     slab_ref,
     ux_ref,
     wx_ref,
@@ -587,13 +590,17 @@
     sh_ref,
     px_ref,
 ):
-    row = add_side(
-        True, slab_ref, ux_ref, wx_ref, field_ref, hd_ref, weight_ref, sum_ref, uh_ref, sh_ref, px_ref
-    )
-    for y in range(8):
-        force = row(y, [part_ref[i * 8 + y] for i in range(3)])
-        for i in range(3):
-            force_ref[i * 8 + y] = force[i]
+    parity = lax.axis_index("gy") % 2
+    shared = (ux_ref, wx_ref, field_ref, hd_ref, weight_ref, sum_ref, uh_ref, sh_ref, px_ref)
+    for low in (True, False):
+
+        @pl.when(parity == (0 if low else 1))
+        def _(low=low):
+            row = add_side(low, True, slab_ref, *shared)
+            for y in range(8):
+                force = row(y, [part_ref[i * 8 + y] for i in range(3)])
+                for i in range(3):
+                    force_ref[i * 8 + y] = force[i]
 
 
 def outer_force(
@@ -614,16 +621,20 @@
     sh_ref,
     px_ref,
 ):
-    row = add_side(
-        False, slab_ref, ux_ref, wx_ref, field_ref, hd_ref, weight_ref, sum_ref, uh_ref, sh_ref, px_ref
-    )
-    for y in range(8):
-        force = row(y, [force_ref[i * 8 + y] for i in range(3)])
-        for i in range(3):
-            rows = pl.ds(i * 64 + y, 8, stride=8)
-            velocity = v_ref[rows, :] + force[i] * step_ref[y]
-            new_v_ref[rows, :] = velocity
-            new_u_ref[rows, :] = u_ref[rows, :] + time_step * velocity
+    parity = lax.axis_index("gy") % 2
+    shared = (ux_ref, wx_ref, field_ref, hd_ref, weight_ref, sum_ref, uh_ref, sh_ref, px_ref)
+    for low in (True, False):
+
+        @pl.when(parity == (1 if low else 0))
+        def _(low=low):
+            row = add_side(low, False, slab_ref, *shared)
+            for y in range(8):
+                force = row(y, [force_ref[i * 8 + y] for i in range(3)])
+                for i in range(3):
+                    rows = pl.ds(i * 64 + y, 8, stride=8)
+                    velocity = v_ref[rows, :] + force[i] * step_ref[y]
+                    new_v_ref[rows, :] = velocity
+                    new_u_ref[rows, :] = u_ref[rows, :] + time_step * velocity
 
 
 def call(body, outs, args, unplaced=(), scratch=(), flops=1000, aliases=None):
@@ -646,13 +657,12 @@
     )
 
 
-def along_y(down, up):
-    size = lax.axis_size("gy")
-    upward = [(i, i + 1) for i in range(size - 1)]
-    downward = [(i + 1, i) for i in range(size - 1)]
-    below = lax.ppermute(up, "gy", upward)
-    above = lax.ppermute(down, "gy", downward)
-    return below, above
+def odd_swap(size):
+    return [(i, ((i - 1) ^ 1) + 1) for i in range(1, size - 1)]
+
+
+def even_swap(size):
+    return [(i, i ^ 1) for i in range(size)]
 
 
 def on_device(displacement, velocity, region, bond_words, moduli):
@@ -666,10 +676,8 @@
         scratch=[copy, copy, copy],
     )
     size = lax.axis_size("gx")
-    odd = lax.ppermute(
-        odd, "gx", [(i, ((i - 1) ^ 1) + 1) for i in range(1, size - 1)]
-    )
-    even = lax.ppermute(even, "gx", [(i, i ^ 1) for i in range(size)])
+    odd = lax.ppermute(odd, "gx", odd_swap(size))
+    even = lax.ppermute(even, "gx", even_swap(size))
     even = even.reshape(SLAB * 8, LANES)
     odd = odd.reshape(SLAB * 8, LANES)
     u = u.reshape(192, LANES)
@@ -686,7 +694,7 @@
         scratch=scalars,
         flops=10_000_000,
     )
-    ux, fields, down, up = call(
+    ux, fields, odd_rows, even_rows = call(
         slabs_y,
         [displaced, per_node, ((SLAB_Y, LANES), F32), ((SLAB_Y, LANES), F32)],
         (u, words, own, moduli, even, odd, ux),
@@ -695,7 +703,9 @@
         flops=10_000_000,
         aliases={6: 0},
     )
-    below, above = along_y(down, up)
+    size = lax.axis_size("gy")
+    odd_rows = lax.ppermute(odd_rows, "gy", odd_swap(size))
+    even_rows = lax.ppermute(even_rows, "gy", even_swap(size))
     fields, wx, part, balance, step, halo, weights = call(
         inner_force,
         [
@@ -720,16 +730,16 @@
         pltpu.VMEM((7, 16 * SU, LANES), F32),
     ]
     (force,) = call(
-        lower_force,
+        early_force,
         [((24, 8, LANES), F32)],
-        (below,) + shared + (part,),
+        (odd_rows,) + shared + (part,),
         scratch=working,
         flops=10_000_000,
     )
     new_u, new_v = call(
         outer_force,
         [((192, LANES), F32)] * 2,
-        (above,) + shared + (force, step, u, velocity.reshape(192, LANES)),
+        (even_rows,) + shared + (force, step, u, velocity.reshape(192, LANES)),
         scratch=working,
         flops=10_000_000,
     )

time: 35.7 us -> 37.8 us (1.059)
  the two profiles are of different devices: /device:TPU:56 before, /device:TPU:12 now
where the time goes in v7:
time: 37.8 us; the launch traced here: 37.5 us
  starting transfers between devices  23.8 us (63%)
  Pallas kernels  9.63 us (25%)
  waiting for transfers between devices  3.32 us (9%)
  between operations  0.74 us (2%)
    ppermute x1, starting transfers between devices, on_device(): odd = lax.ppermute(odd, 'gx', odd_swap(size))  10.9 us
    pallas_call x6, Pallas kernels, call(): pl.pallas_call(body, out_shape=[jax.ShapeDtypeStruct(shape, dtype) for sh...  9.63 us
    ppermute x1, starting transfers between devices, on_device(): odd_rows = lax.ppermute(odd_rows, 'gy', odd_swap(size))  6.01 us
    ppermute x1, starting transfers between devices, on_device(): even_rows = lax.ppermute(even_rows, 'gy', even_swap(size))  4.93 us
    ppermute x1, waiting for transfers between devices, on_device(): odd = lax.ppermute(odd, 'gx', odd_swap(size))  3.32 us
    ppermute x1, starting transfers between devices, on_device(): even = lax.ppermute(even, 'gx', even_swap(size))  1.92 us
  transfers between devices with their start and end apart: 4, of which 1 were waited for; matrix products, arithmetic and copies ran while one was open for 0% of the time, Pallas kernels for 16%

profile of v7, /device:TPU:12, one launch (start us, length us, event | category | flops | bytes accessed | tf_op | source)
XLA Modules:
  0.0 37.5 jit_solution(17311982405084579833)
XLA Ops:
  0.6 1.1 %shard_map.68 = (f32[55,8,128]{2,1,0:T(8,128)S(1)}, f32[55,8,128]{2,1,0:T(8,128)S(1)}, f32[3,8,8,128]{3,2,1,0:T(8,128)S(1)}, s32[11,8,8,128]{3,2,1,0:T(8,128)S(1)}, s32[8,8,128]{2,1,0:T(8,128)S(1)}) custom-call(f32[3,8,8,128]{3,2,1,0:T(8,128)} %u_hbm.1, s32[11,8,8,128]{3,2,1,0:T(8,128)} %w_hbm.1, s32[8,8,128]{2,1,0:T(8,128)} %r_hbm.1), custom_call_target="tpu_custom_call" | custom-call | flops 1000 | bytes 100000 | tf_op jit(solution)/shard_map/pallas_call | solution.py:643
  1.7 1.9 %collective-permute-start = (f32[55,8,128]{2,1,0:T(8,128)S(1)}, f32[55,8,128]{2,1,0:T(8,128)S(1)}, u32[]{:S(2)}, u32[]{:S(2)}) collective-permute-start(f32[55,8,128]{2,1,0:T(8,128)S(1)} %get-tuple-element.26), channel_id=1, source_target_pairs={{0,16},{16,0},{32,48},{48,32},{64,80},{80,64},{96,112},{112,96},{1... | collective-permute-start | bytes 675848 | tf_op jit(solution)/shard_map/ppermute | solution.py:680
  3.6 10.9 %collective-permute-start.1 = (f32[55,8,128]{2,1,0:T(8,128)S(1)}, f32[55,8,128]{2,1,0:T(8,128)S(1)}, u32[]{:S(2)}, u32[]{:S(2)}) collective-permute-start(f32[55,8,128]{2,1,0:T(8,128)S(1)} %get-tuple-element.27), channel_id=1, source_target_pairs={{16,32},{32,16},{48,64},{64,48},{80,96},{96,80},{112,128},{128,112... | collective-permute-start | bytes 675848 | tf_op jit(solution)/shard_map/ppermute | solution.py:679
  14.6 1.5 %shard_map.69 = (f32[21,560,128]{2,1,0:T(8,128)S(1)}, f32[24,8,128]{2,1,0:T(8,128)S(1)}) custom-call(f32[192,128]{1,0:T(8,128)S(1)} %bitcast.15, s32[704,128]{1,0:T(8,128)S(1)} %bitcast.8, s32[64,128]{1,0:T(8,128)S(1)} %bitcast.18, f32[3,4]{1,0:T(4,128)} %moduli_hbm.5), custom_call_target="tpu_custom_call" | custom-call | flops 10000000 | bytes 100000 | tf_op jit(solution)/shard_map/pallas_call | solution.py:643
  16.1 0.0 collective-permute-done
  16.1 3.3 %collective-permute-done.1 = f32[55,8,128]{2,1,0:T(8,128)S(1)} collective-permute-done((f32[55,8,128]{2,1,0:T(8,128)S(1)}, f32[55,8,128]{2,1,0:T(8,128)S(1)}, u32[]{:S(2)}, u32[]{:S(2)}) %collective-permute-start.1) | collective-permute-done | bytes 225312 | tf_op jit(solution)/shard_map/ppermute | solution.py:679
  19.5 1.3 %shard_map.70 = (f32[21,560,128]{2,1,0:T(8,128)S(1)}, f32[3,288,128]{2,1,0:T(8,128)S(1)}, f32[218,128]{1,0:T(8,128)S(1)}, f32[218,128]{1,0:T(8,128)S(1)}) custom-call(f32[192,128]{1,0:T(8,128)S(1)} %bitcast.16, s32[704,128]{1,0:T(8,128)S(1)} %bitcast.9, f32[24,8,128]{2,1,0:T(8,128)S(1)} %get-tuple-element.25.own_ref, ...), custom_call_target="tpu_custom_call", output_to_operand_aliasing={{0}: (6, {})} | custom-call | flops 10000000 | bytes 100000 | tf_op jit(solution)/shard_map/pallas_call | solution.py:643
  20.7 6.0 %collective-permute-start.3 = (f32[218,128]{1,0:T(8,128)S(1)}, f32[218,128]{1,0:T(8,128)S(1)}, u32[]{:S(2)}, u32[]{:S(2)}) collective-permute-start(f32[218,128]{1,0:T(8,128)S(1)} %get-tuple-element.37), channel_id=1, source_target_pairs={{1,2},{2,1},{3,4},{4,3},{5,6},{6,5},{7,8},{8,7},{9,10},{10,9},{11,... | collective-permute-start | bytes 334856 | tf_op jit(solution)/shard_map/ppermute | solution.py:707
  26.7 4.9 %collective-permute-start.2 = (f32[218,128]{1,0:T(8,128)S(1)}, f32[218,128]{1,0:T(8,128)S(1)}, u32[]{:S(2)}, u32[]{:S(2)}) collective-permute-start(f32[218,128]{1,0:T(8,128)S(1)} %get-tuple-element.29), channel_id=1, source_target_pairs={{0,1},{1,0},{2,3},{3,2},{4,5},{5,4},{6,7},{7,6},{8,9},{9,8},{10,11... | collective-permute-start | bytes 334856 | tf_op jit(solution)/shard_map/ppermute | solution.py:708
  31.7 3.4 %shard_map.71 = (f32[3,288,128]{2,1,0:T(8,128)S(1)}, s32[11,288,128]{2,1,0:T(8,128)S(1)}, f32[24,8,128]{2,1,0:T(8,128)S(1)}, f32[24,8,128]{2,1,0:T(8,128)S(1)}, ...) custom-call(f32[21,560,128]{2,1,0:T(8,128)S(1)} %get-tuple-element.3, ...), custom_call_target="tpu_custom_call", output_to_operand_aliasing={{0}: (6, {})} | custom-call | flops 40000000 | bytes 100000 | tf_op jit(solution)/shard_map/pallas_call | solution.py:643
  35.0 0.0 collective-permute-done.3.slab_ref
  35.1 0.0 copy-start
  35.1 0.9 %shard_map.72.force_ref = f32[24,8,128]{2,1,0:T(8,128)S(1)} custom-call(f32[218,128]{1,0:T(8,128)S(1)} %collective-permute-done.3.slab_ref, f32[21,560,128]{2,1,0:T(8,128)S(1)} %get-tuple-element.30.ux_ref, s32[11,288,128]{2,1,0:T(8,128)S(1)} %get-tuple-element.32.wx_ref, f32[3,288,128]{2,1,0:T(8,128)S(1)} %get-tuple-element.33.field_ref, ...), custom_call_target="tpu_custom_call" | custom-call | flops 10000000 | bytes 100000 | tf_op jit(solution)/shard_map/pallas_call | solution.py:643
  36.0 0.0 collective-permute-done.2.slab_ref
  36.0 0.0 copy-done
  36.0 1.5 %shard_map.73 = (f32[192,128]{1,0:T(8,128)}, f32[192,128]{1,0:T(8,128)}) custom-call(f32[218,128]{1,0:T(8,128)S(1)} %collective-permute-done.2.slab_ref, f32[21,560,128]{2,1,0:T(8,128)S(1)} %get-tuple-element.30.ux_ref, s32[11,288,128]{2,1,0:T(8,128)S(1)} %get-tuple-element.32.wx_ref, f32[3,288,128]{2,1,0:T(8,128)S(1)} %get-tuple-element.33.field_ref, ...), custom_call_target="tpu_custom_call" | custom-call | flops 10000000 | bytes 100000 | tf_op jit(solution)/shard_map/pallas_call | solution.py:643
Async XLA Ops:
  1.7 14.4 %collective-permute-start = (f32[55,8,128]{2,1,0:T(8,128)S(1)}, f32[55,8,128]{2,1,0:T(8,128)S(1)}, u32[]{:S(2)}, u32[]{:S(2)}) collective-permute-start(f32[55,8,128]{2,1,0:T(8,128)S(1)} %get-tuple-element.26), channel_id=1, source_target_pairs={{0,16},{16,0},{32,48},{48,32},{64,80},{80,64},{96,112},{112,96},{1... | collective-permute-start | bytes 675848 | tf_op jit(solution)/shard_map/ppermute | solution.py:680
  3.6 15.8 %collective-permute-start.1 = (f32[55,8,128]{2,1,0:T(8,128)S(1)}, f32[55,8,128]{2,1,0:T(8,128)S(1)}, u32[]{:S(2)}, u32[]{:S(2)}) collective-permute-start(f32[55,8,128]{2,1,0:T(8,128)S(1)} %get-tuple-element.27), channel_id=1, source_target_pairs={{16,32},{32,16},{48,64},{64,48},{80,96},{96,80},{112,128},{128,112... | collective-permute-start | bytes 675848 | tf_op jit(solution)/shard_map/ppermute | solution.py:679
  20.7 14.3 %collective-permute-start.3 = (f32[218,128]{1,0:T(8,128)S(1)}, f32[218,128]{1,0:T(8,128)S(1)}, u32[]{:S(2)}, u32[]{:S(2)}) collective-permute-start(f32[218,128]{1,0:T(8,128)S(1)} %get-tuple-element.37), channel_id=1, source_target_pairs={{1,2},{2,1},{3,4},{4,3},{5,6},{6,5},{7,8},{8,7},{9,10},{10,9},{11,... | collective-permute-start | bytes 334856 | tf_op jit(solution)/shard_map/ppermute | solution.py:707
  26.7 9.3 %collective-permute-start.2 = (f32[218,128]{1,0:T(8,128)S(1)}, f32[218,128]{1,0:T(8,128)S(1)}, u32[]{:S(2)}, u32[]{:S(2)}) collective-permute-start(f32[218,128]{1,0:T(8,128)S(1)} %get-tuple-element.29), channel_id=1, source_target_pairs={{0,1},{1,0},{2,3},{3,2},{4,5},{5,4},{6,7},{7,6},{8,9},{9,8},{10,11... | collective-permute-start | bytes 334856 | tf_op jit(solution)/shard_map/ppermute | solution.py:708
  35.1 0.9 %copy-start = (f32[3,8,8,128]{3,2,1,0:T(8,128)S(1)}, f32[3,8,8,128]{3,2,1,0:T(8,128)}, u32[]{:S(2)}) copy-start(f32[3,8,8,128]{3,2,1,0:T(8,128)} %param.6) | copy-start | bytes 294916

commit v8 on v7

--- a/solution.py
+++ b/solution.py
@@ -303,8 +303,8 @@
     ux_in_ref,
     ux_ref,
     field_ref,
-    odd_rows_ref,
-    even_rows_ref,
+    first_rows_ref,
+    second_rows_ref,
     moduli_ref,
     moduli_sem,
 ):
@@ -338,7 +338,7 @@
             lambda k, x=x: halo_word(k, x), halo_region(x), moduli_ref
         )
     parity_y = lax.axis_index("gy") % 2
-    for ref, upward in ((odd_rows_ref, parity_y), (even_rows_ref, 1 - parity_y)):
+    for ref, upward in ((first_rows_ref, 1 - parity_y), (second_rows_ref, parity_y)):
         for depth in range(3):
             y = depth + upward * (7 - 2 * depth)
             places, field_places = slab_places(depth)
@@ -594,7 +594,7 @@
     shared = (ux_ref, wx_ref, field_ref, hd_ref, weight_ref, sum_ref, uh_ref, sh_ref, px_ref)
     for low in (True, False):
 
-        @pl.when(parity == (0 if low else 1))
+        @pl.when(parity == (1 if low else 0))
         def _(low=low):
             row = add_side(low, True, slab_ref, *shared)
             for y in range(8):
@@ -625,7 +625,7 @@
     shared = (ux_ref, wx_ref, field_ref, hd_ref, weight_ref, sum_ref, uh_ref, sh_ref, px_ref)
     for low in (True, False):
 
-        @pl.when(parity == (1 if low else 0))
+        @pl.when(parity == (0 if low else 1))
         def _(low=low):
             row = add_side(low, False, slab_ref, *shared)
             for y in range(8):
@@ -694,7 +694,7 @@
         scratch=scalars,
         flops=10_000_000,
     )
-    ux, fields, odd_rows, even_rows = call(
+    ux, fields, first_rows, second_rows = call(
         slabs_y,
         [displaced, per_node, ((SLAB_Y, LANES), F32), ((SLAB_Y, LANES), F32)],
         (u, words, own, moduli, even, odd, ux),
@@ -704,8 +704,8 @@
         aliases={6: 0},
     )
     size = lax.axis_size("gy")
-    odd_rows = lax.ppermute(odd_rows, "gy", odd_swap(size))
-    even_rows = lax.ppermute(even_rows, "gy", even_swap(size))
+    first_rows = lax.ppermute(first_rows, "gy", even_swap(size))
+    second_rows = lax.ppermute(second_rows, "gy", odd_swap(size))
     fields, wx, part, balance, step, halo, weights = call(
         inner_force,
         [
@@ -732,14 +732,14 @@
     (force,) = call(
         early_force,
         [((24, 8, LANES), F32)],
-        (odd_rows,) + shared + (part,),
+        (first_rows,) + shared + (part,),
         scratch=working,
         flops=10_000_000,
     )
     new_u, new_v = call(
         outer_force,
         [((192, LANES), F32)] * 2,
-        (even_rows,) + shared + (force, step, u, velocity.reshape(192, LANES)),
+        (second_rows,) + shared + (force, step, u, velocity.reshape(192, LANES)),
         scratch=working,
         flops=10_000_000,
     )

time: 37.8 us -> 38.2 us (1.011)
  the two profiles are of different devices: /device:TPU:12 before, /device:TPU:56 now
where the time goes in v8:
time: 38.2 us; the launch traced here: 37.9 us
  starting transfers between devices  21.6 us (57%)
  Pallas kernels  9.61 us (25%)
  waiting for transfers between devices  5.89 us (15%)
  between operations  0.73 us (2%)
    ppermute x1, starting transfers between devices, on_device(): odd = lax.ppermute(odd, 'gx', odd_swap(size))  11.8 us
    pallas_call x6, Pallas kernels, call(): pl.pallas_call(body, out_shape=[jax.ShapeDtypeStruct(shape, dtype) for sh...  9.61 us
    ppermute x1, starting transfers between devices, on_device(): first_rows = lax.ppermute(first_rows, 'gy', even_swap(size))  5.27 us
    ppermute x1, waiting for transfers between devices, on_device(): odd = lax.ppermute(odd, 'gx', odd_swap(size))  3.14 us
    ppermute x1, waiting for transfers between devices, on_device(): second_rows = lax.ppermute(second_rows, 'gy', odd_swap(size))  2.75 us
    ppermute x1, starting transfers between devices, on_device(): second_rows = lax.ppermute(second_rows, 'gy', odd_swap(size))  2.61 us
    ppermute x1, starting transfers between devices, on_device(): even = lax.ppermute(even, 'gx', even_swap(size))  1.92 us
  transfers between devices with their start and end apart: 4, of which 2 were waited for; matrix products, arithmetic and copies ran while one was open for 0% of the time, Pallas kernels for 15%

profile of v8, /device:TPU:56, one launch (start us, length us, event | category | flops | bytes accessed | tf_op | source)
XLA Modules:
  0.0 37.9 jit_solution(8174533361736815476)
XLA Ops:
  0.6 1.1 %shard_map.68 = (f32[55,8,128]{2,1,0:T(8,128)S(1)}, f32[55,8,128]{2,1,0:T(8,128)S(1)}, f32[3,8,8,128]{3,2,1,0:T(8,128)S(1)}, s32[11,8,8,128]{3,2,1,0:T(8,128)S(1)}, s32[8,8,128]{2,1,0:T(8,128)S(1)}) custom-call(f32[3,8,8,128]{3,2,1,0:T(8,128)} %u_hbm.1, s32[11,8,8,128]{3,2,1,0:T(8,128)} %w_hbm.1, s32[8,8,128]{2,1,0:T(8,128)} %r_hbm.1), custom_call_target="tpu_custom_call" | custom-call | flops 1000 | bytes 100000 | tf_op jit(solution)/shard_map/pallas_call | solution.py:643
  1.7 1.9 %collective-permute-start = (f32[55,8,128]{2,1,0:T(8,128)S(1)}, f32[55,8,128]{2,1,0:T(8,128)S(1)}, u32[]{:S(2)}, u32[]{:S(2)}) collective-permute-start(f32[55,8,128]{2,1,0:T(8,128)S(1)} %get-tuple-element.26), channel_id=1, source_target_pairs={{0,16},{16,0},{32,48},{48,32},{64,80},{80,64},{96,112},{112,96},{1... | collective-permute-start | bytes 675848 | tf_op jit(solution)/shard_map/ppermute | solution.py:680
  3.6 11.8 %collective-permute-start.1 = (f32[55,8,128]{2,1,0:T(8,128)S(1)}, f32[55,8,128]{2,1,0:T(8,128)S(1)}, u32[]{:S(2)}, u32[]{:S(2)}) collective-permute-start(f32[55,8,128]{2,1,0:T(8,128)S(1)} %get-tuple-element.27), channel_id=1, source_target_pairs={{16,32},{32,16},{48,64},{64,48},{80,96},{96,80},{112,128},{128,112... | collective-permute-start | bytes 675848 | tf_op jit(solution)/shard_map/ppermute | solution.py:679
  15.5 1.5 %shard_map.69 = (f32[21,560,128]{2,1,0:T(8,128)S(1)}, f32[24,8,128]{2,1,0:T(8,128)S(1)}) custom-call(f32[192,128]{1,0:T(8,128)S(1)} %bitcast.15, s32[704,128]{1,0:T(8,128)S(1)} %bitcast.8, s32[64,128]{1,0:T(8,128)S(1)} %bitcast.18, f32[3,4]{1,0:T(4,128)} %moduli_hbm.5), custom_call_target="tpu_custom_call" | custom-call | flops 10000000 | bytes 100000 | tf_op jit(solution)/shard_map/pallas_call | solution.py:643
  17.0 0.0 collective-permute-done
  17.0 3.1 %collective-permute-done.1 = f32[55,8,128]{2,1,0:T(8,128)S(1)} collective-permute-done((f32[55,8,128]{2,1,0:T(8,128)S(1)}, f32[55,8,128]{2,1,0:T(8,128)S(1)}, u32[]{:S(2)}, u32[]{:S(2)}) %collective-permute-start.1) | collective-permute-done | bytes 225312 | tf_op jit(solution)/shard_map/ppermute | solution.py:679
  20.2 1.3 %shard_map.70 = (f32[21,560,128]{2,1,0:T(8,128)S(1)}, f32[3,288,128]{2,1,0:T(8,128)S(1)}, f32[218,128]{1,0:T(8,128)S(1)}, f32[218,128]{1,0:T(8,128)S(1)}) custom-call(f32[192,128]{1,0:T(8,128)S(1)} %bitcast.16, s32[704,128]{1,0:T(8,128)S(1)} %bitcast.9, f32[24,8,128]{2,1,0:T(8,128)S(1)} %get-tuple-element.25.own_ref, ...), custom_call_target="tpu_custom_call", output_to_operand_aliasing={{0}: (6, {})} | custom-call | flops 10000000 | bytes 100000 | tf_op jit(solution)/shard_map/pallas_call | solution.py:643
  21.4 5.3 %collective-permute-start.3 = (f32[218,128]{1,0:T(8,128)S(1)}, f32[218,128]{1,0:T(8,128)S(1)}, u32[]{:S(2)}, u32[]{:S(2)}) collective-permute-start(f32[218,128]{1,0:T(8,128)S(1)} %get-tuple-element.37), channel_id=1, source_target_pairs={{0,1},{1,0},{2,3},{3,2},{4,5},{5,4},{6,7},{7,6},{8,9},{9,8},{10,11... | collective-permute-start | bytes 334856 | tf_op jit(solution)/shard_map/ppermute | solution.py:707
  26.7 2.6 %collective-permute-start.2 = (f32[218,128]{1,0:T(8,128)S(1)}, f32[218,128]{1,0:T(8,128)S(1)}, u32[]{:S(2)}, u32[]{:S(2)}) collective-permute-start(f32[218,128]{1,0:T(8,128)S(1)} %get-tuple-element.29), channel_id=1, source_target_pairs={{1,2},{2,1},{3,4},{4,3},{5,6},{6,5},{7,8},{8,7},{9,10},{10,9},{11,... | collective-permute-start | bytes 334856 | tf_op jit(solution)/shard_map/ppermute | solution.py:708
  29.3 3.4 %shard_map.71 = (f32[3,288,128]{2,1,0:T(8,128)S(1)}, s32[11,288,128]{2,1,0:T(8,128)S(1)}, f32[24,8,128]{2,1,0:T(8,128)S(1)}, f32[24,8,128]{2,1,0:T(8,128)S(1)}, ...) custom-call(f32[21,560,128]{2,1,0:T(8,128)S(1)} %get-tuple-element.3, ...), custom_call_target="tpu_custom_call", output_to_operand_aliasing={{0}: (6, {})} | custom-call | flops 40000000 | bytes 100000 | tf_op jit(solution)/shard_map/pallas_call | solution.py:643
  32.7 0.0 collective-permute-done.3.slab_ref
  32.7 0.0 copy-start
  32.7 0.9 %shard_map.72.force_ref = f32[24,8,128]{2,1,0:T(8,128)S(1)} custom-call(f32[218,128]{1,0:T(8,128)S(1)} %collective-permute-done.3.slab_ref, f32[21,560,128]{2,1,0:T(8,128)S(1)} %get-tuple-element.30.ux_ref, s32[11,288,128]{2,1,0:T(8,128)S(1)} %get-tuple-element.32.wx_ref, f32[3,288,128]{2,1,0:T(8,128)S(1)} %get-tuple-element.33.field_ref, ...), custom_call_target="tpu_custom_call" | custom-call | flops 10000000 | bytes 100000 | tf_op jit(solution)/shard_map/pallas_call | solution.py:643
  33.7 2.8 %collective-permute-done.2.slab_ref = f32[218,128]{1,0:T(8,128)S(1)} collective-permute-done((f32[218,128]{1,0:T(8,128)S(1)}, f32[218,128]{1,0:T(8,128)S(1)}, u32[]{:S(2)}, u32[]{:S(2)}) %collective-permute-start.2) | collective-permute-done | bytes 111648 | tf_op jit(solution)/shard_map/ppermute | solution.py:708
  36.4 0.0 copy-done
  36.4 1.5 %shard_map.73 = (f32[192,128]{1,0:T(8,128)}, f32[192,128]{1,0:T(8,128)}) custom-call(f32[218,128]{1,0:T(8,128)S(1)} %collective-permute-done.2.slab_ref, f32[21,560,128]{2,1,0:T(8,128)S(1)} %get-tuple-element.30.ux_ref, s32[11,288,128]{2,1,0:T(8,128)S(1)} %get-tuple-element.32.wx_ref, f32[3,288,128]{2,1,0:T(8,128)S(1)} %get-tuple-element.33.field_ref, ...), custom_call_target="tpu_custom_call" | custom-call | flops 10000000 | bytes 100000 | tf_op jit(solution)/shard_map/pallas_call | solution.py:643
Async XLA Ops:
  1.7 15.3 %collective-permute-start = (f32[55,8,128]{2,1,0:T(8,128)S(1)}, f32[55,8,128]{2,1,0:T(8,128)S(1)}, u32[]{:S(2)}, u32[]{:S(2)}) collective-permute-start(f32[55,8,128]{2,1,0:T(8,128)S(1)} %get-tuple-element.26), channel_id=1, source_target_pairs={{0,16},{16,0},{32,48},{48,32},{64,80},{80,64},{96,112},{112,96},{1... | collective-permute-start | bytes 675848 | tf_op jit(solution)/shard_map/ppermute | solution.py:680
  3.6 16.5 %collective-permute-start.1 = (f32[55,8,128]{2,1,0:T(8,128)S(1)}, f32[55,8,128]{2,1,0:T(8,128)S(1)}, u32[]{:S(2)}, u32[]{:S(2)}) collective-permute-start(f32[55,8,128]{2,1,0:T(8,128)S(1)} %get-tuple-element.27), channel_id=1, source_target_pairs={{16,32},{32,16},{48,64},{64,48},{80,96},{96,80},{112,128},{128,112... | collective-permute-start | bytes 675848 | tf_op jit(solution)/shard_map/ppermute | solution.py:679
  21.4 11.3 %collective-permute-start.3 = (f32[218,128]{1,0:T(8,128)S(1)}, f32[218,128]{1,0:T(8,128)S(1)}, u32[]{:S(2)}, u32[]{:S(2)}) collective-permute-start(f32[218,128]{1,0:T(8,128)S(1)} %get-tuple-element.37), channel_id=1, source_target_pairs={{0,1},{1,0},{2,3},{3,2},{4,5},{5,4},{6,7},{7,6},{8,9},{9,8},{10,11... | collective-permute-start | bytes 334856 | tf_op jit(solution)/shard_map/ppermute | solution.py:707
  26.7 9.7 %collective-permute-start.2 = (f32[218,128]{1,0:T(8,128)S(1)}, f32[218,128]{1,0:T(8,128)S(1)}, u32[]{:S(2)}, u32[]{:S(2)}) collective-permute-start(f32[218,128]{1,0:T(8,128)S(1)} %get-tuple-element.29), channel_id=1, source_target_pairs={{1,2},{2,1},{3,4},{4,3},{5,6},{6,5},{7,8},{8,7},{9,10},{10,9},{11,... | collective-permute-start | bytes 334856 | tf_op jit(solution)/shard_map/ppermute | solution.py:708
  32.7 3.7 %copy-start = (f32[3,8,8,128]{3,2,1,0:T(8,128)S(1)}, f32[3,8,8,128]{3,2,1,0:T(8,128)}, u32[]{:S(2)}) copy-start(f32[3,8,8,128]{3,2,1,0:T(8,128)} %param.6) | copy-start | bytes 294916
